TPU v7x, 1024 devices: a whole 8x8x8 slice. The times are simulated.
1024 devices in a mesh: cell: 64 (over y, x_hi, core), state: 16 (over z, x_lo).
Axes of the slice: x: 8 (x_hi: 4, x_lo: 2; x = x_hi * 2 + x_lo), y: 8, z: 8, core: 2. Of those that a mesh axis runs over, the one named last changes fastest.
Arguments:
- start_block: float32 [1024, 32768], P('state', 'cell'), may hold values from -6 to 6
- connectivity: int32 [128, 343], P('cell'), may hold values from 0 to 575, as said below
- cell_matrices: bfloat16 [128, 343, 343], P('cell'), may hold values from -4 to 4
- bounds: float32 [3], replicated, may hold values from -1 to 32, as said below
Outputs:
- filtered: float32 [1024, 32768], P('state', 'cell')
- projected: float32 [1024, 1024], P('cell', 'state')
Inputs may be any that keep to these rules, and one draw needn't show every extreme that they name: `connectivity`: each row names 343 different local nodes; numbers below 512 are nodes owned by the index of cell that holds the cell, the others the first 64 nodes of the next index of cell, cyclically. `bounds`: lowest < cut < upper, and every eigenvalue of H lies above lowest.
All inputs are finite; a program needn't handle non-finite values.
Results may differ from a plain program's by a relative error of at most 0.0016.
Values may be sent and summed in bfloat16 or wider, within the bound.
No kernel may reach another device: no remote copies, remote signals or barrier semaphores. Data moves between devices by JAX's collectives and lax.ppermute only.
A program may use at most 32 MiB of HBM per device.

v0:
```python
import functools

import jax
import jax.numpy as jnp
from jax import lax
from jax.experimental import pallas as pl
from jax.experimental.pallas import tpu as pltpu
from jax.sharding import PartitionSpec as P

DEGREE = 8


def passed_along(value, axis, steps):
    count = lax.axis_size(axis)
    pairs = [(source, (source + steps) % count) for source in range(count)]
    return lax.ppermute(value, axis, pairs)


def swapped(value, axis, first):
    count = lax.axis_size(axis)
    pairs = []
    for low in range(first, first + count, 2):
        left, right = low % count, (low + 1) % count
        pairs += [(left, right), (right, left)]
    return lax.ppermute(value, axis, pairs)


def scattered(connectivity, cell_matrices, extent):
    nodes = lax.broadcasted_iota(jnp.int32, (*connectivity.shape, extent), 2)
    chosen = (connectivity[:, :, None] == nodes).astype(jnp.bfloat16)
    half = jnp.einsum(
        "cba,cbk->cak", cell_matrices, chosen, preferred_element_type=jnp.float32
    ).astype(jnp.bfloat16)
    whole = jnp.einsum("cai,cak->cik", chosen, half, preferred_element_type=jnp.float32)
    cells = connectivity.shape[0]
    return whole.astype(jnp.bfloat16).reshape(cells * extent, extent)


def completed(flag, own, ghost, chip, link):
    even = flag[0] == 0
    first = ghost.shape[1]
    left = jnp.where(even, link, chip)
    right = jnp.where(even, chip, link)
    return own[:, :first] + left, ghost + right


def multiplied(extended, weights, cells):
    extent = weights.shape[0] // cells
    total = None
    for cell in range(cells):
        part = jnp.dot(
            extended,
            weights[cell * extent : (cell + 1) * extent, :],
            preferred_element_type=jnp.float32,
        )
        total = part if total is None else total + part
    return total


def degree_body(cells, flag, coef, own, ghost, chip, link, previous, weights, current, upcoming, spill, to_chip, to_link, extended):
    shared, owned = ghost.shape[1], own.shape[1]
    left, right = completed(flag, own[...], ghost[...], chip[...], link[...])
    current[...] = own[...]
    current[:, :shared] = left
    values = current[...]
    extended[:, :owned] = values.astype(jnp.bfloat16)
    extended[:, owned:] = right.astype(jnp.bfloat16)
    product = multiplied(extended[...], weights, cells)
    fresh = coef[0] * product[:, :owned] + coef[1] * values + coef[2] * previous[...]
    beyond = coef[0] * product[:, owned:]
    upcoming[...] = fresh
    spill[...] = beyond
    even = flag[0] == 0
    first = fresh[:, :shared]
    to_chip[...] = jnp.where(even, beyond, first)
    to_link[...] = jnp.where(even, first, beyond)


def image_body(cells, flag, own, ghost, chip, link, weights, current, low, product_out, spill, extended):
    shared, owned = ghost.shape[1], own.shape[1]
    left, right = completed(flag, own[...], ghost[...], chip[...], link[...])
    current[...] = own[...]
    current[:, :shared] = left
    values = current[...].astype(jnp.bfloat16)
    low[...] = values
    extended[:, :owned] = values
    extended[:, owned:] = right.astype(jnp.bfloat16)
    product = multiplied(extended[...], weights, cells)
    product_out[...] = product[:, :owned]
    spill[...] = product[:, owned:]


def project_body(lows, product, incoming, out):
    states, shared = incoming.shape
    value = product[...]
    first = value[:, :shared] + incoming[...]
    image = jnp.concatenate([first, value[:, shared:]], axis=1).astype(jnp.bfloat16)
    partial = lax.dot_general(
        lows[...], image, (((1,), (1,)), ((), ())), preferred_element_type=jnp.float32
    )
    pieces = partial.reshape(partial.shape[0] // 16, 2, 8, states)
    out[...] = jnp.concatenate([pieces[:, 0], pieces[:, 1]], axis=2)


def in_smem(count):
    return [pl.BlockSpec(memory_space=pltpu.SMEM)] * count


def in_vmem(count):
    return [pl.BlockSpec(memory_space=pltpu.VMEM)] * count


def per_device(start_block, connectivity, cell_matrices, bounds):
    f32 = jnp.float32
    states, owned = start_block.shape
    shared = owned // 8
    extent = owned + shared
    cells = connectivity.shape[0]
    flag = (lax.axis_index("cell") % 2).astype(jnp.int32).reshape(1)
    weights = scattered(connectivity, cell_matrices, extent)

    whole = jax.ShapeDtypeStruct((states, owned), f32)
    group = jax.ShapeDtypeStruct((states, shared), f32)
    scratch = [pltpu.VMEM((states, extent), jnp.bfloat16)]
    step = pl.pallas_call(
        functools.partial(degree_body, cells),
        in_specs=in_smem(2) + in_vmem(6),
        out_specs=tuple(in_vmem(5)),
        out_shape=(whole, whole, group, group, group),
        scratch_shapes=scratch,
        name="degree",
    )
    last = pl.pallas_call(
        functools.partial(image_body, cells),
        in_specs=in_smem(1) + in_vmem(5),
        out_specs=tuple(in_vmem(4)),
        out_shape=(whole, jax.ShapeDtypeStruct((states, owned), jnp.bfloat16), whole, group),
        scratch_shapes=scratch,
        name="image",
    )

    lowest, cut, upper = (bounds[0], bounds[1], bounds[2])
    half = (upper - cut) / 2.0
    centre = (upper + cut) / 2.0
    sigma = half / (lowest - centre)
    tau = 2.0 / sigma
    coefs = [jnp.stack([sigma / half, -centre * (sigma / half), jnp.zeros((), f32)])]
    for degree in range(2, DEGREE + 1):
        sigma_new = 1.0 / (tau - sigma)
        scale = 2.0 * sigma_new / half
        coefs.append(jnp.stack([scale, -centre * scale, -(sigma * sigma_new)]))
        sigma = sigma_new

    ghost = passed_along(start_block[:, :shared].astype(jnp.bfloat16), "cell", -1).astype(f32)
    own, previous = start_block, start_block
    chip = link = jnp.zeros((states, shared), f32)
    for coef in coefs:
        previous, own, ghost, to_chip, to_link = step(
            flag, coef, own, ghost, chip, link, previous, weights
        )
        chip = swapped(to_chip, "cell", 0)
        link = swapped(to_link, "cell", 1)
    filtered, low, product, spill = last(flag, own, ghost, chip, link, weights)
    incoming = passed_along(spill, "cell", 1)
    peers = lax.axis_size("state")
    lows = lax.all_to_all(
        jnp.broadcast_to(low[None], (peers, states, owned)), "state", 0, 0, tiled=True
    ).reshape(peers * states, owned)

    count = lax.axis_size("cell")
    rows = peers * states // count
    pieces = pl.pallas_call(
        project_body,
        in_specs=in_vmem(3),
        out_specs=in_vmem(1)[0],
        out_shape=jax.ShapeDtypeStruct((peers * states // 16, 8, 2 * states), f32),
        name="project",
    )(lows, product, incoming)
    arrived = lax.all_to_all(pieces, "cell", 0, 0, tiled=True)
    total = jnp.sum(arrived.reshape(count, rows // 16, 8, 2, states), axis=0)
    projected = jnp.swapaxes(total, 1, 2).reshape(rows, states)
    return (filtered, projected)


def solution(mesh):
    in_specs = (P("state", "cell"), P("cell", None), P("cell", None, None), P())
    out_specs = (P("state", "cell"), P("cell", "state"))
    return jax.shard_map(
        per_device, mesh=mesh, in_specs=in_specs, out_specs=out_specs, check_vma=False
    )
```

profile of v0, /device:TPU:1, one launch (start us, length us, event | category | flops | bytes accessed | tf_op | source)
XLA Modules:
  0.0 212.2 jit_solution(3521246412706127639)
XLA Ops:
  0.6 0.8 slice.19
  1.5 16.0 %collective-permute-start = (bf16[64,64]{1,0:T(8,128)(2,1)S(1)}, bf16[64,64]{1,0:T(8,128)(2,1)S(1)}, u32[]{:S(2)}, u32[]{:S(2)}) collective-permute-start(bf16[64,64]{1,0:T(8,128)(2,1)S(1)} %slice.19), channel_id=1, source_target_pairs={{0,1008},{16,0},{32,16},{48,32},{64,48},{80,64},{96,80},{112,96},{... | collective-permute-start | bytes 24584 | tf_op jit(solution)/shard_map/ppermute | solution.py:16
  17.5 1.4 fusion.8
  22.2 3.7 %fusion.2 = bf16[2,576,576]{2,1,0:T(8,128)(2,1)} fusion(s32[2,343]{1,0:T(2,128)} %param.5, bf16[2,343,343]{2,0,1:T(2,128)(2,1)S(1)} %copy-done), kind=kOutput, calls=%fused_computation.3 | convolution fusion | flops 728108928 | bytes 1800444 | tf_op jit(solution)/shard_map/cai,cak->cik/dot_general | solution.py:34
  25.9 0.6 pad_maximum_fusion.7.coef
  26.7 0.6 convert_element_type.12.ghost
  27.3 0.6 broadcast_in_dim.4.chip.link
  27.9 2.6 %degree.8 = (f32[64,512]{1,0:T(8,128)}, f32[64,512]{1,0:T(8,128)}, f32[64,64]{1,0:T(8,128)}, f32[64,64]{1,0:T(8,128)}, f32[64,64]{1,0:T(8,128)}) custom-call(s32[1]{0:T(128)} %bitcast.flag, f32[3]{0:T(128)} %pad_maximum_fusion.7.coef, f32[64,512]{1,0:T(8,128)} %previous.1, f32[64,64]{1,0:T(8,128)} %convert_element_type.12.ghost, ...), custom_call_target="tpu_custom_call" | custom-call | tf_op jit(solution)/shard_map/degree/pallas_call | solution.py:158
  30.5 1.9 collective-permute-start.1
  32.4 1.9 collective-permute-start.2
  34.3 0.6 pad_maximum_fusion.6.coef
  35.0 3.7 %collective-permute-done.2.link = f32[64,64]{1,0:T(8,128)S(1)} collective-permute-done((f32[64,64]{1,0:T(8,128)}, f32[64,64]{1,0:T(8,128)S(1)}, u32[]{:S(2)}, u32[]{:S(2)}) %collective-permute-start.2) | collective-permute-done | bytes 16416 | tf_op jit(solution)/shard_map/ppermute | solution.py:25
  38.7 0.6 copy-done.9
  39.3 2.6 %degree.9 = (f32[64,512]{1,0:T(8,128)}, f32[64,512]{1,0:T(8,128)}, f32[64,64]{1,0:T(8,128)}, f32[64,64]{1,0:T(8,128)}, f32[64,64]{1,0:T(8,128)}) custom-call(s32[1]{0:T(128)} %bitcast.flag, f32[3]{0:T(128)} %pad_maximum_fusion.6.coef, f32[64,512]{1,0:T(8,128)} %get-tuple-element.45.own, f32[64,64]{1,0:T(8,128)} %get-tuple-element.46.ghost, ...), custom_call_target="tpu_custom_call" | custom-call | tf_op jit(solution)/shard_map/degree/pallas_call | solution.py:158
  42.0 5.7 %collective-permute-start.3 = (f32[64,64]{1,0:T(8,128)}, f32[64,64]{1,0:T(8,128)S(1)}, u32[]{:S(2)}, u32[]{:S(2)}) collective-permute-start(f32[64,64]{1,0:T(8,128)} %get-tuple-element.52), channel_id=1, source_target_pairs={{0,16},{16,0},{32,48},{48,32},{64,80},{80,64},{96,112},{112,96},{1... | collective-permute-start | bytes 49160 | tf_op jit(solution)/shard_map/ppermute | solution.py:25
  47.7 1.9 collective-permute-start.4
  49.6 0.6 pad_maximum_fusion.5.coef
  50.3 3.7 %collective-permute-done.4.link = f32[64,64]{1,0:T(8,128)S(1)} collective-permute-done((f32[64,64]{1,0:T(8,128)}, f32[64,64]{1,0:T(8,128)S(1)}, u32[]{:S(2)}, u32[]{:S(2)}) %collective-permute-start.4) | collective-permute-done | bytes 16416 | tf_op jit(solution)/shard_map/ppermute | solution.py:25
  54.0 0.6 copy-done.10
  54.6 2.6 %degree.10 = (f32[64,512]{1,0:T(8,128)}, f32[64,512]{1,0:T(8,128)}, f32[64,64]{1,0:T(8,128)}, f32[64,64]{1,0:T(8,128)}, f32[64,64]{1,0:T(8,128)}) custom-call(s32[1]{0:T(128)} %bitcast.flag, f32[3]{0:T(128)} %pad_maximum_fusion.5.coef, f32[64,512]{1,0:T(8,128)} %get-tuple-element.50.own, f32[64,64]{1,0:T(8,128)} %get-tuple-element.51.ghost, ...), custom_call_target="tpu_custom_call" | custom-call | tf_op jit(solution)/shard_map/degree/pallas_call | solution.py:158
  57.2 5.2 %collective-permute-start.5 = (f32[64,64]{1,0:T(8,128)}, f32[64,64]{1,0:T(8,128)S(1)}, u32[]{:S(2)}, u32[]{:S(2)}) collective-permute-start(f32[64,64]{1,0:T(8,128)} %get-tuple-element.57), channel_id=1, source_target_pairs={{0,16},{16,0},{32,48},{48,32},{64,80},{80,64},{96,112},{112,96},{1... | collective-permute-start | bytes 49160 | tf_op jit(solution)/shard_map/ppermute | solution.py:25
  62.5 1.9 collective-permute-start.6
  64.4 0.7 pad_maximum_fusion.4.coef
  65.1 3.6 %collective-permute-done.6.link = f32[64,64]{1,0:T(8,128)S(1)} collective-permute-done((f32[64,64]{1,0:T(8,128)}, f32[64,64]{1,0:T(8,128)S(1)}, u32[]{:S(2)}, u32[]{:S(2)}) %collective-permute-start.6) | collective-permute-done | bytes 16416 | tf_op jit(solution)/shard_map/ppermute | solution.py:25
  68.8 0.6 copy-done.11
  69.4 2.6 %degree.11 = (f32[64,512]{1,0:T(8,128)}, f32[64,512]{1,0:T(8,128)}, f32[64,64]{1,0:T(8,128)}, f32[64,64]{1,0:T(8,128)}, f32[64,64]{1,0:T(8,128)}) custom-call(s32[1]{0:T(128)} %bitcast.flag, f32[3]{0:T(128)} %pad_maximum_fusion.4.coef, f32[64,512]{1,0:T(8,128)} %get-tuple-element.55.own, f32[64,64]{1,0:T(8,128)} %get-tuple-element.56.ghost, ...), custom_call_target="tpu_custom_call" | custom-call | tf_op jit(solution)/shard_map/degree/pallas_call | solution.py:158
  72.0 5.2 %collective-permute-start.7 = (f32[64,64]{1,0:T(8,128)}, f32[64,64]{1,0:T(8,128)S(1)}, u32[]{:S(2)}, u32[]{:S(2)}) collective-permute-start(f32[64,64]{1,0:T(8,128)} %get-tuple-element.62), channel_id=1, source_target_pairs={{0,16},{16,0},{32,48},{48,32},{64,80},{80,64},{96,112},{112,96},{1... | collective-permute-start | bytes 49160 | tf_op jit(solution)/shard_map/ppermute | solution.py:25
  77.3 1.9 collective-permute-start.8
  79.2 0.6 pad_maximum_fusion.3.coef
  79.9 3.7 %collective-permute-done.8.link = f32[64,64]{1,0:T(8,128)S(1)} collective-permute-done((f32[64,64]{1,0:T(8,128)}, f32[64,64]{1,0:T(8,128)S(1)}, u32[]{:S(2)}, u32[]{:S(2)}) %collective-permute-start.8) | collective-permute-done | bytes 16416 | tf_op jit(solution)/shard_map/ppermute | solution.py:25
  83.6 0.6 copy-done.12
  84.2 2.6 %degree.12 = (f32[64,512]{1,0:T(8,128)}, f32[64,512]{1,0:T(8,128)}, f32[64,64]{1,0:T(8,128)}, f32[64,64]{1,0:T(8,128)}, f32[64,64]{1,0:T(8,128)}) custom-call(s32[1]{0:T(128)} %bitcast.flag, f32[3]{0:T(128)} %pad_maximum_fusion.3.coef, f32[64,512]{1,0:T(8,128)} %get-tuple-element.60.own, f32[64,64]{1,0:T(8,128)} %get-tuple-element.61.ghost, ...), custom_call_target="tpu_custom_call" | custom-call | tf_op jit(solution)/shard_map/degree/pallas_call | solution.py:158
  86.8 5.2 %collective-permute-start.9 = (f32[64,64]{1,0:T(8,128)}, f32[64,64]{1,0:T(8,128)S(1)}, u32[]{:S(2)}, u32[]{:S(2)}) collective-permute-start(f32[64,64]{1,0:T(8,128)} %get-tuple-element.67), channel_id=1, source_target_pairs={{0,16},{16,0},{32,48},{48,32},{64,80},{80,64},{96,112},{112,96},{1... | collective-permute-start | bytes 49160 | tf_op jit(solution)/shard_map/ppermute | solution.py:25
  92.0 1.9 collective-permute-start.10
  94.0 0.7 pad_maximum_fusion.2.coef
  94.8 3.6 %collective-permute-done.10.link = f32[64,64]{1,0:T(8,128)S(1)} collective-permute-done((f32[64,64]{1,0:T(8,128)}, f32[64,64]{1,0:T(8,128)S(1)}, u32[]{:S(2)}, u32[]{:S(2)}) %collective-permute-start.10) | collective-permute-done | bytes 16416 | tf_op jit(solution)/shard_map/ppermute | solution.py:25
  98.4 0.6 copy-done.13
  99.0 2.6 %degree.13 = (f32[64,512]{1,0:T(8,128)}, f32[64,512]{1,0:T(8,128)}, f32[64,64]{1,0:T(8,128)}, f32[64,64]{1,0:T(8,128)}, f32[64,64]{1,0:T(8,128)}) custom-call(s32[1]{0:T(128)} %bitcast.flag, f32[3]{0:T(128)} %pad_maximum_fusion.2.coef, f32[64,512]{1,0:T(8,128)} %get-tuple-element.65.own, f32[64,64]{1,0:T(8,128)} %get-tuple-element.66.ghost, ...), custom_call_target="tpu_custom_call" | custom-call | tf_op jit(solution)/shard_map/degree/pallas_call | solution.py:158
  101.6 5.2 %collective-permute-start.11 = (f32[64,64]{1,0:T(8,128)}, f32[64,64]{1,0:T(8,128)S(1)}, u32[]{:S(2)}, u32[]{:S(2)}) collective-permute-start(f32[64,64]{1,0:T(8,128)} %get-tuple-element.72), channel_id=1, source_target_pairs={{0,16},{16,0},{32,48},{48,32},{64,80},{80,64},{96,112},{112,96},{1... | collective-permute-start | bytes 49160 | tf_op jit(solution)/shard_map/ppermute | solution.py:25
  106.9 1.9 collective-permute-start.12
  108.8 0.7 pad_maximum_fusion.1.coef
  109.6 3.6 %collective-permute-done.12.link = f32[64,64]{1,0:T(8,128)S(1)} collective-permute-done((f32[64,64]{1,0:T(8,128)}, f32[64,64]{1,0:T(8,128)S(1)}, u32[]{:S(2)}, u32[]{:S(2)}) %collective-permute-start.12) | collective-permute-done | bytes 16416 | tf_op jit(solution)/shard_map/ppermute | solution.py:25
  113.2 0.6 copy-done.3
  113.8 2.6 %degree.14 = (f32[64,512]{1,0:T(8,128)}, f32[64,512]{1,0:T(8,128)}, f32[64,64]{1,0:T(8,128)}, f32[64,64]{1,0:T(8,128)}, f32[64,64]{1,0:T(8,128)}) custom-call(s32[1]{0:T(128)} %bitcast.flag, f32[3]{0:T(128)} %pad_maximum_fusion.1.coef, f32[64,512]{1,0:T(8,128)} %get-tuple-element.70.own, f32[64,64]{1,0:T(8,128)} %get-tuple-element.71.ghost, ...), custom_call_target="tpu_custom_call" | custom-call | tf_op jit(solution)/shard_map/degree/pallas_call | solution.py:158
  116.4 5.2 %collective-permute-start.13 = (f32[64,64]{1,0:T(8,128)}, f32[64,64]{1,0:T(8,128)S(1)}, u32[]{:S(2)}, u32[]{:S(2)}) collective-permute-start(f32[64,64]{1,0:T(8,128)} %get-tuple-element.77), channel_id=1, source_target_pairs={{0,16},{16,0},{32,48},{48,32},{64,80},{80,64},{96,112},{112,96},{1... | collective-permute-start | bytes 49160 | tf_op jit(solution)/shard_map/ppermute | solution.py:25
  121.6 1.9 collective-permute-start.14
  123.6 0.7 pad_maximum_fusion.coef
  124.2 3.7 %collective-permute-done.14.link = f32[64,64]{1,0:T(8,128)S(1)} collective-permute-done((f32[64,64]{1,0:T(8,128)}, f32[64,64]{1,0:T(8,128)S(1)}, u32[]{:S(2)}, u32[]{:S(2)}) %collective-permute-start.14) | collective-permute-done | bytes 16416 | tf_op jit(solution)/shard_map/ppermute | solution.py:25
  128.0 0.6 copy-done.15
  128.6 2.6 %degree.15 = (f32[64,512]{1,0:T(8,128)}, f32[64,512]{1,0:T(8,128)}, f32[64,64]{1,0:T(8,128)}, f32[64,64]{1,0:T(8,128)}, f32[64,64]{1,0:T(8,128)}) custom-call(s32[1]{0:T(128)} %bitcast.flag, f32[3]{0:T(128)} %pad_maximum_fusion.coef, f32[64,512]{1,0:T(8,128)} %get-tuple-element.75.own, f32[64,64]{1,0:T(8,128)} %get-tuple-element.76.ghost, ...), custom_call_target="tpu_custom_call" | custom-call | tf_op jit(solution)/shard_map/degree/pallas_call | solution.py:158
  131.2 5.2 %collective-permute-start.15 = (f32[64,64]{1,0:T(8,128)}, f32[64,64]{1,0:T(8,128)S(1)}, u32[]{:S(2)}, u32[]{:S(2)}) collective-permute-start(f32[64,64]{1,0:T(8,128)} %get-tuple-element.82), channel_id=1, source_target_pairs={{0,16},{16,0},{32,48},{48,32},{64,80},{80,64},{96,112},{112,96},{1... | collective-permute-start | bytes 49160 | tf_op jit(solution)/shard_map/ppermute | solution.py:25
  136.5 1.9 collective-permute-start.16
  138.4 4.4 %collective-permute-done.16.link = f32[64,64]{1,0:T(8,128)S(1)} collective-permute-done((f32[64,64]{1,0:T(8,128)}, f32[64,64]{1,0:T(8,128)S(1)}, u32[]{:S(2)}, u32[]{:S(2)}) %collective-permute-start.16) | collective-permute-done | bytes 16416 | tf_op jit(solution)/shard_map/ppermute | solution.py:25
  142.8 0.6 copy-done.17
  143.4 2.5 %image.1 = (f32[64,512]{1,0:T(8,128)}, bf16[64,512]{1,0:T(8,128)(2,1)}, f32[64,512]{1,0:T(8,128)}, f32[64,64]{1,0:T(8,128)}) custom-call(s32[1]{0:T(128)} %bitcast.flag, f32[64,512]{1,0:T(8,128)} %get-tuple-element.80.own, f32[64,64]{1,0:T(8,128)} %get-tuple-element.81.ghost, f32[64,64]{1,0:T(8,128)} %copy-done.16, f32[64,64]{1,0:T(8,128)} %copy-done.17, ...), custom_call_target="tpu_custom_call" | custom-call | tf_op jit(solution)/shard_map/image/pallas_call | solution.py:163
  145.9 1.9 broadcast_in_dim.5
  147.9 10.6 %all-to-all-start = ((bf16[16,64,512]{2,1,0:T(8,128)(2,1)}), bf16[16,64,512]{2,1,0:T(8,128)(2,1)S(1)}, u32[]{:S(2)}, u32[]{:S(2)}) async-start(bf16[16,64,512]{2,1,0:T(8,128)(2,1)} %broadcast_in_dim.5), calls=%async_computation | async-start | bytes 2097152 | tf_op jit(solution)/shard_map/all_to_all | solution.py:166
  158.5 2.2 %collective-permute-start.17 = (f32[64,64]{1,0:T(8,128)S(1)}, f32[64,64]{1,0:T(8,128)S(1)}, u32[]{:S(2)}, u32[]{:S(2)}) collective-permute-start(f32[64,64]{1,0:T(8,128)S(1)} %copy-done.19), channel_id=1, source_target_pairs={{0,16},{16,32},{32,48},{48,64},{64,80},{80,96},{96,112},{112,128},... | collective-permute-start | bytes 49160 | tf_op jit(solution)/shard_map/ppermute | solution.py:16
  160.7 7.2 %collective-permute-done.17.incoming = f32[64,64]{1,0:T(8,128)S(1)} collective-permute-done((f32[64,64]{1,0:T(8,128)S(1)}, f32[64,64]{1,0:T(8,128)S(1)}, u32[]{:S(2)}, u32[]{:S(2)}) %collective-permute-start.17) | collective-permute-done | bytes 16416 | tf_op jit(solution)/shard_map/ppermute | solution.py:16
  167.9 15.8 %all-to-all-done = bf16[16,64,512]{2,1,0:T(8,128)(2,1)S(1)} async-done(((bf16[16,64,512]{2,1,0:T(8,128)(2,1)}), bf16[16,64,512]{2,1,0:T(8,128)(2,1)S(1)}, u32[]{:S(2)}, u32[]{:S(2)}) %all-to-all-start) | async-done | bytes 1048608 | tf_op jit(solution)/shard_map/all_to_all | solution.py:166
  183.7 1.0 copy-done.1
  184.7 2.5 %project.1 = f32[64,8,128]{2,1,0:T(8,128)} custom-call(bf16[1024,512]{1,0:T(8,128)(2,1)} %bitcast.42, f32[64,512]{1,0:T(8,128)} %get-tuple-element.86.product, f32[64,64]{1,0:T(8,128)} %copy-done.18), custom_call_target="tpu_custom_call" | custom-call | tf_op jit(solution)/shard_map/project/pallas_call | solution.py:172
  187.2 24.3 %all_to_all.10 = f32[64,8,128]{2,1,0:T(8,128)S(1)} all-to-all(f32[64,8,128]{2,1,0:T(8,128)} %project.1), channel_id=1, replica_groups=mesh['cell'=64,'state'=16] {'cell'}, dimensions={0} | all-to-all | bytes 524288 | tf_op jit(solution)/shard_map/all_to_all | solution.py:179
  211.6 0.6 copy.12
  (42 shorter events, 0.2 us)
Async XLA Ops:
  0.6 21.5 %copy-start = (bf16[2,343,343]{2,0,1:T(2,128)(2,1)S(1)}, bf16[2,343,343]{2,0,1:T(2,128)(2,1)}, u32[]{:S(2)}) copy-start(bf16[2,343,343]{2,0,1:T(2,128)(2,1)} %param.6) | copy-start | bytes 1411792
  1.5 25.2 %collective-permute-start = (bf16[64,64]{1,0:T(8,128)(2,1)S(1)}, bf16[64,64]{1,0:T(8,128)(2,1)S(1)}, u32[]{:S(2)}, u32[]{:S(2)}) collective-permute-start(bf16[64,64]{1,0:T(8,128)(2,1)S(1)} %slice.19), channel_id=1, source_target_pairs={{0,1008},{16,0},{32,16},{48,32},{64,48},{80,64},{96,80},{112,96},{... | collective-permute-start | bytes 24584 | tf_op jit(solution)/shard_map/ppermute | solution.py:16
  30.5 4.5 %collective-permute-start.1 = (f32[64,64]{1,0:T(8,128)}, f32[64,64]{1,0:T(8,128)S(1)}, u32[]{:S(2)}, u32[]{:S(2)}) collective-permute-start(f32[64,64]{1,0:T(8,128)} %get-tuple-element.47), channel_id=1, source_target_pairs={{0,16},{16,0},{32,48},{48,32},{64,80},{80,64},{96,112},{112,96},{1... | collective-permute-start | bytes 49160 | tf_op jit(solution)/shard_map/ppermute | solution.py:25
  32.4 6.3 %collective-permute-start.2 = (f32[64,64]{1,0:T(8,128)}, f32[64,64]{1,0:T(8,128)S(1)}, u32[]{:S(2)}, u32[]{:S(2)}) collective-permute-start(f32[64,64]{1,0:T(8,128)} %get-tuple-element.48), channel_id=1, source_target_pairs={{16,32},{32,16},{48,64},{64,48},{80,96},{96,80},{112,128},{128,112... | collective-permute-start | bytes 49160 | tf_op jit(solution)/shard_map/ppermute | solution.py:25
  35.0 3.7 %copy-start.4 = (f32[64,64]{1,0:T(8,128)}, f32[64,64]{1,0:T(8,128)S(1)}, u32[]{:S(2)}) copy-start(f32[64,64]{1,0:T(8,128)S(1)} %collective-permute-done.1.chip) | copy-start | bytes 49156
  38.7 0.6 copy-start.9
  42.0 8.3 %collective-permute-start.3 = (f32[64,64]{1,0:T(8,128)}, f32[64,64]{1,0:T(8,128)S(1)}, u32[]{:S(2)}, u32[]{:S(2)}) collective-permute-start(f32[64,64]{1,0:T(8,128)} %get-tuple-element.52), channel_id=1, source_target_pairs={{0,16},{16,0},{32,48},{48,32},{64,80},{80,64},{96,112},{112,96},{1... | collective-permute-start | bytes 49160 | tf_op jit(solution)/shard_map/ppermute | solution.py:25
  47.7 6.3 %collective-permute-start.4 = (f32[64,64]{1,0:T(8,128)}, f32[64,64]{1,0:T(8,128)S(1)}, u32[]{:S(2)}, u32[]{:S(2)}) collective-permute-start(f32[64,64]{1,0:T(8,128)} %get-tuple-element.53), channel_id=1, source_target_pairs={{16,32},{32,16},{48,64},{64,48},{80,96},{96,80},{112,128},{128,112... | collective-permute-start | bytes 49160 | tf_op jit(solution)/shard_map/ppermute | solution.py:25
  50.3 3.7 %copy-start.5 = (f32[64,64]{1,0:T(8,128)}, f32[64,64]{1,0:T(8,128)S(1)}, u32[]{:S(2)}) copy-start(f32[64,64]{1,0:T(8,128)S(1)} %collective-permute-done.3.chip) | copy-start | bytes 49156
  54.0 0.6 copy-start.10
  57.2 7.9 %collective-permute-start.5 = (f32[64,64]{1,0:T(8,128)}, f32[64,64]{1,0:T(8,128)S(1)}, u32[]{:S(2)}, u32[]{:S(2)}) collective-permute-start(f32[64,64]{1,0:T(8,128)} %get-tuple-element.57), channel_id=1, source_target_pairs={{0,16},{16,0},{32,48},{48,32},{64,80},{80,64},{96,112},{112,96},{1... | collective-permute-start | bytes 49160 | tf_op jit(solution)/shard_map/ppermute | solution.py:25
  62.5 6.3 %collective-permute-start.6 = (f32[64,64]{1,0:T(8,128)}, f32[64,64]{1,0:T(8,128)S(1)}, u32[]{:S(2)}, u32[]{:S(2)}) collective-permute-start(f32[64,64]{1,0:T(8,128)} %get-tuple-element.58), channel_id=1, source_target_pairs={{16,32},{32,16},{48,64},{64,48},{80,96},{96,80},{112,128},{128,112... | collective-permute-start | bytes 49160 | tf_op jit(solution)/shard_map/ppermute | solution.py:25
  65.1 3.7 %copy-start.6 = (f32[64,64]{1,0:T(8,128)}, f32[64,64]{1,0:T(8,128)S(1)}, u32[]{:S(2)}) copy-start(f32[64,64]{1,0:T(8,128)S(1)} %collective-permute-done.5.chip) | copy-start | bytes 49156
  68.8 0.6 copy-start.11
  72.0 7.9 %collective-permute-start.7 = (f32[64,64]{1,0:T(8,128)}, f32[64,64]{1,0:T(8,128)S(1)}, u32[]{:S(2)}, u32[]{:S(2)}) collective-permute-start(f32[64,64]{1,0:T(8,128)} %get-tuple-element.62), channel_id=1, source_target_pairs={{0,16},{16,0},{32,48},{48,32},{64,80},{80,64},{96,112},{112,96},{1... | collective-permute-start | bytes 49160 | tf_op jit(solution)/shard_map/ppermute | solution.py:25
  77.3 6.3 %collective-permute-start.8 = (f32[64,64]{1,0:T(8,128)}, f32[64,64]{1,0:T(8,128)S(1)}, u32[]{:S(2)}, u32[]{:S(2)}) collective-permute-start(f32[64,64]{1,0:T(8,128)} %get-tuple-element.63), channel_id=1, source_target_pairs={{16,32},{32,16},{48,64},{64,48},{80,96},{96,80},{112,128},{128,112... | collective-permute-start | bytes 49160 | tf_op jit(solution)/shard_map/ppermute | solution.py:25
  79.9 3.7 %copy-start.7 = (f32[64,64]{1,0:T(8,128)}, f32[64,64]{1,0:T(8,128)S(1)}, u32[]{:S(2)}) copy-start(f32[64,64]{1,0:T(8,128)S(1)} %collective-permute-done.7.chip) | copy-start | bytes 49156
  83.6 0.6 copy-start.12
  86.8 7.9 %collective-permute-start.9 = (f32[64,64]{1,0:T(8,128)}, f32[64,64]{1,0:T(8,128)S(1)}, u32[]{:S(2)}, u32[]{:S(2)}) collective-permute-start(f32[64,64]{1,0:T(8,128)} %get-tuple-element.67), channel_id=1, source_target_pairs={{0,16},{16,0},{32,48},{48,32},{64,80},{80,64},{96,112},{112,96},{1... | collective-permute-start | bytes 49160 | tf_op jit(solution)/shard_map/ppermute | solution.py:25
  92.0 6.3 %collective-permute-start.10 = (f32[64,64]{1,0:T(8,128)}, f32[64,64]{1,0:T(8,128)S(1)}, u32[]{:S(2)}, u32[]{:S(2)}) collective-permute-start(f32[64,64]{1,0:T(8,128)} %get-tuple-element.68), channel_id=1, source_target_pairs={{16,32},{32,16},{48,64},{64,48},{80,96},{96,80},{112,128},{128,112... | collective-permute-start | bytes 49160 | tf_op jit(solution)/shard_map/ppermute | solution.py:25
  94.7 3.6 %copy-start.8 = (f32[64,64]{1,0:T(8,128)}, f32[64,64]{1,0:T(8,128)S(1)}, u32[]{:S(2)}) copy-start(f32[64,64]{1,0:T(8,128)S(1)} %collective-permute-done.9.chip) | copy-start | bytes 49156
  98.4 0.6 copy-start.13
  101.6 7.9 %collective-permute-start.11 = (f32[64,64]{1,0:T(8,128)}, f32[64,64]{1,0:T(8,128)S(1)}, u32[]{:S(2)}, u32[]{:S(2)}) collective-permute-start(f32[64,64]{1,0:T(8,128)} %get-tuple-element.72), channel_id=1, source_target_pairs={{0,16},{16,0},{32,48},{48,32},{64,80},{80,64},{96,112},{112,96},{1... | collective-permute-start | bytes 49160 | tf_op jit(solution)/shard_map/ppermute | solution.py:25
  106.9 6.3 %collective-permute-start.12 = (f32[64,64]{1,0:T(8,128)}, f32[64,64]{1,0:T(8,128)S(1)}, u32[]{:S(2)}, u32[]{:S(2)}) collective-permute-start(f32[64,64]{1,0:T(8,128)} %get-tuple-element.73), channel_id=1, source_target_pairs={{16,32},{32,16},{48,64},{64,48},{80,96},{96,80},{112,128},{128,112... | collective-permute-start | bytes 49160 | tf_op jit(solution)/shard_map/ppermute | solution.py:25
  109.6 3.6 %copy-start.2 = (f32[64,64]{1,0:T(8,128)}, f32[64,64]{1,0:T(8,128)S(1)}, u32[]{:S(2)}) copy-start(f32[64,64]{1,0:T(8,128)S(1)} %collective-permute-done.11.chip) | copy-start | bytes 49156
  113.2 0.6 copy-start.3
  116.4 7.8 %collective-permute-start.13 = (f32[64,64]{1,0:T(8,128)}, f32[64,64]{1,0:T(8,128)S(1)}, u32[]{:S(2)}, u32[]{:S(2)}) collective-permute-start(f32[64,64]{1,0:T(8,128)} %get-tuple-element.77), channel_id=1, source_target_pairs={{0,16},{16,0},{32,48},{48,32},{64,80},{80,64},{96,112},{112,96},{1... | collective-permute-start | bytes 49160 | tf_op jit(solution)/shard_map/ppermute | solution.py:25
  121.6 6.3 %collective-permute-start.14 = (f32[64,64]{1,0:T(8,128)}, f32[64,64]{1,0:T(8,128)S(1)}, u32[]{:S(2)}, u32[]{:S(2)}) collective-permute-start(f32[64,64]{1,0:T(8,128)} %get-tuple-element.78), channel_id=1, source_target_pairs={{16,32},{32,16},{48,64},{64,48},{80,96},{96,80},{112,128},{128,112... | collective-permute-start | bytes 49160 | tf_op jit(solution)/shard_map/ppermute | solution.py:25
  124.2 3.7 %copy-start.14 = (f32[64,64]{1,0:T(8,128)}, f32[64,64]{1,0:T(8,128)S(1)}, u32[]{:S(2)}) copy-start(f32[64,64]{1,0:T(8,128)S(1)} %collective-permute-done.13.chip) | copy-start | bytes 49156
  128.0 0.6 copy-start.15
  131.2 7.2 %collective-permute-start.15 = (f32[64,64]{1,0:T(8,128)}, f32[64,64]{1,0:T(8,128)S(1)}, u32[]{:S(2)}, u32[]{:S(2)}) collective-permute-start(f32[64,64]{1,0:T(8,128)} %get-tuple-element.82), channel_id=1, source_target_pairs={{0,16},{16,0},{32,48},{48,32},{64,80},{80,64},{96,112},{112,96},{1... | collective-permute-start | bytes 49160 | tf_op jit(solution)/shard_map/ppermute | solution.py:25
  136.5 6.3 %collective-permute-start.16 = (f32[64,64]{1,0:T(8,128)}, f32[64,64]{1,0:T(8,128)S(1)}, u32[]{:S(2)}, u32[]{:S(2)}) collective-permute-start(f32[64,64]{1,0:T(8,128)} %get-tuple-element.83), channel_id=1, source_target_pairs={{16,32},{32,16},{48,64},{64,48},{80,96},{96,80},{112,128},{128,112... | collective-permute-start | bytes 49160 | tf_op jit(solution)/shard_map/ppermute | solution.py:25
  138.4 4.4 %copy-start.16 = (f32[64,64]{1,0:T(8,128)}, f32[64,64]{1,0:T(8,128)S(1)}, u32[]{:S(2)}) copy-start(f32[64,64]{1,0:T(8,128)S(1)} %collective-permute-done.15.chip) | copy-start | bytes 49156
  142.8 0.6 copy-start.17
  145.9 12.6 %copy-start.19 = (f32[64,64]{1,0:T(8,128)S(1)}, f32[64,64]{1,0:T(8,128)}, u32[]{:S(2)}) copy-start(f32[64,64]{1,0:T(8,128)} %get-tuple-element.87) | copy-start | bytes 49156
  147.9 35.8 %all-to-all-start = ((bf16[16,64,512]{2,1,0:T(8,128)(2,1)}), bf16[16,64,512]{2,1,0:T(8,128)(2,1)S(1)}, u32[]{:S(2)}, u32[]{:S(2)}) async-start(bf16[16,64,512]{2,1,0:T(8,128)(2,1)} %broadcast_in_dim.5), calls=%async_computation | async-start | bytes 2097152 | tf_op jit(solution)/shard_map/all_to_all | solution.py:166
  158.5 9.4 %collective-permute-start.17 = (f32[64,64]{1,0:T(8,128)S(1)}, f32[64,64]{1,0:T(8,128)S(1)}, u32[]{:S(2)}, u32[]{:S(2)}) collective-permute-start(f32[64,64]{1,0:T(8,128)S(1)} %copy-done.19), channel_id=1, source_target_pairs={{0,16},{16,32},{32,48},{48,64},{64,80},{80,96},{96,112},{112,128},... | collective-permute-start | bytes 49160 | tf_op jit(solution)/shard_map/ppermute | solution.py:16
  167.9 15.8 %copy-start.18 = (f32[64,64]{1,0:T(8,128)}, f32[64,64]{1,0:T(8,128)S(1)}, u32[]{:S(2)}) copy-start(f32[64,64]{1,0:T(8,128)S(1)} %collective-permute-done.17.incoming) | copy-start | bytes 49156
  183.7 1.0 copy-start.1
where the time goes:
time: 213 us; the launch traced here: 212 us
  starting transfers between devices  83.1 us (39%)
  waiting for transfers between devices  53.2 us (25%)
  Pallas kernels  25.9 us (12%)
  blocking collectives  24.3 us (11%)
  local copies, waits for them, and re-layouts  11.3 us (5%)
  other arithmetic  5.72 us (3%)
  between operations  4.93 us (2%)
  matrix products  3.71 us (2%)
    ppermute x16, starting transfers between devices, swapped(): return lax.ppermute(value, axis, pairs)  54.4 us
    ppermute x16, waiting for transfers between devices, swapped(): return lax.ppermute(value, axis, pairs)  30.2 us
    all_to_all x1, blocking collectives, per_device(): arrived = lax.all_to_all(pieces, 'cell', 0, 0, tiled=True)  24.3 us
    pallas_call x8, Pallas kernels, per_device(): step(flag, coef, own, ghost, chip, link, previous, weights)  20.9 us
    ppermute x2, starting transfers between devices, passed_along(): return lax.ppermute(value, axis, pairs)  18.2 us
    all_to_all x1, waiting for transfers between devices, per_device(): lax.all_to_all(jnp.broadcast_to(low[None], (peers, states, owned)), 'stat...  15.8 us
    all_to_all x1, starting transfers between devices, per_device(): lax.all_to_all(jnp.broadcast_to(low[None], (peers, states, owned)), 'stat...  10.6 us
    ppermute x2, waiting for transfers between devices, passed_along(): return lax.ppermute(value, axis, pairs)  7.18 us
  transfers between devices with their start and end apart: 19, of which 10 were waited for; matrix products, arithmetic and copies ran while one was open for 5% of the time, Pallas kernels for 0%

commit v1 on v0

v1 whole, which is shorter than its diff:
```python
import functools

import jax
import jax.numpy as jnp
from jax import lax
from jax.experimental import pallas as pl
from jax.experimental.pallas import tpu as pltpu
from jax.sharding import PartitionSpec as P

DEGREE = 8


def passed_along(value, axis, steps):
    count = lax.axis_size(axis)
    pairs = [(source, (source + steps) % count) for source in range(count)]
    return lax.ppermute(value, axis, pairs)


def swapped(value, axis, first):
    count = lax.axis_size(axis)
    pairs = []
    for low in range(first, first + count, 2):
        left, right = low % count, (low + 1) % count
        pairs += [(left, right), (right, left)]
    return lax.ppermute(value, axis, pairs)


def scattered(connectivity, cell_matrices, extent):
    nodes = lax.broadcasted_iota(jnp.int32, (*connectivity.shape, extent), 2)
    chosen = (connectivity[:, :, None] == nodes).astype(jnp.bfloat16)
    half = jnp.einsum(
        "cba,cbk->cak", cell_matrices, chosen, preferred_element_type=jnp.float32
    ).astype(jnp.bfloat16)
    whole = jnp.einsum("cai,cak->cik", chosen, half, preferred_element_type=jnp.float32)
    return whole.astype(jnp.bfloat16)


def completed(flag, own, ghost, chip, link):
    even = flag[0] == 0
    first = ghost.shape[1]
    left = jnp.where(even, link, chip)
    right = jnp.where(even, chip, link)
    return own[:, :first] + left, ghost + right


def multiplied(extended, weights, cells):
    total = None
    for cell in range(cells):
        part = jnp.dot(
            extended,
            weights[cell],
            preferred_element_type=jnp.float32,
        )
        total = part if total is None else total + part
    return total


def advanced(cells, flag, coef, values, right, previous, weights, upcoming, spill, to_chip, to_link, extended):
    shared, owned = right.shape[1], values.shape[1]
    extended[:, :owned] = values.astype(jnp.bfloat16)
    extended[:, owned:] = right.astype(jnp.bfloat16)
    product = multiplied(extended[...], weights, cells)
    fresh = coef[0] * product[:, :owned] + coef[1] * values
    if previous is not None:
        fresh = fresh + coef[2] * previous
    beyond = coef[0] * product[:, owned:]
    upcoming[...] = fresh
    spill[...] = beyond
    even = flag[0] == 0
    first = fresh[:, :shared]
    to_chip[...] = jnp.where(even, beyond, first)
    to_link[...] = jnp.where(even, first, beyond)


def first_body(cells, flag, coef, start, ghost, weights, upcoming, spill, to_chip, to_link, extended):
    advanced(cells, flag, coef, start[...], ghost[...], None, weights, upcoming, spill, to_chip, to_link, extended)


def degree_body(cells, flag, coef, own, ghost, chip, link, previous, weights, current, upcoming, spill, to_chip, to_link, extended):
    shared = ghost.shape[1]
    left, right = completed(flag, own[...], ghost[...], chip[...], link[...])
    current[...] = own[...]
    current[:, :shared] = left
    advanced(cells, flag, coef, current[...], right, previous[...], weights, upcoming, spill, to_chip, to_link, extended)


def image_body(cells, flag, own, ghost, chip, link, weights, current, low, product_out, spill, extended):
    shared, owned = ghost.shape[1], own.shape[1]
    left, right = completed(flag, own[...], ghost[...], chip[...], link[...])
    current[...] = own[...]
    current[:, :shared] = left
    values = current[...].astype(jnp.bfloat16)
    low[...] = jnp.broadcast_to(values[None], low.shape)
    extended[:, :owned] = values
    extended[:, owned:] = right.astype(jnp.bfloat16)
    product = multiplied(extended[...], weights, cells)
    product_out[...] = product[:, :owned]
    spill[...] = product[:, owned:]


def project_body(lows, product, incoming, out):
    states, shared = incoming.shape
    value = product[...]
    first = value[:, :shared] + incoming[...]
    image = jnp.concatenate([first, value[:, shared:]], axis=1).astype(jnp.bfloat16)
    partial = lax.dot_general(
        lows[...], image, (((1,), (1,)), ((), ())), preferred_element_type=jnp.float32
    )
    pieces = partial.reshape(partial.shape[0] // 16, 2, 8, states)
    out[...] = jnp.concatenate([pieces[:, 0], pieces[:, 1]], axis=2)


def kernel(body, cells, scalars, out_shape, scratch):
    def run(*operands):
        small, large = operands[:scalars], operands[scalars:]
        large = [pltpu.with_memory_space_constraint(value, pltpu.VMEM) for value in large]
        in_specs = [pl.BlockSpec(memory_space=pltpu.SMEM)] * scalars
        in_specs += [pl.BlockSpec(memory_space=pltpu.VMEM)] * len(large)
        single = not isinstance(out_shape, tuple)
        outs = pl.BlockSpec(memory_space=pltpu.VMEM)
        return pl.pallas_call(
            functools.partial(body, cells) if cells else body,
            in_specs=in_specs,
            out_specs=outs if single else (outs,) * len(out_shape),
            out_shape=out_shape,
            scratch_shapes=scratch,
            compiler_params=pltpu.CompilerParams(vmem_limit_bytes=16 * 2**20),
        )(*small, *large)

    return run


def exchanged(to_link, to_chip):
    link = swapped(to_link, "cell", 1)
    chip = swapped(to_chip, "cell", 0)
    return link, chip


def per_device(start_block, connectivity, cell_matrices, bounds):
    f32 = jnp.float32
    states, owned = start_block.shape
    shared = owned // 8
    extent = owned + shared
    cells = connectivity.shape[0]
    flag = (lax.axis_index("cell") % 2).astype(jnp.int32).reshape(1)
    weights = scattered(connectivity, cell_matrices, extent)

    peers = lax.axis_size("state")
    whole = pltpu.VMEM((states, owned), f32)
    group = pltpu.VMEM((states, shared), f32)
    bf16 = jnp.bfloat16
    scratch = [pltpu.VMEM((states, extent), bf16)]
    first = kernel(first_body, cells, 2, (whole, group, group, group), scratch)
    step = kernel(degree_body, cells, 2, (whole, whole, group, group, group), scratch)
    out = jax.ShapeDtypeStruct((states, owned), f32)
    lows = pltpu.VMEM((peers, states, owned), bf16)
    last = kernel(image_body, cells, 1, (out, lows, whole, group), scratch)

    lowest, cut, upper = (bounds[0], bounds[1], bounds[2])
    half = (upper - cut) / 2.0
    centre = (upper + cut) / 2.0
    sigma = half / (lowest - centre)
    tau = 2.0 / sigma
    coefs = [jnp.stack([sigma / half, -centre * (sigma / half), jnp.zeros((), f32)])]
    for _ in range(2, DEGREE + 1):
        sigma_new = 1.0 / (tau - sigma)
        scale = 2.0 * sigma_new / half
        coefs.append(jnp.stack([scale, -centre * scale, -(sigma * sigma_new)]))
        sigma = sigma_new

    ghost = passed_along(start_block[:, :shared].astype(bf16), "cell", -1)
    own, ghost, to_chip, to_link = first(flag, coefs[0], start_block, ghost, weights)
    previous = start_block
    for coef in coefs[1:]:
        link, chip = exchanged(to_link, to_chip)
        previous, own, ghost, to_chip, to_link = step(
            flag, coef, own, ghost, chip, link, previous, weights
        )
    link, chip = exchanged(to_link, to_chip)
    filtered, low, product, spill = last(flag, own, ghost, chip, link, weights)
    incoming = passed_along(spill, "cell", 1)
    lows = lax.all_to_all(low, "state", 0, 0, tiled=True)
    lows = lows.reshape(peers * states, owned)

    count = lax.axis_size("cell")
    rows = peers * states // count
    shape = pltpu.VMEM((peers * states // 16, 8, 2 * states), f32)
    pieces = kernel(project_body, 0, 0, shape, [])(lows, product, incoming)
    arrived = lax.all_to_all(pieces, "cell", 0, 0, tiled=True)
    total = jnp.sum(arrived.reshape(count, rows // 16, 8, 2, states), axis=0)
    projected = jnp.swapaxes(total, 1, 2).reshape(rows, states)
    return (filtered, projected)


def solution(mesh):
    in_specs = (P("state", "cell"), P("cell", None), P("cell", None, None), P())
    out_specs = (P("state", "cell"), P("cell", "state"))
    return jax.shard_map(
        per_device, mesh=mesh, in_specs=in_specs, out_specs=out_specs, check_vma=False
    )
```

time: 213 us -> 184 us (0.86)
  Pallas kernels: 25.9 us -> 9.54 us
  local copies, waits for them, and re-layouts: 11.3 us -> 2.9 us
  other arithmetic: 5.72 us -> 0.7 us
  waiting for transfers between devices: 53.2 us -> 55.8 us
    pallas_call x10, Pallas kernels: 25.9 us -> 9.54 us  [run(): pl.pallas_call(functools.partial(body, cells) if cells else body, in_spec...]
    unnamed x40 -> x4, local copies, waits for them, and re-layouts: 5.85 us -> 0.02 us
    another operation x7, other arithmetic: 4.44 us -> 0.56 us  [per_device(): coefs.append(jnp.stack([scale, -centre * scale, -(sigma * sigma_new)]))]
    broadcast_in_dim x2 -> x0, local copies, waits for them, and re-layouts: 2.55 us -> none  [the longest x1 1.94 us: per_device(): jnp.broadcast_to(low[None], (peers, states, owned))]
    ppermute x16, waiting for transfers between devices: 30.2 us -> 32.5 us  [swapped(): return lax.ppermute(value, axis, pairs)]
  transfers between devices with their start and end apart: 19 -> 19, of which waited for: 10 -> 10; matrix products, arithmetic and copies ran while one was open for 5% -> 2% of each run, Pallas kernels for 0% -> 0%
where the time goes in v1:
time: 184 us; the launch traced here: 183 us
  starting transfers between devices  83.1 us (45%)
  waiting for transfers between devices  55.8 us (30%)
  blocking collectives  23.8 us (13%)
  Pallas kernels  9.54 us (5%)
  between operations  4.94 us (3%)
  local copies, waits for them, and re-layouts  2.9 us (2%)
  matrix products  2.56 us (1%)
    ppermute x16, starting transfers between devices, swapped(): return lax.ppermute(value, axis, pairs)  54.4 us
    ppermute x16, waiting for transfers between devices, swapped(): return lax.ppermute(value, axis, pairs)  32.5 us
    all_to_all x1, blocking collectives, per_device(): arrived = lax.all_to_all(pieces, 'cell', 0, 0, tiled=True)  23.8 us
    ppermute x2, starting transfers between devices, passed_along(): return lax.ppermute(value, axis, pairs)  18.1 us
    all_to_all x1, waiting for transfers between devices, per_device(): lows = lax.all_to_all(low, 'state', 0, 0, tiled=True)  16 us
    all_to_all x1, starting transfers between devices, per_device(): lows = lax.all_to_all(low, 'state', 0, 0, tiled=True)  10.6 us
    pallas_call x10, Pallas kernels, run(): pl.pallas_call(functools.partial(body, cells) if cells else body, in_spec...  9.54 us
    ppermute x2, waiting for transfers between devices, passed_along(): return lax.ppermute(value, axis, pairs)  7.33 us
  transfers between devices with their start and end apart: 19, of which 10 were waited for; matrix products, arithmetic and copies ran while one was open for 2% of the time, Pallas kernels for 0%

profile of v1, /device:TPU:1, one launch (start us, length us, event | category | flops | bytes accessed | tf_op | source)
XLA Modules:
  0.0 183.4 jit_solution(18175695432423601257)
XLA Ops:
  0.6 0.0 copy-start
  0.6 0.8 slice.19
  1.5 16.0 %collective-permute-start = (bf16[64,64]{1,0:T(8,128)(2,1)S(1)}, bf16[64,64]{1,0:T(8,128)(2,1)S(1)}, u32[]{:S(2)}, u32[]{:S(2)}) collective-permute-start(bf16[64,64]{1,0:T(8,128)(2,1)S(1)} %slice.19), channel_id=1, source_target_pairs={{0,1008},{16,0},{32,16},{48,32},{64,48},{80,64},{96,80},{112,96},{... | collective-permute-start | bytes 24584 | tf_op jit(solution)/shard_map/ppermute | solution.py:16
  17.5 1.4 fusion.8
  22.1 0.0 copy-start.1
  22.1 2.6 %fusion.2.weights = bf16[2,576,576]{2,1,0:T(8,128)(2,1)S(1)} fusion(s32[2,343]{1,0:T(2,128)} %param.5, bf16[2,343,343]{2,0,1:T(2,128)(2,1)S(1)} %copy-done), kind=kOutput, calls=%fused_computation.3 | convolution fusion | flops 728108928 | bytes 1800444 | tf_op jit(solution)/shard_map/cai,cak->cik/dot_general | solution.py:34
  24.7 0.1 pad_maximum_fusion.7.coef
  25.0 0.0 collective-permute-done.ghost
  25.0 0.9 shard_map.59
  25.9 1.9 %collective-permute-start.1 = (f32[64,64]{1,0:T(8,128)S(1)}, f32[64,64]{1,0:T(8,128)S(1)}, u32[]{:S(2)}, u32[]{:S(2)}) collective-permute-start(f32[64,64]{1,0:T(8,128)S(1)} %get-tuple-element.46), channel_id=1, source_target_pairs={{0,16},{16,0},{32,48},{48,32},{64,80},{80,64},{96,112},{112,96},{1... | collective-permute-start | bytes 49160 | tf_op jit(solution)/shard_map/ppermute | solution.py:25
  27.9 1.9 %collective-permute-start.2 = (f32[64,64]{1,0:T(8,128)S(1)}, f32[64,64]{1,0:T(8,128)S(1)}, u32[]{:S(2)}, u32[]{:S(2)}) collective-permute-start(f32[64,64]{1,0:T(8,128)S(1)} %get-tuple-element.47), channel_id=1, source_target_pairs={{16,32},{32,16},{48,64},{64,48},{80,96},{96,80},{112,128},{128,112... | collective-permute-start | bytes 49160 | tf_op jit(solution)/shard_map/ppermute | solution.py:25
  29.8 0.1 pad_maximum_fusion.6.coef
  30.0 0.0 collective-permute-done.1.chip
  30.0 4.0 %collective-permute-done.2.link = f32[64,64]{1,0:T(8,128)S(1)} collective-permute-done((f32[64,64]{1,0:T(8,128)S(1)}, f32[64,64]{1,0:T(8,128)S(1)}, u32[]{:S(2)}, u32[]{:S(2)}) %collective-permute-start.2) | collective-permute-done | bytes 16416 | tf_op jit(solution)/shard_map/ppermute | solution.py:25
  34.0 0.9 shard_map.60
  34.9 5.7 %collective-permute-start.3 = (f32[64,64]{1,0:T(8,128)S(1)}, f32[64,64]{1,0:T(8,128)S(1)}, u32[]{:S(2)}, u32[]{:S(2)}) collective-permute-start(f32[64,64]{1,0:T(8,128)S(1)} %get-tuple-element.50), channel_id=1, source_target_pairs={{0,16},{16,0},{32,48},{48,32},{64,80},{80,64},{96,112},{112,96},{1... | collective-permute-start | bytes 49160 | tf_op jit(solution)/shard_map/ppermute | solution.py:25
  40.6 1.9 %collective-permute-start.4 = (f32[64,64]{1,0:T(8,128)S(1)}, f32[64,64]{1,0:T(8,128)S(1)}, u32[]{:S(2)}, u32[]{:S(2)}) collective-permute-start(f32[64,64]{1,0:T(8,128)S(1)} %get-tuple-element.51), channel_id=1, source_target_pairs={{16,32},{32,16},{48,64},{64,48},{80,96},{96,80},{112,128},{128,112... | collective-permute-start | bytes 49160 | tf_op jit(solution)/shard_map/ppermute | solution.py:25
  42.6 0.1 pad_maximum_fusion.5.coef
  42.7 0.0 collective-permute-done.3.chip
  42.8 4.0 %collective-permute-done.4.link = f32[64,64]{1,0:T(8,128)S(1)} collective-permute-done((f32[64,64]{1,0:T(8,128)S(1)}, f32[64,64]{1,0:T(8,128)S(1)}, u32[]{:S(2)}, u32[]{:S(2)}) %collective-permute-start.4) | collective-permute-done | bytes 16416 | tf_op jit(solution)/shard_map/ppermute | solution.py:25
  46.8 0.9 shard_map.61
  47.7 5.2 %collective-permute-start.5 = (f32[64,64]{1,0:T(8,128)S(1)}, f32[64,64]{1,0:T(8,128)S(1)}, u32[]{:S(2)}, u32[]{:S(2)}) collective-permute-start(f32[64,64]{1,0:T(8,128)S(1)} %get-tuple-element.55), channel_id=1, source_target_pairs={{0,16},{16,0},{32,48},{48,32},{64,80},{80,64},{96,112},{112,96},{1... | collective-permute-start | bytes 49160 | tf_op jit(solution)/shard_map/ppermute | solution.py:25
  52.9 1.9 %collective-permute-start.6 = (f32[64,64]{1,0:T(8,128)S(1)}, f32[64,64]{1,0:T(8,128)S(1)}, u32[]{:S(2)}, u32[]{:S(2)}) collective-permute-start(f32[64,64]{1,0:T(8,128)S(1)} %get-tuple-element.56), channel_id=1, source_target_pairs={{16,32},{32,16},{48,64},{64,48},{80,96},{96,80},{112,128},{128,112... | collective-permute-start | bytes 49160 | tf_op jit(solution)/shard_map/ppermute | solution.py:25
  54.9 0.1 pad_maximum_fusion.4.coef
  55.0 0.0 collective-permute-done.5.chip
  55.1 4.0 %collective-permute-done.6.link = f32[64,64]{1,0:T(8,128)S(1)} collective-permute-done((f32[64,64]{1,0:T(8,128)S(1)}, f32[64,64]{1,0:T(8,128)S(1)}, u32[]{:S(2)}, u32[]{:S(2)}) %collective-permute-start.6) | collective-permute-done | bytes 16416 | tf_op jit(solution)/shard_map/ppermute | solution.py:25
  59.1 0.9 shard_map.62
  60.0 5.2 %collective-permute-start.7 = (f32[64,64]{1,0:T(8,128)S(1)}, f32[64,64]{1,0:T(8,128)S(1)}, u32[]{:S(2)}, u32[]{:S(2)}) collective-permute-start(f32[64,64]{1,0:T(8,128)S(1)} %get-tuple-element.60), channel_id=1, source_target_pairs={{0,16},{16,0},{32,48},{48,32},{64,80},{80,64},{96,112},{112,96},{1... | collective-permute-start | bytes 49160 | tf_op jit(solution)/shard_map/ppermute | solution.py:25
  65.2 1.9 %collective-permute-start.8 = (f32[64,64]{1,0:T(8,128)S(1)}, f32[64,64]{1,0:T(8,128)S(1)}, u32[]{:S(2)}, u32[]{:S(2)}) collective-permute-start(f32[64,64]{1,0:T(8,128)S(1)} %get-tuple-element.61), channel_id=1, source_target_pairs={{16,32},{32,16},{48,64},{64,48},{80,96},{96,80},{112,128},{128,112... | collective-permute-start | bytes 49160 | tf_op jit(solution)/shard_map/ppermute | solution.py:25
  67.2 0.1 pad_maximum_fusion.3.coef
  67.3 0.0 collective-permute-done.7.chip
  67.4 4.0 %collective-permute-done.8.link = f32[64,64]{1,0:T(8,128)S(1)} collective-permute-done((f32[64,64]{1,0:T(8,128)S(1)}, f32[64,64]{1,0:T(8,128)S(1)}, u32[]{:S(2)}, u32[]{:S(2)}) %collective-permute-start.8) | collective-permute-done | bytes 16416 | tf_op jit(solution)/shard_map/ppermute | solution.py:25
  71.4 0.9 shard_map.63
  72.3 5.2 %collective-permute-start.9 = (f32[64,64]{1,0:T(8,128)S(1)}, f32[64,64]{1,0:T(8,128)S(1)}, u32[]{:S(2)}, u32[]{:S(2)}) collective-permute-start(f32[64,64]{1,0:T(8,128)S(1)} %get-tuple-element.65), channel_id=1, source_target_pairs={{0,16},{16,0},{32,48},{48,32},{64,80},{80,64},{96,112},{112,96},{1... | collective-permute-start | bytes 49160 | tf_op jit(solution)/shard_map/ppermute | solution.py:25
  77.5 1.9 %collective-permute-start.10 = (f32[64,64]{1,0:T(8,128)S(1)}, f32[64,64]{1,0:T(8,128)S(1)}, u32[]{:S(2)}, u32[]{:S(2)}) collective-permute-start(f32[64,64]{1,0:T(8,128)S(1)} %get-tuple-element.66), channel_id=1, source_target_pairs={{16,32},{32,16},{48,64},{64,48},{80,96},{96,80},{112,128},{128,112... | collective-permute-start | bytes 49160 | tf_op jit(solution)/shard_map/ppermute | solution.py:25
  79.5 0.1 pad_maximum_fusion.2.coef
  79.6 0.0 collective-permute-done.9.chip
  79.7 4.0 %collective-permute-done.10.link = f32[64,64]{1,0:T(8,128)S(1)} collective-permute-done((f32[64,64]{1,0:T(8,128)S(1)}, f32[64,64]{1,0:T(8,128)S(1)}, u32[]{:S(2)}, u32[]{:S(2)}) %collective-permute-start.10) | collective-permute-done | bytes 16416 | tf_op jit(solution)/shard_map/ppermute | solution.py:25
  83.7 0.9 shard_map.64
  84.6 5.2 %collective-permute-start.11 = (f32[64,64]{1,0:T(8,128)S(1)}, f32[64,64]{1,0:T(8,128)S(1)}, u32[]{:S(2)}, u32[]{:S(2)}) collective-permute-start(f32[64,64]{1,0:T(8,128)S(1)} %get-tuple-element.70), channel_id=1, source_target_pairs={{0,16},{16,0},{32,48},{48,32},{64,80},{80,64},{96,112},{112,96},{1... | collective-permute-start | bytes 49160 | tf_op jit(solution)/shard_map/ppermute | solution.py:25
  89.8 1.9 %collective-permute-start.12 = (f32[64,64]{1,0:T(8,128)S(1)}, f32[64,64]{1,0:T(8,128)S(1)}, u32[]{:S(2)}, u32[]{:S(2)}) collective-permute-start(f32[64,64]{1,0:T(8,128)S(1)} %get-tuple-element.71), channel_id=1, source_target_pairs={{16,32},{32,16},{48,64},{64,48},{80,96},{96,80},{112,128},{128,112... | collective-permute-start | bytes 49160 | tf_op jit(solution)/shard_map/ppermute | solution.py:25
  91.8 0.1 pad_maximum_fusion.1.coef
  91.9 0.0 collective-permute-done.11.chip
  92.0 4.0 %collective-permute-done.12.link = f32[64,64]{1,0:T(8,128)S(1)} collective-permute-done((f32[64,64]{1,0:T(8,128)S(1)}, f32[64,64]{1,0:T(8,128)S(1)}, u32[]{:S(2)}, u32[]{:S(2)}) %collective-permute-start.12) | collective-permute-done | bytes 16416 | tf_op jit(solution)/shard_map/ppermute | solution.py:25
  96.0 0.9 shard_map.65
  96.9 5.2 %collective-permute-start.13 = (f32[64,64]{1,0:T(8,128)S(1)}, f32[64,64]{1,0:T(8,128)S(1)}, u32[]{:S(2)}, u32[]{:S(2)}) collective-permute-start(f32[64,64]{1,0:T(8,128)S(1)} %get-tuple-element.75), channel_id=1, source_target_pairs={{0,16},{16,0},{32,48},{48,32},{64,80},{80,64},{96,112},{112,96},{1... | collective-permute-start | bytes 49160 | tf_op jit(solution)/shard_map/ppermute | solution.py:25
  102.1 1.9 %collective-permute-start.14 = (f32[64,64]{1,0:T(8,128)S(1)}, f32[64,64]{1,0:T(8,128)S(1)}, u32[]{:S(2)}, u32[]{:S(2)}) collective-permute-start(f32[64,64]{1,0:T(8,128)S(1)} %get-tuple-element.76), channel_id=1, source_target_pairs={{16,32},{32,16},{48,64},{64,48},{80,96},{96,80},{112,128},{128,112... | collective-permute-start | bytes 49160 | tf_op jit(solution)/shard_map/ppermute | solution.py:25
  104.1 0.1 pad_maximum_fusion.coef
  104.2 4.1 %collective-permute-done.14.link = f32[64,64]{1,0:T(8,128)S(1)} collective-permute-done((f32[64,64]{1,0:T(8,128)S(1)}, f32[64,64]{1,0:T(8,128)S(1)}, u32[]{:S(2)}, u32[]{:S(2)}) %collective-permute-start.14) | collective-permute-done | bytes 16416 | tf_op jit(solution)/shard_map/ppermute | solution.py:25
  108.3 1.4 shard_map.66
  109.7 5.2 %collective-permute-start.15 = (f32[64,64]{1,0:T(8,128)S(1)}, f32[64,64]{1,0:T(8,128)S(1)}, u32[]{:S(2)}, u32[]{:S(2)}) collective-permute-start(f32[64,64]{1,0:T(8,128)S(1)} %get-tuple-element.80), channel_id=1, source_target_pairs={{0,16},{16,0},{32,48},{48,32},{64,80},{80,64},{96,112},{112,96},{1... | collective-permute-start | bytes 49160 | tf_op jit(solution)/shard_map/ppermute | solution.py:25
  115.0 1.9 %collective-permute-start.16 = (f32[64,64]{1,0:T(8,128)S(1)}, f32[64,64]{1,0:T(8,128)S(1)}, u32[]{:S(2)}, u32[]{:S(2)}) collective-permute-start(f32[64,64]{1,0:T(8,128)S(1)} %get-tuple-element.81), channel_id=1, source_target_pairs={{16,32},{32,16},{48,64},{64,48},{80,96},{96,80},{112,128},{128,112... | collective-permute-start | bytes 49160 | tf_op jit(solution)/shard_map/ppermute | solution.py:25
  116.9 0.0 collective-permute-done.15.chip
  116.9 4.2 %collective-permute-done.16.link = f32[64,64]{1,0:T(8,128)S(1)} collective-permute-done((f32[64,64]{1,0:T(8,128)S(1)}, f32[64,64]{1,0:T(8,128)S(1)}, u32[]{:S(2)}, u32[]{:S(2)}) %collective-permute-start.16) | collective-permute-done | bytes 16416 | tf_op jit(solution)/shard_map/ppermute | solution.py:25
  121.1 1.2 shard_map.67
  122.3 10.6 %all-to-all-start = ((bf16[16,64,512]{2,1,0:T(8,128)(2,1)}), bf16[16,64,512]{2,1,0:T(8,128)(2,1)S(1)}, u32[]{:S(2)}, u32[]{:S(2)}) async-start(bf16[16,64,512]{2,1,0:T(8,128)(2,1)} %get-tuple-element.83), calls=%async_computation | async-start | bytes 2097152 | tf_op jit(solution)/shard_map/all_to_all | solution.py:182
  132.9 2.1 %collective-permute-start.17 = (f32[64,64]{1,0:T(8,128)S(1)}, f32[64,64]{1,0:T(8,128)S(1)}, u32[]{:S(2)}, u32[]{:S(2)}) collective-permute-start(f32[64,64]{1,0:T(8,128)S(1)} %get-tuple-element.85), channel_id=1, source_target_pairs={{0,16},{16,32},{32,48},{48,64},{64,80},{80,96},{96,112},{112,128},... | collective-permute-start | bytes 49160 | tf_op jit(solution)/shard_map/ppermute | solution.py:16
  135.0 7.3 %collective-permute-done.17.incoming = f32[64,64]{1,0:T(8,128)S(1)} collective-permute-done((f32[64,64]{1,0:T(8,128)S(1)}, f32[64,64]{1,0:T(8,128)S(1)}, u32[]{:S(2)}, u32[]{:S(2)}) %collective-permute-start.17) | collective-permute-done | bytes 16416 | tf_op jit(solution)/shard_map/ppermute | solution.py:16
  142.3 16.0 %all-to-all-done = bf16[16,64,512]{2,1,0:T(8,128)(2,1)S(1)} async-done(((bf16[16,64,512]{2,1,0:T(8,128)(2,1)}), bf16[16,64,512]{2,1,0:T(8,128)(2,1)S(1)}, u32[]{:S(2)}, u32[]{:S(2)}) %all-to-all-start) | async-done | bytes 1048608 | tf_op jit(solution)/shard_map/all_to_all | solution.py:182
  158.3 0.5 shard_map.68
  158.8 23.8 %all_to_all.10 = f32[64,8,128]{2,1,0:T(8,128)S(1)} all-to-all(f32[64,8,128]{2,1,0:T(8,128)S(1)} %shard_map.68), channel_id=1, replica_groups=mesh['cell'=64,'state'=16] {'cell'}, dimensions={0} | all-to-all | bytes 524288 | tf_op jit(solution)/shard_map/all_to_all | solution.py:189
  182.6 0.1 reduce_sum.11
  182.7 0.1 reduce_sum.12
  182.8 0.6 copy.12
  (3 shorter events, 0.0 us)
Async XLA Ops:
  0.6 21.5 %copy-start = (bf16[2,343,343]{2,0,1:T(2,128)(2,1)S(1)}, bf16[2,343,343]{2,0,1:T(2,128)(2,1)}, u32[]{:S(2)}) copy-start(bf16[2,343,343]{2,0,1:T(2,128)(2,1)} %param.6) | copy-start | bytes 1411792
  1.5 23.5 %collective-permute-start = (bf16[64,64]{1,0:T(8,128)(2,1)S(1)}, bf16[64,64]{1,0:T(8,128)(2,1)S(1)}, u32[]{:S(2)}, u32[]{:S(2)}) collective-permute-start(bf16[64,64]{1,0:T(8,128)(2,1)S(1)} %slice.19), channel_id=1, source_target_pairs={{0,1008},{16,0},{32,16},{48,32},{64,48},{80,64},{96,80},{112,96},{... | collective-permute-start | bytes 24584 | tf_op jit(solution)/shard_map/ppermute | solution.py:16
  22.1 2.9 %copy-start.1 = (f32[64,512]{1,0:T(8,128)S(1)}, f32[64,512]{1,0:T(8,128)}, u32[]{:S(2)}) copy-start(f32[64,512]{1,0:T(8,128)} %previous.1) | copy-start | bytes 393220
  25.9 4.0 %collective-permute-start.1 = (f32[64,64]{1,0:T(8,128)S(1)}, f32[64,64]{1,0:T(8,128)S(1)}, u32[]{:S(2)}, u32[]{:S(2)}) collective-permute-start(f32[64,64]{1,0:T(8,128)S(1)} %get-tuple-element.46), channel_id=1, source_target_pairs={{0,16},{16,0},{32,48},{48,32},{64,80},{80,64},{96,112},{112,96},{1... | collective-permute-start | bytes 49160 | tf_op jit(solution)/shard_map/ppermute | solution.py:25
  27.9 6.1 %collective-permute-start.2 = (f32[64,64]{1,0:T(8,128)S(1)}, f32[64,64]{1,0:T(8,128)S(1)}, u32[]{:S(2)}, u32[]{:S(2)}) collective-permute-start(f32[64,64]{1,0:T(8,128)S(1)} %get-tuple-element.47), channel_id=1, source_target_pairs={{16,32},{32,16},{48,64},{64,48},{80,96},{96,80},{112,128},{128,112... | collective-permute-start | bytes 49160 | tf_op jit(solution)/shard_map/ppermute | solution.py:25
  34.9 7.8 %collective-permute-start.3 = (f32[64,64]{1,0:T(8,128)S(1)}, f32[64,64]{1,0:T(8,128)S(1)}, u32[]{:S(2)}, u32[]{:S(2)}) collective-permute-start(f32[64,64]{1,0:T(8,128)S(1)} %get-tuple-element.50), channel_id=1, source_target_pairs={{0,16},{16,0},{32,48},{48,32},{64,80},{80,64},{96,112},{112,96},{1... | collective-permute-start | bytes 49160 | tf_op jit(solution)/shard_map/ppermute | solution.py:25
  40.6 6.1 %collective-permute-start.4 = (f32[64,64]{1,0:T(8,128)S(1)}, f32[64,64]{1,0:T(8,128)S(1)}, u32[]{:S(2)}, u32[]{:S(2)}) collective-permute-start(f32[64,64]{1,0:T(8,128)S(1)} %get-tuple-element.51), channel_id=1, source_target_pairs={{16,32},{32,16},{48,64},{64,48},{80,96},{96,80},{112,128},{128,112... | collective-permute-start | bytes 49160 | tf_op jit(solution)/shard_map/ppermute | solution.py:25
  47.7 7.4 %collective-permute-start.5 = (f32[64,64]{1,0:T(8,128)S(1)}, f32[64,64]{1,0:T(8,128)S(1)}, u32[]{:S(2)}, u32[]{:S(2)}) collective-permute-start(f32[64,64]{1,0:T(8,128)S(1)} %get-tuple-element.55), channel_id=1, source_target_pairs={{0,16},{16,0},{32,48},{48,32},{64,80},{80,64},{96,112},{112,96},{1... | collective-permute-start | bytes 49160 | tf_op jit(solution)/shard_map/ppermute | solution.py:25
  52.9 6.1 %collective-permute-start.6 = (f32[64,64]{1,0:T(8,128)S(1)}, f32[64,64]{1,0:T(8,128)S(1)}, u32[]{:S(2)}, u32[]{:S(2)}) collective-permute-start(f32[64,64]{1,0:T(8,128)S(1)} %get-tuple-element.56), channel_id=1, source_target_pairs={{16,32},{32,16},{48,64},{64,48},{80,96},{96,80},{112,128},{128,112... | collective-permute-start | bytes 49160 | tf_op jit(solution)/shard_map/ppermute | solution.py:25
  60.0 7.4 %collective-permute-start.7 = (f32[64,64]{1,0:T(8,128)S(1)}, f32[64,64]{1,0:T(8,128)S(1)}, u32[]{:S(2)}, u32[]{:S(2)}) collective-permute-start(f32[64,64]{1,0:T(8,128)S(1)} %get-tuple-element.60), channel_id=1, source_target_pairs={{0,16},{16,0},{32,48},{48,32},{64,80},{80,64},{96,112},{112,96},{1... | collective-permute-start | bytes 49160 | tf_op jit(solution)/shard_map/ppermute | solution.py:25
  65.2 6.1 %collective-permute-start.8 = (f32[64,64]{1,0:T(8,128)S(1)}, f32[64,64]{1,0:T(8,128)S(1)}, u32[]{:S(2)}, u32[]{:S(2)}) collective-permute-start(f32[64,64]{1,0:T(8,128)S(1)} %get-tuple-element.61), channel_id=1, source_target_pairs={{16,32},{32,16},{48,64},{64,48},{80,96},{96,80},{112,128},{128,112... | collective-permute-start | bytes 49160 | tf_op jit(solution)/shard_map/ppermute | solution.py:25
  72.3 7.4 %collective-permute-start.9 = (f32[64,64]{1,0:T(8,128)S(1)}, f32[64,64]{1,0:T(8,128)S(1)}, u32[]{:S(2)}, u32[]{:S(2)}) collective-permute-start(f32[64,64]{1,0:T(8,128)S(1)} %get-tuple-element.65), channel_id=1, source_target_pairs={{0,16},{16,0},{32,48},{48,32},{64,80},{80,64},{96,112},{112,96},{1... | collective-permute-start | bytes 49160 | tf_op jit(solution)/shard_map/ppermute | solution.py:25
  77.5 6.1 %collective-permute-start.10 = (f32[64,64]{1,0:T(8,128)S(1)}, f32[64,64]{1,0:T(8,128)S(1)}, u32[]{:S(2)}, u32[]{:S(2)}) collective-permute-start(f32[64,64]{1,0:T(8,128)S(1)} %get-tuple-element.66), channel_id=1, source_target_pairs={{16,32},{32,16},{48,64},{64,48},{80,96},{96,80},{112,128},{128,112... | collective-permute-start | bytes 49160 | tf_op jit(solution)/shard_map/ppermute | solution.py:25
  84.6 7.4 %collective-permute-start.11 = (f32[64,64]{1,0:T(8,128)S(1)}, f32[64,64]{1,0:T(8,128)S(1)}, u32[]{:S(2)}, u32[]{:S(2)}) collective-permute-start(f32[64,64]{1,0:T(8,128)S(1)} %get-tuple-element.70), channel_id=1, source_target_pairs={{0,16},{16,0},{32,48},{48,32},{64,80},{80,64},{96,112},{112,96},{1... | collective-permute-start | bytes 49160 | tf_op jit(solution)/shard_map/ppermute | solution.py:25
  89.8 6.1 %collective-permute-start.12 = (f32[64,64]{1,0:T(8,128)S(1)}, f32[64,64]{1,0:T(8,128)S(1)}, u32[]{:S(2)}, u32[]{:S(2)}) collective-permute-start(f32[64,64]{1,0:T(8,128)S(1)} %get-tuple-element.71), channel_id=1, source_target_pairs={{16,32},{32,16},{48,64},{64,48},{80,96},{96,80},{112,128},{128,112... | collective-permute-start | bytes 49160 | tf_op jit(solution)/shard_map/ppermute | solution.py:25
  96.9 7.3 %collective-permute-start.13 = (f32[64,64]{1,0:T(8,128)S(1)}, f32[64,64]{1,0:T(8,128)S(1)}, u32[]{:S(2)}, u32[]{:S(2)}) collective-permute-start(f32[64,64]{1,0:T(8,128)S(1)} %get-tuple-element.75), channel_id=1, source_target_pairs={{0,16},{16,0},{32,48},{48,32},{64,80},{80,64},{96,112},{112,96},{1... | collective-permute-start | bytes 49160 | tf_op jit(solution)/shard_map/ppermute | solution.py:25
  102.1 6.1 %collective-permute-start.14 = (f32[64,64]{1,0:T(8,128)S(1)}, f32[64,64]{1,0:T(8,128)S(1)}, u32[]{:S(2)}, u32[]{:S(2)}) collective-permute-start(f32[64,64]{1,0:T(8,128)S(1)} %get-tuple-element.76), channel_id=1, source_target_pairs={{16,32},{32,16},{48,64},{64,48},{80,96},{96,80},{112,128},{128,112... | collective-permute-start | bytes 49160 | tf_op jit(solution)/shard_map/ppermute | solution.py:25
  109.7 7.2 %collective-permute-start.15 = (f32[64,64]{1,0:T(8,128)S(1)}, f32[64,64]{1,0:T(8,128)S(1)}, u32[]{:S(2)}, u32[]{:S(2)}) collective-permute-start(f32[64,64]{1,0:T(8,128)S(1)} %get-tuple-element.80), channel_id=1, source_target_pairs={{0,16},{16,0},{32,48},{48,32},{64,80},{80,64},{96,112},{112,96},{1... | collective-permute-start | bytes 49160 | tf_op jit(solution)/shard_map/ppermute | solution.py:25
  115.0 6.1 %collective-permute-start.16 = (f32[64,64]{1,0:T(8,128)S(1)}, f32[64,64]{1,0:T(8,128)S(1)}, u32[]{:S(2)}, u32[]{:S(2)}) collective-permute-start(f32[64,64]{1,0:T(8,128)S(1)} %get-tuple-element.81), channel_id=1, source_target_pairs={{16,32},{32,16},{48,64},{64,48},{80,96},{96,80},{112,128},{128,112... | collective-permute-start | bytes 49160 | tf_op jit(solution)/shard_map/ppermute | solution.py:25
  122.3 36.0 %all-to-all-start = ((bf16[16,64,512]{2,1,0:T(8,128)(2,1)}), bf16[16,64,512]{2,1,0:T(8,128)(2,1)S(1)}, u32[]{:S(2)}, u32[]{:S(2)}) async-start(bf16[16,64,512]{2,1,0:T(8,128)(2,1)} %get-tuple-element.83), calls=%async_computation | async-start | bytes 2097152 | tf_op jit(solution)/shard_map/all_to_all | solution.py:182
  132.9 9.4 %collective-permute-start.17 = (f32[64,64]{1,0:T(8,128)S(1)}, f32[64,64]{1,0:T(8,128)S(1)}, u32[]{:S(2)}, u32[]{:S(2)}) collective-permute-start(f32[64,64]{1,0:T(8,128)S(1)} %get-tuple-element.85), channel_id=1, source_target_pairs={{0,16},{16,32},{32,48},{48,64},{64,80},{80,96},{96,112},{112,128},... | collective-permute-start | bytes 49160 | tf_op jit(solution)/shard_map/ppermute | solution.py:16

commit v2 on v1

--- a/solution.py
+++ b/solution.py
@@ -98,16 +98,39 @@
     spill[...] = product[:, owned:]
 
 
-def project_body(lows, product, incoming, out):
-    states, shared = incoming.shape
-    value = product[...]
-    first = value[:, :shared] + incoming[...]
-    image = jnp.concatenate([first, value[:, shared:]], axis=1).astype(jnp.bfloat16)
+def finish_body(product, incoming, image):
+    shared = incoming.shape[1]
+    image[...] = product[...].astype(jnp.bfloat16)
+    image[:, :shared] = (product[:, :shared] + incoming[...]).astype(jnp.bfloat16)
+
+
+def project_body(flag, lows, image, neighbour, keep, handed):
+    states = image.shape[0]
+    images = jnp.concatenate([image[...], neighbour[...]], axis=0)
     partial = lax.dot_general(
-        lows[...], image, (((1,), (1,)), ((), ())), preferred_element_type=jnp.float32
-    )
-    pieces = partial.reshape(partial.shape[0] // 16, 2, 8, states)
-    out[...] = jnp.concatenate([pieces[:, 0], pieces[:, 1]], axis=2)
+        lows[...], images, (((1,), (1,)), ((), ())), preferred_element_type=jnp.float32
+    )
+    rows = partial.reshape(partial.shape[0] // 32, 2, 2, 8, 2 * states)
+    even = flag[0] == 0
+    mine = jnp.where(even, rows[:, 0], rows[:, 1])
+    other = jnp.where(even, rows[:, 1], rows[:, 0])
+    for place, value in ((keep, mine), (handed, other)):
+        place[0] = jnp.concatenate([value[:, 0, :, :states], value[:, 1, :, :states]], axis=2)
+        place[1] = jnp.concatenate([value[:, 0, :, states:], value[:, 1, :, states:]], axis=2)
+
+
+def add_body(keep, received, own, other):
+    own[...] = keep[0] + received[0]
+    other[...] = keep[1] + received[1]
+
+
+def place_body(half, own, received, out):
+    low = half[0] == 0
+    groups = out.shape[0]
+    mine = own[...].reshape(groups, 2, *own.shape[1:])
+    theirs = received[...].reshape(groups, 2, *own.shape[1:])
+    out[:, 0] = jnp.where(low, mine, theirs)
+    out[:, 1] = jnp.where(low, theirs, mine)
 
 
 def kernel(body, cells, scalars, out_shape, scratch):
@@ -130,6 +153,10 @@
     return run
 
 
+def alternate(count):
+    return [list(range(first, count, 2)) for first in range(2)]
+
+
 def exchanged(to_link, to_chip):
     link = swapped(to_link, "cell", 1)
     chip = swapped(to_chip, "cell", 0)
@@ -153,7 +180,8 @@
     first = kernel(first_body, cells, 2, (whole, group, group, group), scratch)
     step = kernel(degree_body, cells, 2, (whole, whole, group, group, group), scratch)
     out = jax.ShapeDtypeStruct((states, owned), f32)
-    lows = pltpu.VMEM((peers, states, owned), bf16)
+    line = peers // 2
+    lows = pltpu.VMEM((line, states, owned), bf16)
     last = kernel(image_body, cells, 1, (out, lows, whole, group), scratch)
 
     lowest, cut, upper = (bounds[0], bounds[1], bounds[2])
@@ -171,7 +199,7 @@
     ghost = passed_along(start_block[:, :shared].astype(bf16), "cell", -1)
     own, ghost, to_chip, to_link = first(flag, coefs[0], start_block, ghost, weights)
     previous = start_block
-    for coef in coefs[1:]:
+    for number, coef in enumerate(coefs[1:]):
         link, chip = exchanged(to_link, to_chip)
         previous, own, ghost, to_chip, to_link = step(
             flag, coef, own, ghost, chip, link, previous, weights
@@ -179,15 +207,32 @@
     link, chip = exchanged(to_link, to_chip)
     filtered, low, product, spill = last(flag, own, ghost, chip, link, weights)
     incoming = passed_along(spill, "cell", 1)
-    lows = lax.all_to_all(low, "state", 0, 0, tiled=True)
-    lows = lows.reshape(peers * states, owned)
+    lows = lax.all_to_all(
+        low, "state", 0, 0, axis_index_groups=alternate(peers), tiled=True
+    )
+    lows = lows.reshape(line * states, owned)
+    shape = pltpu.VMEM((states, owned), bf16)
+    image = kernel(finish_body, 0, 0, shape, [])(product, incoming)
+    neighbour = swapped(image, "state", 0)
 
     count = lax.axis_size("cell")
+    half = (lax.axis_index("state") % 2).astype(jnp.int32).reshape(1)
+    number = line * states // 32
+    both = pltpu.VMEM((2, number, 8, 2 * states), f32)
+    keep, handed = kernel(project_body, 0, 1, (both, both), [])(
+        flag, lows, image, neighbour
+    )
+    part = pltpu.VMEM((number, 8, 2 * states), f32)
+    own, other = kernel(add_body, 0, 0, (part, part), [])(keep, swapped(handed, "cell", 0))
+    received = swapped(other, "state", 0)
+    shape = pltpu.VMEM((number // 2, 2, 2, 8, 2 * states), f32)
+    pieces = kernel(place_body, 0, 1, shape, [])(half, own, received)
+    pieces = pieces.reshape(2 * number, 8, 2 * states)
+    arrived = lax.all_to_all(
+        pieces, "cell", 0, 0, axis_index_groups=alternate(count), tiled=True
+    )
     rows = peers * states // count
-    shape = pltpu.VMEM((peers * states // 16, 8, 2 * states), f32)
-    pieces = kernel(project_body, 0, 0, shape, [])(lows, product, incoming)
-    arrived = lax.all_to_all(pieces, "cell", 0, 0, tiled=True)
-    total = jnp.sum(arrived.reshape(count, rows // 16, 8, 2, states), axis=0)
+    total = jnp.sum(arrived.reshape(count // 2, rows // 16, 8, 2, states), axis=0)
     projected = jnp.swapaxes(total, 1, 2).reshape(rows, states)
     return (filtered, projected)
 

time: 184 us -> 178 us (0.967)
  starting transfers between devices: 83.1 us -> 94 us
  waiting for transfers between devices: 55.8 us -> 46.2 us
  blocking collectives: 23.8 us -> 16.5 us
    all_to_all x1, waiting for transfers between devices: 16 us -> 3.1 us  [per_device(): lax.all_to_all(low, 'state', 0, 0, axis_index_groups=alternate(peers), ti...]
    ppermute x16 -> x19, starting transfers between devices: 54.4 us -> 65.4 us  [swapped(): return lax.ppermute(value, axis, pairs)]
    all_to_all x1, blocking collectives: 23.8 us -> 16.5 us  [per_device(): lax.all_to_all(pieces, 'cell', 0, 0, axis_index_groups=alternate(count),...]
    ppermute x16 -> x19, waiting for transfers between devices: 32.5 us -> 39.3 us  [swapped(): return lax.ppermute(value, axis, pairs)]
    ppermute x2, waiting for transfers between devices: 7.33 us -> 3.8 us  [passed_along(): return lax.ppermute(value, axis, pairs)]
    pallas_call x10 -> x13, Pallas kernels: 9.54 us -> 9.26 us  [run(): pl.pallas_call(functools.partial(body, cells) if cells else body, in_spec...]
  transfers between devices with their start and end apart: 19 -> 22, of which waited for: 10 -> 13; matrix products, arithmetic and copies ran while one was open for 2% -> 3% of each run, Pallas kernels for 0% -> 0%
where the time goes in v2:
time: 178 us; the launch traced here: 177 us
  starting transfers between devices  94 us (53%)
  waiting for transfers between devices  46.2 us (26%)
  blocking collectives  16.5 us (9%)
  Pallas kernels  9.26 us (5%)
  between operations  4.93 us (3%)
  local copies, waits for them, and re-layouts  2.9 us (2%)
  matrix products  2.56 us (1%)
    ppermute x19, starting transfers between devices, swapped(): return lax.ppermute(value, axis, pairs)  65.4 us
    ppermute x19, waiting for transfers between devices, swapped(): return lax.ppermute(value, axis, pairs)  39.3 us
    ppermute x2, starting transfers between devices, passed_along(): return lax.ppermute(value, axis, pairs)  18.1 us
    all_to_all x1, blocking collectives, per_device(): lax.all_to_all(pieces, 'cell', 0, 0, axis_index_groups=alternate(count),...  16.5 us
    all_to_all x1, starting transfers between devices, per_device(): lax.all_to_all(low, 'state', 0, 0, axis_index_groups=alternate(peers), ti...  10.5 us
    pallas_call x13, Pallas kernels, run(): pl.pallas_call(functools.partial(body, cells) if cells else body, in_spec...  9.26 us
    ppermute x2, waiting for transfers between devices, passed_along(): return lax.ppermute(value, axis, pairs)  3.8 us
  transfers between devices with their start and end apart: 22, of which 13 were waited for; matrix products, arithmetic and copies ran while one was open for 3% of the time, Pallas kernels for 0%

profile of v2, /device:TPU:1, one launch (start us, length us, event | category | flops | bytes accessed | tf_op | source)
XLA Modules:
  0.0 177.0 jit_solution(570961631890951146)
XLA Ops:
  0.6 0.0 copy-start
  0.6 0.8 slice.19
  1.5 16.0 %collective-permute-start = (bf16[64,64]{1,0:T(8,128)(2,1)S(1)}, bf16[64,64]{1,0:T(8,128)(2,1)S(1)}, u32[]{:S(2)}, u32[]{:S(2)}) collective-permute-start(bf16[64,64]{1,0:T(8,128)(2,1)S(1)} %slice.19), channel_id=1, source_target_pairs={{0,1008},{16,0},{32,16},{48,32},{64,48},{80,64},{96,80},{112,96},{... | collective-permute-start | bytes 24584 | tf_op jit(solution)/shard_map/ppermute | solution.py:16
  17.5 1.4 fusion.8
  22.1 0.0 copy-start.1
  22.1 2.6 %fusion.2.weights = bf16[2,576,576]{2,1,0:T(8,128)(2,1)S(1)} fusion(s32[2,343]{1,0:T(2,128)} %param.5, bf16[2,343,343]{2,0,1:T(2,128)(2,1)S(1)} %copy-done), kind=kOutput, calls=%fused_computation.3 | convolution fusion | flops 728108928 | bytes 1800444 | tf_op jit(solution)/shard_map/cai,cak->cik/dot_general | solution.py:34
  24.7 0.1 pad_maximum_fusion.7.coef
  24.9 0.9 shard_map.59
  25.9 1.9 %collective-permute-start.1 = (f32[64,64]{1,0:T(8,128)S(1)}, f32[64,64]{1,0:T(8,128)S(1)}, u32[]{:S(2)}, u32[]{:S(2)}) collective-permute-start(f32[64,64]{1,0:T(8,128)S(1)} %get-tuple-element.50), channel_id=1, source_target_pairs={{0,16},{16,0},{32,48},{48,32},{64,80},{80,64},{96,112},{112,96},{1... | collective-permute-start | bytes 49160 | tf_op jit(solution)/shard_map/ppermute | solution.py:25
  27.8 1.9 %collective-permute-start.2 = (f32[64,64]{1,0:T(8,128)S(1)}, f32[64,64]{1,0:T(8,128)S(1)}, u32[]{:S(2)}, u32[]{:S(2)}) collective-permute-start(f32[64,64]{1,0:T(8,128)S(1)} %get-tuple-element.51), channel_id=1, source_target_pairs={{16,32},{32,16},{48,64},{64,48},{80,96},{96,80},{112,128},{128,112... | collective-permute-start | bytes 49160 | tf_op jit(solution)/shard_map/ppermute | solution.py:25
  29.7 0.1 pad_maximum_fusion.6.coef
  29.9 0.0 collective-permute-done.1.chip
  29.9 4.0 %collective-permute-done.2.link = f32[64,64]{1,0:T(8,128)S(1)} collective-permute-done((f32[64,64]{1,0:T(8,128)S(1)}, f32[64,64]{1,0:T(8,128)S(1)}, u32[]{:S(2)}, u32[]{:S(2)}) %collective-permute-start.2) | collective-permute-done | bytes 16416 | tf_op jit(solution)/shard_map/ppermute | solution.py:25
  34.0 0.9 shard_map.60
  34.9 5.7 %collective-permute-start.3 = (f32[64,64]{1,0:T(8,128)S(1)}, f32[64,64]{1,0:T(8,128)S(1)}, u32[]{:S(2)}, u32[]{:S(2)}) collective-permute-start(f32[64,64]{1,0:T(8,128)S(1)} %get-tuple-element.54), channel_id=1, source_target_pairs={{0,16},{16,0},{32,48},{48,32},{64,80},{80,64},{96,112},{112,96},{1... | collective-permute-start | bytes 49160 | tf_op jit(solution)/shard_map/ppermute | solution.py:25
  40.6 1.9 %collective-permute-start.4 = (f32[64,64]{1,0:T(8,128)S(1)}, f32[64,64]{1,0:T(8,128)S(1)}, u32[]{:S(2)}, u32[]{:S(2)}) collective-permute-start(f32[64,64]{1,0:T(8,128)S(1)} %get-tuple-element.55), channel_id=1, source_target_pairs={{16,32},{32,16},{48,64},{64,48},{80,96},{96,80},{112,128},{128,112... | collective-permute-start | bytes 49160 | tf_op jit(solution)/shard_map/ppermute | solution.py:25
  42.5 0.1 pad_maximum_fusion.5.coef
  42.7 0.0 collective-permute-done.3.chip
  42.7 4.0 %collective-permute-done.4.link = f32[64,64]{1,0:T(8,128)S(1)} collective-permute-done((f32[64,64]{1,0:T(8,128)S(1)}, f32[64,64]{1,0:T(8,128)S(1)}, u32[]{:S(2)}, u32[]{:S(2)}) %collective-permute-start.4) | collective-permute-done | bytes 16416 | tf_op jit(solution)/shard_map/ppermute | solution.py:25
  46.7 0.9 shard_map.61
  47.7 5.2 %collective-permute-start.5 = (f32[64,64]{1,0:T(8,128)S(1)}, f32[64,64]{1,0:T(8,128)S(1)}, u32[]{:S(2)}, u32[]{:S(2)}) collective-permute-start(f32[64,64]{1,0:T(8,128)S(1)} %get-tuple-element.59), channel_id=1, source_target_pairs={{0,16},{16,0},{32,48},{48,32},{64,80},{80,64},{96,112},{112,96},{1... | collective-permute-start | bytes 49160 | tf_op jit(solution)/shard_map/ppermute | solution.py:25
  52.9 1.9 %collective-permute-start.6 = (f32[64,64]{1,0:T(8,128)S(1)}, f32[64,64]{1,0:T(8,128)S(1)}, u32[]{:S(2)}, u32[]{:S(2)}) collective-permute-start(f32[64,64]{1,0:T(8,128)S(1)} %get-tuple-element.60), channel_id=1, source_target_pairs={{16,32},{32,16},{48,64},{64,48},{80,96},{96,80},{112,128},{128,112... | collective-permute-start | bytes 49160 | tf_op jit(solution)/shard_map/ppermute | solution.py:25
  54.8 0.1 pad_maximum_fusion.4.coef
  55.0 4.0 %collective-permute-done.6.link = f32[64,64]{1,0:T(8,128)S(1)} collective-permute-done((f32[64,64]{1,0:T(8,128)S(1)}, f32[64,64]{1,0:T(8,128)S(1)}, u32[]{:S(2)}, u32[]{:S(2)}) %collective-permute-start.6) | collective-permute-done | bytes 16416 | tf_op jit(solution)/shard_map/ppermute | solution.py:25
  59.0 0.9 shard_map.62
  60.0 5.2 %collective-permute-start.7 = (f32[64,64]{1,0:T(8,128)S(1)}, f32[64,64]{1,0:T(8,128)S(1)}, u32[]{:S(2)}, u32[]{:S(2)}) collective-permute-start(f32[64,64]{1,0:T(8,128)S(1)} %get-tuple-element.64), channel_id=1, source_target_pairs={{0,16},{16,0},{32,48},{48,32},{64,80},{80,64},{96,112},{112,96},{1... | collective-permute-start | bytes 49160 | tf_op jit(solution)/shard_map/ppermute | solution.py:25
  65.2 1.9 %collective-permute-start.8 = (f32[64,64]{1,0:T(8,128)S(1)}, f32[64,64]{1,0:T(8,128)S(1)}, u32[]{:S(2)}, u32[]{:S(2)}) collective-permute-start(f32[64,64]{1,0:T(8,128)S(1)} %get-tuple-element.65), channel_id=1, source_target_pairs={{16,32},{32,16},{48,64},{64,48},{80,96},{96,80},{112,128},{128,112... | collective-permute-start | bytes 49160 | tf_op jit(solution)/shard_map/ppermute | solution.py:25
  67.1 0.1 pad_maximum_fusion.3.coef
  67.3 4.0 %collective-permute-done.8.link = f32[64,64]{1,0:T(8,128)S(1)} collective-permute-done((f32[64,64]{1,0:T(8,128)S(1)}, f32[64,64]{1,0:T(8,128)S(1)}, u32[]{:S(2)}, u32[]{:S(2)}) %collective-permute-start.8) | collective-permute-done | bytes 16416 | tf_op jit(solution)/shard_map/ppermute | solution.py:25
  71.3 0.9 shard_map.63
  72.3 5.2 %collective-permute-start.9 = (f32[64,64]{1,0:T(8,128)S(1)}, f32[64,64]{1,0:T(8,128)S(1)}, u32[]{:S(2)}, u32[]{:S(2)}) collective-permute-start(f32[64,64]{1,0:T(8,128)S(1)} %get-tuple-element.69), channel_id=1, source_target_pairs={{0,16},{16,0},{32,48},{48,32},{64,80},{80,64},{96,112},{112,96},{1... | collective-permute-start | bytes 49160 | tf_op jit(solution)/shard_map/ppermute | solution.py:25
  77.5 1.9 %collective-permute-start.10 = (f32[64,64]{1,0:T(8,128)S(1)}, f32[64,64]{1,0:T(8,128)S(1)}, u32[]{:S(2)}, u32[]{:S(2)}) collective-permute-start(f32[64,64]{1,0:T(8,128)S(1)} %get-tuple-element.70), channel_id=1, source_target_pairs={{16,32},{32,16},{48,64},{64,48},{80,96},{96,80},{112,128},{128,112... | collective-permute-start | bytes 49160 | tf_op jit(solution)/shard_map/ppermute | solution.py:25
  79.4 0.1 pad_maximum_fusion.2.coef
  79.6 0.0 collective-permute-done.9.chip
  79.6 4.0 %collective-permute-done.10.link = f32[64,64]{1,0:T(8,128)S(1)} collective-permute-done((f32[64,64]{1,0:T(8,128)S(1)}, f32[64,64]{1,0:T(8,128)S(1)}, u32[]{:S(2)}, u32[]{:S(2)}) %collective-permute-start.10) | collective-permute-done | bytes 16416 | tf_op jit(solution)/shard_map/ppermute | solution.py:25
  83.6 0.9 shard_map.64
  84.5 5.2 %collective-permute-start.11 = (f32[64,64]{1,0:T(8,128)S(1)}, f32[64,64]{1,0:T(8,128)S(1)}, u32[]{:S(2)}, u32[]{:S(2)}) collective-permute-start(f32[64,64]{1,0:T(8,128)S(1)} %get-tuple-element.74), channel_id=1, source_target_pairs={{0,16},{16,0},{32,48},{48,32},{64,80},{80,64},{96,112},{112,96},{1... | collective-permute-start | bytes 49160 | tf_op jit(solution)/shard_map/ppermute | solution.py:25
  89.8 1.9 %collective-permute-start.12 = (f32[64,64]{1,0:T(8,128)S(1)}, f32[64,64]{1,0:T(8,128)S(1)}, u32[]{:S(2)}, u32[]{:S(2)}) collective-permute-start(f32[64,64]{1,0:T(8,128)S(1)} %get-tuple-element.75), channel_id=1, source_target_pairs={{16,32},{32,16},{48,64},{64,48},{80,96},{96,80},{112,128},{128,112... | collective-permute-start | bytes 49160 | tf_op jit(solution)/shard_map/ppermute | solution.py:25
  91.7 0.1 pad_maximum_fusion.1.coef
  91.9 4.0 %collective-permute-done.12.link = f32[64,64]{1,0:T(8,128)S(1)} collective-permute-done((f32[64,64]{1,0:T(8,128)S(1)}, f32[64,64]{1,0:T(8,128)S(1)}, u32[]{:S(2)}, u32[]{:S(2)}) %collective-permute-start.12) | collective-permute-done | bytes 16416 | tf_op jit(solution)/shard_map/ppermute | solution.py:25
  95.9 0.9 shard_map.65
  96.8 5.2 %collective-permute-start.13 = (f32[64,64]{1,0:T(8,128)S(1)}, f32[64,64]{1,0:T(8,128)S(1)}, u32[]{:S(2)}, u32[]{:S(2)}) collective-permute-start(f32[64,64]{1,0:T(8,128)S(1)} %get-tuple-element.79), channel_id=1, source_target_pairs={{0,16},{16,0},{32,48},{48,32},{64,80},{80,64},{96,112},{112,96},{1... | collective-permute-start | bytes 49160 | tf_op jit(solution)/shard_map/ppermute | solution.py:25
  102.1 1.9 %collective-permute-start.14 = (f32[64,64]{1,0:T(8,128)S(1)}, f32[64,64]{1,0:T(8,128)S(1)}, u32[]{:S(2)}, u32[]{:S(2)}) collective-permute-start(f32[64,64]{1,0:T(8,128)S(1)} %get-tuple-element.80), channel_id=1, source_target_pairs={{16,32},{32,16},{48,64},{64,48},{80,96},{96,80},{112,128},{128,112... | collective-permute-start | bytes 49160 | tf_op jit(solution)/shard_map/ppermute | solution.py:25
  104.0 0.1 pad_maximum_fusion.coef
  104.1 4.1 %collective-permute-done.14.link = f32[64,64]{1,0:T(8,128)S(1)} collective-permute-done((f32[64,64]{1,0:T(8,128)S(1)}, f32[64,64]{1,0:T(8,128)S(1)}, u32[]{:S(2)}, u32[]{:S(2)}) %collective-permute-start.14) | collective-permute-done | bytes 16416 | tf_op jit(solution)/shard_map/ppermute | solution.py:25
  108.2 1.4 shard_map.66
  109.7 5.2 %collective-permute-start.15 = (f32[64,64]{1,0:T(8,128)S(1)}, f32[64,64]{1,0:T(8,128)S(1)}, u32[]{:S(2)}, u32[]{:S(2)}) collective-permute-start(f32[64,64]{1,0:T(8,128)S(1)} %get-tuple-element.84), channel_id=1, source_target_pairs={{0,16},{16,0},{32,48},{48,32},{64,80},{80,64},{96,112},{112,96},{1... | collective-permute-start | bytes 49160 | tf_op jit(solution)/shard_map/ppermute | solution.py:25
  114.9 1.9 %collective-permute-start.16 = (f32[64,64]{1,0:T(8,128)S(1)}, f32[64,64]{1,0:T(8,128)S(1)}, u32[]{:S(2)}, u32[]{:S(2)}) collective-permute-start(f32[64,64]{1,0:T(8,128)S(1)} %get-tuple-element.85), channel_id=1, source_target_pairs={{16,32},{32,16},{48,64},{64,48},{80,96},{96,80},{112,128},{128,112... | collective-permute-start | bytes 49160 | tf_op jit(solution)/shard_map/ppermute | solution.py:25
  116.8 4.2 %collective-permute-done.16.link = f32[64,64]{1,0:T(8,128)S(1)} collective-permute-done((f32[64,64]{1,0:T(8,128)S(1)}, f32[64,64]{1,0:T(8,128)S(1)}, u32[]{:S(2)}, u32[]{:S(2)}) %collective-permute-start.16) | collective-permute-done | bytes 16416 | tf_op jit(solution)/shard_map/ppermute | solution.py:25
  121.0 1.0 shard_map.67
  122.1 10.5 %all-to-all-start = ((bf16[8,64,512]{2,1,0:T(8,128)(2,1)}), bf16[8,64,512]{2,1,0:T(8,128)(2,1)S(1)}, u32[]{:S(2)}, u32[]{:S(2)}) async-start(bf16[8,64,512]{2,1,0:T(8,128)(2,1)} %get-tuple-element.87), calls=%async_computation | async-start | bytes 1048576 | tf_op jit(solution)/shard_map/all_to_all | solution.py:210
  132.6 2.0 %collective-permute-start.17 = (f32[64,64]{1,0:T(8,128)S(1)}, f32[64,64]{1,0:T(8,128)S(1)}, u32[]{:S(2)}, u32[]{:S(2)}) collective-permute-start(f32[64,64]{1,0:T(8,128)S(1)} %get-tuple-element.89), channel_id=1, source_target_pairs={{0,16},{16,32},{32,48},{48,64},{64,80},{80,96},{96,112},{112,128},... | collective-permute-start | bytes 49160 | tf_op jit(solution)/shard_map/ppermute | solution.py:16
  134.6 3.8 %collective-permute-done.17.incoming = f32[64,64]{1,0:T(8,128)S(1)} collective-permute-done((f32[64,64]{1,0:T(8,128)S(1)}, f32[64,64]{1,0:T(8,128)S(1)}, u32[]{:S(2)}, u32[]{:S(2)}) %collective-permute-start.17) | collective-permute-done | bytes 16416 | tf_op jit(solution)/shard_map/ppermute | solution.py:16
  138.4 2.2 %collective-permute-start.18 = (bf16[64,512]{1,0:T(8,128)(2,1)S(1)}, bf16[64,512]{1,0:T(8,128)(2,1)S(1)}, u32[]{:S(2)}, u32[]{:S(2)}) collective-permute-start(bf16[64,512]{1,0:T(8,128)(2,1)S(1)} %shard_map.68.image), channel_id=1, source_target_pairs={{0,1},{1,0},{2,3},{3,2},{4,5},{5,4},{6,7},{7,6},{8,9},{9,8},{10,11... | collective-permute-start | bytes 196616 | tf_op jit(solution)/shard_map/ppermute | solution.py:25
  140.7 3.1 %collective-permute-done.18.neighbour = bf16[64,512]{1,0:T(8,128)(2,1)S(1)} collective-permute-done((bf16[64,512]{1,0:T(8,128)(2,1)S(1)}, bf16[64,512]{1,0:T(8,128)(2,1)S(1)}, u32[]{:S(2)}, u32[]{:S(2)}) %collective-permute-start.18) | collective-permute-done | bytes 65568 | tf_op jit(solution)/shard_map/ppermute | solution.py:25
  143.7 3.1 %all-to-all-done = bf16[8,64,512]{2,1,0:T(8,128)(2,1)S(1)} async-done(((bf16[8,64,512]{2,1,0:T(8,128)(2,1)}), bf16[8,64,512]{2,1,0:T(8,128)(2,1)S(1)}, u32[]{:S(2)}, u32[]{:S(2)}) %all-to-all-start) | async-done | bytes 524320 | tf_op jit(solution)/shard_map/all_to_all | solution.py:210
  146.8 0.4 shard_map.69
  147.2 6.5 %collective-permute-start.19 = (f32[2,16,8,128]{3,2,1,0:T(8,128)S(1)}, f32[2,16,8,128]{3,2,1,0:T(8,128)S(1)}, u32[]{:S(2)}, u32[]{:S(2)}) collective-permute-start(f32[2,16,8,128]{3,2,1,0:T(8,128)S(1)} %get-tuple-element.91), channel_id=1, source_target_pairs={{0,16},{16,0},{32,48},{48,32},{64,80},{80,64},{96,112},{112,96},{1... | collective-permute-start | bytes 393224 | tf_op jit(solution)/shard_map/ppermute | solution.py:25
  153.7 1.0 collective-permute-done.19.received
  154.7 2.2 %collective-permute-start.20 = (f32[16,8,128]{2,1,0:T(8,128)S(1)}, f32[16,8,128]{2,1,0:T(8,128)S(1)}, u32[]{:S(2)}, u32[]{:S(2)}) collective-permute-start(f32[16,8,128]{2,1,0:T(8,128)S(1)} %get-tuple-element.93), channel_id=1, source_target_pairs={{0,1},{1,0},{2,3},{3,2},{4,5},{5,4},{6,7},{7,6},{8,9},{9,8},{10,11... | collective-permute-start | bytes 196616 | tf_op jit(solution)/shard_map/ppermute | solution.py:25
  157.0 2.8 %collective-permute-done.20.received = f32[16,8,128]{2,1,0:T(8,128)S(1)} collective-permute-done((f32[16,8,128]{2,1,0:T(8,128)S(1)}, f32[16,8,128]{2,1,0:T(8,128)S(1)}, u32[]{:S(2)}, u32[]{:S(2)}) %collective-permute-start.20) | collective-permute-done | bytes 65568 | tf_op jit(solution)/shard_map/ppermute | solution.py:25
  159.7 16.5 %all_to_all.10 = f32[32,8,128]{2,1,0:T(8,128)S(1)} all-to-all(f32[32,8,128]{2,1,0:T(8,128)S(1)} %bitcast.35), channel_id=1, replica_groups={{0,32,64,96,128,160,192,224,256,288,320,352,384,416,448,480,512,544,576..., dimensions={0} | all-to-all | bytes 262144 | tf_op jit(solution)/shard_map/all_to_all | solution.py:231
  176.3 0.1 reduce_sum.12
  176.3 0.6 copy.12
  (12 shorter events, 0.1 us)
Async XLA Ops:
  0.6 21.4 %copy-start = (bf16[2,343,343]{2,0,1:T(2,128)(2,1)S(1)}, bf16[2,343,343]{2,0,1:T(2,128)(2,1)}, u32[]{:S(2)}) copy-start(bf16[2,343,343]{2,0,1:T(2,128)(2,1)} %param.6) | copy-start | bytes 1411792
  1.5 23.5 %collective-permute-start = (bf16[64,64]{1,0:T(8,128)(2,1)S(1)}, bf16[64,64]{1,0:T(8,128)(2,1)S(1)}, u32[]{:S(2)}, u32[]{:S(2)}) collective-permute-start(bf16[64,64]{1,0:T(8,128)(2,1)S(1)} %slice.19), channel_id=1, source_target_pairs={{0,1008},{16,0},{32,16},{48,32},{64,48},{80,64},{96,80},{112,96},{... | collective-permute-start | bytes 24584 | tf_op jit(solution)/shard_map/ppermute | solution.py:16
  22.1 2.8 %copy-start.1 = (f32[64,512]{1,0:T(8,128)S(1)}, f32[64,512]{1,0:T(8,128)}, u32[]{:S(2)}) copy-start(f32[64,512]{1,0:T(8,128)} %previous.1) | copy-start | bytes 393220
  25.9 4.0 %collective-permute-start.1 = (f32[64,64]{1,0:T(8,128)S(1)}, f32[64,64]{1,0:T(8,128)S(1)}, u32[]{:S(2)}, u32[]{:S(2)}) collective-permute-start(f32[64,64]{1,0:T(8,128)S(1)} %get-tuple-element.50), channel_id=1, source_target_pairs={{0,16},{16,0},{32,48},{48,32},{64,80},{80,64},{96,112},{112,96},{1... | collective-permute-start | bytes 49160 | tf_op jit(solution)/shard_map/ppermute | solution.py:25
  27.8 6.1 %collective-permute-start.2 = (f32[64,64]{1,0:T(8,128)S(1)}, f32[64,64]{1,0:T(8,128)S(1)}, u32[]{:S(2)}, u32[]{:S(2)}) collective-permute-start(f32[64,64]{1,0:T(8,128)S(1)} %get-tuple-element.51), channel_id=1, source_target_pairs={{16,32},{32,16},{48,64},{64,48},{80,96},{96,80},{112,128},{128,112... | collective-permute-start | bytes 49160 | tf_op jit(solution)/shard_map/ppermute | solution.py:25
  34.9 7.8 %collective-permute-start.3 = (f32[64,64]{1,0:T(8,128)S(1)}, f32[64,64]{1,0:T(8,128)S(1)}, u32[]{:S(2)}, u32[]{:S(2)}) collective-permute-start(f32[64,64]{1,0:T(8,128)S(1)} %get-tuple-element.54), channel_id=1, source_target_pairs={{0,16},{16,0},{32,48},{48,32},{64,80},{80,64},{96,112},{112,96},{1... | collective-permute-start | bytes 49160 | tf_op jit(solution)/shard_map/ppermute | solution.py:25
  40.6 6.1 %collective-permute-start.4 = (f32[64,64]{1,0:T(8,128)S(1)}, f32[64,64]{1,0:T(8,128)S(1)}, u32[]{:S(2)}, u32[]{:S(2)}) collective-permute-start(f32[64,64]{1,0:T(8,128)S(1)} %get-tuple-element.55), channel_id=1, source_target_pairs={{16,32},{32,16},{48,64},{64,48},{80,96},{96,80},{112,128},{128,112... | collective-permute-start | bytes 49160 | tf_op jit(solution)/shard_map/ppermute | solution.py:25
  47.7 7.4 %collective-permute-start.5 = (f32[64,64]{1,0:T(8,128)S(1)}, f32[64,64]{1,0:T(8,128)S(1)}, u32[]{:S(2)}, u32[]{:S(2)}) collective-permute-start(f32[64,64]{1,0:T(8,128)S(1)} %get-tuple-element.59), channel_id=1, source_target_pairs={{0,16},{16,0},{32,48},{48,32},{64,80},{80,64},{96,112},{112,96},{1... | collective-permute-start | bytes 49160 | tf_op jit(solution)/shard_map/ppermute | solution.py:25
  52.9 6.1 %collective-permute-start.6 = (f32[64,64]{1,0:T(8,128)S(1)}, f32[64,64]{1,0:T(8,128)S(1)}, u32[]{:S(2)}, u32[]{:S(2)}) collective-permute-start(f32[64,64]{1,0:T(8,128)S(1)} %get-tuple-element.60), channel_id=1, source_target_pairs={{16,32},{32,16},{48,64},{64,48},{80,96},{96,80},{112,128},{128,112... | collective-permute-start | bytes 49160 | tf_op jit(solution)/shard_map/ppermute | solution.py:25
  60.0 7.4 %collective-permute-start.7 = (f32[64,64]{1,0:T(8,128)S(1)}, f32[64,64]{1,0:T(8,128)S(1)}, u32[]{:S(2)}, u32[]{:S(2)}) collective-permute-start(f32[64,64]{1,0:T(8,128)S(1)} %get-tuple-element.64), channel_id=1, source_target_pairs={{0,16},{16,0},{32,48},{48,32},{64,80},{80,64},{96,112},{112,96},{1... | collective-permute-start | bytes 49160 | tf_op jit(solution)/shard_map/ppermute | solution.py:25
  65.2 6.1 %collective-permute-start.8 = (f32[64,64]{1,0:T(8,128)S(1)}, f32[64,64]{1,0:T(8,128)S(1)}, u32[]{:S(2)}, u32[]{:S(2)}) collective-permute-start(f32[64,64]{1,0:T(8,128)S(1)} %get-tuple-element.65), channel_id=1, source_target_pairs={{16,32},{32,16},{48,64},{64,48},{80,96},{96,80},{112,128},{128,112... | collective-permute-start | bytes 49160 | tf_op jit(solution)/shard_map/ppermute | solution.py:25
  72.3 7.4 %collective-permute-start.9 = (f32[64,64]{1,0:T(8,128)S(1)}, f32[64,64]{1,0:T(8,128)S(1)}, u32[]{:S(2)}, u32[]{:S(2)}) collective-permute-start(f32[64,64]{1,0:T(8,128)S(1)} %get-tuple-element.69), channel_id=1, source_target_pairs={{0,16},{16,0},{32,48},{48,32},{64,80},{80,64},{96,112},{112,96},{1... | collective-permute-start | bytes 49160 | tf_op jit(solution)/shard_map/ppermute | solution.py:25
  77.5 6.1 %collective-permute-start.10 = (f32[64,64]{1,0:T(8,128)S(1)}, f32[64,64]{1,0:T(8,128)S(1)}, u32[]{:S(2)}, u32[]{:S(2)}) collective-permute-start(f32[64,64]{1,0:T(8,128)S(1)} %get-tuple-element.70), channel_id=1, source_target_pairs={{16,32},{32,16},{48,64},{64,48},{80,96},{96,80},{112,128},{128,112... | collective-permute-start | bytes 49160 | tf_op jit(solution)/shard_map/ppermute | solution.py:25
  84.5 7.4 %collective-permute-start.11 = (f32[64,64]{1,0:T(8,128)S(1)}, f32[64,64]{1,0:T(8,128)S(1)}, u32[]{:S(2)}, u32[]{:S(2)}) collective-permute-start(f32[64,64]{1,0:T(8,128)S(1)} %get-tuple-element.74), channel_id=1, source_target_pairs={{0,16},{16,0},{32,48},{48,32},{64,80},{80,64},{96,112},{112,96},{1... | collective-permute-start | bytes 49160 | tf_op jit(solution)/shard_map/ppermute | solution.py:25
  89.8 6.1 %collective-permute-start.12 = (f32[64,64]{1,0:T(8,128)S(1)}, f32[64,64]{1,0:T(8,128)S(1)}, u32[]{:S(2)}, u32[]{:S(2)}) collective-permute-start(f32[64,64]{1,0:T(8,128)S(1)} %get-tuple-element.75), channel_id=1, source_target_pairs={{16,32},{32,16},{48,64},{64,48},{80,96},{96,80},{112,128},{128,112... | collective-permute-start | bytes 49160 | tf_op jit(solution)/shard_map/ppermute | solution.py:25
  96.8 7.3 %collective-permute-start.13 = (f32[64,64]{1,0:T(8,128)S(1)}, f32[64,64]{1,0:T(8,128)S(1)}, u32[]{:S(2)}, u32[]{:S(2)}) collective-permute-start(f32[64,64]{1,0:T(8,128)S(1)} %get-tuple-element.79), channel_id=1, source_target_pairs={{0,16},{16,0},{32,48},{48,32},{64,80},{80,64},{96,112},{112,96},{1... | collective-permute-start | bytes 49160 | tf_op jit(solution)/shard_map/ppermute | solution.py:25
  102.1 6.1 %collective-permute-start.14 = (f32[64,64]{1,0:T(8,128)S(1)}, f32[64,64]{1,0:T(8,128)S(1)}, u32[]{:S(2)}, u32[]{:S(2)}) collective-permute-start(f32[64,64]{1,0:T(8,128)S(1)} %get-tuple-element.80), channel_id=1, source_target_pairs={{16,32},{32,16},{48,64},{64,48},{80,96},{96,80},{112,128},{128,112... | collective-permute-start | bytes 49160 | tf_op jit(solution)/shard_map/ppermute | solution.py:25
  109.7 7.2 %collective-permute-start.15 = (f32[64,64]{1,0:T(8,128)S(1)}, f32[64,64]{1,0:T(8,128)S(1)}, u32[]{:S(2)}, u32[]{:S(2)}) collective-permute-start(f32[64,64]{1,0:T(8,128)S(1)} %get-tuple-element.84), channel_id=1, source_target_pairs={{0,16},{16,0},{32,48},{48,32},{64,80},{80,64},{96,112},{112,96},{1... | collective-permute-start | bytes 49160 | tf_op jit(solution)/shard_map/ppermute | solution.py:25
  114.9 6.1 %collective-permute-start.16 = (f32[64,64]{1,0:T(8,128)S(1)}, f32[64,64]{1,0:T(8,128)S(1)}, u32[]{:S(2)}, u32[]{:S(2)}) collective-permute-start(f32[64,64]{1,0:T(8,128)S(1)} %get-tuple-element.85), channel_id=1, source_target_pairs={{16,32},{32,16},{48,64},{64,48},{80,96},{96,80},{112,128},{128,112... | collective-permute-start | bytes 49160 | tf_op jit(solution)/shard_map/ppermute | solution.py:25
  122.1 24.8 %all-to-all-start = ((bf16[8,64,512]{2,1,0:T(8,128)(2,1)}), bf16[8,64,512]{2,1,0:T(8,128)(2,1)S(1)}, u32[]{:S(2)}, u32[]{:S(2)}) async-start(bf16[8,64,512]{2,1,0:T(8,128)(2,1)} %get-tuple-element.87), calls=%async_computation | async-start | bytes 1048576 | tf_op jit(solution)/shard_map/all_to_all | solution.py:210
  132.6 5.9 %collective-permute-start.17 = (f32[64,64]{1,0:T(8,128)S(1)}, f32[64,64]{1,0:T(8,128)S(1)}, u32[]{:S(2)}, u32[]{:S(2)}) collective-permute-start(f32[64,64]{1,0:T(8,128)S(1)} %get-tuple-element.89), channel_id=1, source_target_pairs={{0,16},{16,32},{32,48},{48,64},{64,80},{80,96},{96,112},{112,128},... | collective-permute-start | bytes 49160 | tf_op jit(solution)/shard_map/ppermute | solution.py:16
  138.4 5.3 %collective-permute-start.18 = (bf16[64,512]{1,0:T(8,128)(2,1)S(1)}, bf16[64,512]{1,0:T(8,128)(2,1)S(1)}, u32[]{:S(2)}, u32[]{:S(2)}) collective-permute-start(bf16[64,512]{1,0:T(8,128)(2,1)S(1)} %shard_map.68.image), channel_id=1, source_target_pairs={{0,1},{1,0},{2,3},{3,2},{4,5},{5,4},{6,7},{7,6},{8,9},{9,8},{10,11... | collective-permute-start | bytes 196616 | tf_op jit(solution)/shard_map/ppermute | solution.py:25
  147.2 7.5 %collective-permute-start.19 = (f32[2,16,8,128]{3,2,1,0:T(8,128)S(1)}, f32[2,16,8,128]{3,2,1,0:T(8,128)S(1)}, u32[]{:S(2)}, u32[]{:S(2)}) collective-permute-start(f32[2,16,8,128]{3,2,1,0:T(8,128)S(1)} %get-tuple-element.91), channel_id=1, source_target_pairs={{0,16},{16,0},{32,48},{48,32},{64,80},{80,64},{96,112},{112,96},{1... | collective-permute-start | bytes 393224 | tf_op jit(solution)/shard_map/ppermute | solution.py:25
  154.7 5.0 %collective-permute-start.20 = (f32[16,8,128]{2,1,0:T(8,128)S(1)}, f32[16,8,128]{2,1,0:T(8,128)S(1)}, u32[]{:S(2)}, u32[]{:S(2)}) collective-permute-start(f32[16,8,128]{2,1,0:T(8,128)S(1)} %get-tuple-element.93), channel_id=1, source_target_pairs={{0,1},{1,0},{2,3},{3,2},{4,5},{5,4},{6,7},{7,6},{8,9},{9,8},{10,11... | collective-permute-start | bytes 196616 | tf_op jit(solution)/shard_map/ppermute | solution.py:25

commit v3 on v2

v3 whole, which is shorter than its diff:
```python
import jax
import jax.numpy as jnp
from jax import lax
from jax.experimental import pallas as pl
from jax.experimental.pallas import tpu as pltpu
from jax.sharding import PartitionSpec as P

DEGREE = 8


def passed_along(value, axis, steps):
    count = lax.axis_size(axis)
    pairs = [(source, (source + steps) % count) for source in range(count)]
    return lax.ppermute(value, axis, pairs)


def swapped(value, axis, first):
    count = lax.axis_size(axis)
    pairs = []
    for low in range(first, first + count, 2):
        left, right = low % count, (low + 1) % count
        pairs += [(left, right), (right, left)]
    return lax.ppermute(value, axis, pairs)


def scattered(connectivity, cell_matrices, owned, shared):
    index = lax.broadcasted_iota(jnp.int32, (*connectivity.shape, owned + shared), 2)
    rest = jnp.where(index < 2 * shared, index + owned - shared, index - shared)
    nodes = jnp.where(index < shared, index, rest)
    chosen = (connectivity[:, :, None] == nodes).astype(jnp.bfloat16)
    half = jnp.einsum(
        "cba,cbk->cak", cell_matrices, chosen, preferred_element_type=jnp.float32
    ).astype(jnp.bfloat16)
    whole = jnp.einsum("cai,cak->cik", chosen, half, preferred_element_type=jnp.float32)
    return whole.astype(jnp.bfloat16)


def turned(value):
    middle = value.shape[1] // 2
    return jnp.concatenate([value[:, middle:], value[:, :middle]], axis=1)


def in_own(value):
    return lax.broadcasted_iota(jnp.int32, value.shape, 1) < value.shape[1] // 2


def completed(flag, fresh, link, chip):
    even = flag[0] == 0
    link, chip = turned(link), turned(chip)
    left = jnp.where(even, link, chip)
    right = jnp.where(even, chip, link)
    return fresh + jnp.where(in_own(fresh), left, right)


def fill(extended, edge, inner):
    width = edge.shape[1]
    extended[:, :width] = edge.astype(jnp.bfloat16)
    extended[:, width:] = inner.astype(jnp.bfloat16)


def multiplied(extended, weights, begin, end):
    total = None
    for cell in range(weights.shape[0]):
        part = jnp.dot(
            extended[...], weights[cell, :, begin:end], preferred_element_type=jnp.float32
        )
        total = part if total is None else total + part
    return total


def first_body(coef, start, ghost, weights, edge, inner, upcoming, extended):
    shared = ghost.shape[1]
    values = jnp.concatenate([start[:, :shared], ghost[...].astype(jnp.float32)], axis=1)
    edge[...] = values
    inner[...] = start[:, shared:]
    fill(extended, values, inner[...])
    product = multiplied(extended, weights, 0, 2 * shared)
    upcoming[...] = coef[0] * product + jnp.where(in_own(values), coef[1] * values, 0.0)


def edge_body(flag, coef, fresh, link, chip, inner, before, weights, edge, upcoming, extended):
    values = completed(flag, fresh[...], link[...], chip[...])
    edge[...] = values
    fill(extended, values, inner[...])
    product = multiplied(extended, weights, 0, values.shape[1])
    kept = coef[1] * values + coef[2] * before[...]
    upcoming[...] = coef[0] * product + jnp.where(in_own(values), kept, 0.0)


def inner_body(coef, edge, inner, weights, *rest):
    before, upcoming, extended = rest if len(rest) == 3 else (None, *rest)
    fill(extended, edge[...], inner[...])
    product = multiplied(extended, weights, edge.shape[1], weights.shape[2])
    fresh = coef[0] * product + coef[1] * inner[...]
    if before is not None:
        fresh = fresh + coef[2] * before[...]
    upcoming[...] = fresh


def last_edge_body(flag, fresh, link, chip, inner, weights, edge, low, product, extended):
    values = completed(flag, fresh[...], link[...], chip[...])
    edge[...] = values
    fill(extended, values, inner[...])
    shared = values.shape[1] // 2
    rounded = jnp.concatenate([inner[...], values[:, :shared]], axis=1).astype(jnp.bfloat16)
    low[...] = jnp.broadcast_to(rounded[None], low.shape)
    product[...] = multiplied(extended, weights, 0, values.shape[1])


def last_inner_body(edge, inner, weights, filtered, product, extended):
    shared = edge.shape[1] // 2
    fill(extended, edge[...], inner[...])
    product[...] = multiplied(extended, weights, edge.shape[1], weights.shape[2])
    filtered[...] = jnp.concatenate([edge[:, :shared], inner[...]], axis=1)


def finish_body(edge, inner, incoming, image):
    shared = edge.shape[1] // 2
    first = edge[:, :shared] + incoming[:, shared:]
    image[...] = jnp.concatenate([inner[...], first], axis=1).astype(jnp.bfloat16)


def project_body(flag, lows, image, neighbour, keep, handed):
    states = image.shape[0]
    images = jnp.concatenate([image[...], neighbour[...]], axis=0)
    partial = lax.dot_general(
        lows[...], images, (((1,), (1,)), ((), ())), preferred_element_type=jnp.float32
    )
    rows = partial.reshape(partial.shape[0] // 32, 2, 2, 8, 2 * states)
    even = flag[0] == 0
    mine = jnp.where(even, rows[:, 0], rows[:, 1])
    other = jnp.where(even, rows[:, 1], rows[:, 0])
    for place, value in ((keep, mine), (handed, other)):
        place[0] = jnp.concatenate([value[:, 0, :, :states], value[:, 1, :, :states]], axis=2)
        place[1] = jnp.concatenate([value[:, 0, :, states:], value[:, 1, :, states:]], axis=2)


def add_body(keep, received, own, other):
    own[...] = keep[0] + received[0]
    other[...] = keep[1] + received[1]


def place_body(half, own, received, out):
    low = half[0] == 0
    groups = out.shape[0]
    mine = own[...].reshape(groups, 2, *own.shape[1:])
    theirs = received[...].reshape(groups, 2, *own.shape[1:])
    out[:, 0] = jnp.where(low, mine, theirs)
    out[:, 1] = jnp.where(low, theirs, mine)


def kernel(body, scalars, out_shape, scratch):
    def run(*operands):
        small, large = operands[:scalars], operands[scalars:]
        large = [pltpu.with_memory_space_constraint(value, pltpu.VMEM) for value in large]
        in_specs = [pl.BlockSpec(memory_space=pltpu.SMEM)] * scalars
        in_specs += [pl.BlockSpec(memory_space=pltpu.VMEM)] * len(large)
        single = not isinstance(out_shape, tuple)
        outs = pl.BlockSpec(memory_space=pltpu.VMEM)
        return pl.pallas_call(
            body,
            in_specs=in_specs,
            out_specs=outs if single else (outs,) * len(out_shape),
            out_shape=out_shape,
            scratch_shapes=scratch,
            compiler_params=pltpu.CompilerParams(vmem_limit_bytes=16 * 2**20),
        )(*small, *large)

    return run


def alternate(count):
    return [list(range(first, count, 2)) for first in range(2)]


def exchanged(value):
    link = swapped(value, "cell", 1)
    chip = swapped(value, "cell", 0)
    return link, chip


def per_device(start_block, connectivity, cell_matrices, bounds):
    f32 = jnp.float32
    states, owned = start_block.shape
    shared = owned // 8
    extent = owned + shared
    flag = (lax.axis_index("cell") % 2).astype(jnp.int32).reshape(1)
    weights = scattered(connectivity, cell_matrices, owned, shared)

    peers = lax.axis_size("state")
    line = peers // 2
    bf16 = jnp.bfloat16
    rim = pltpu.VMEM((states, 2 * shared), f32)
    core = pltpu.VMEM((states, owned - shared), f32)
    scratch = [pltpu.VMEM((states, extent), bf16)]
    first = kernel(first_body, 1, (rim, core, rim), scratch)
    edge_step = kernel(edge_body, 2, (rim, rim), scratch)
    inner_step = kernel(inner_body, 1, core, scratch)
    lows = pltpu.VMEM((line, states, owned), bf16)
    last_edge = kernel(last_edge_body, 1, (rim, lows, rim), scratch)
    out = jax.ShapeDtypeStruct((states, owned), f32)
    last_inner = kernel(last_inner_body, 0, (out, core), scratch)

    lowest, cut, upper = (bounds[0], bounds[1], bounds[2])
    half = (upper - cut) / 2.0
    centre = (upper + cut) / 2.0
    sigma = half / (lowest - centre)
    tau = 2.0 / sigma
    coefs = [jnp.stack([sigma / half, -centre * (sigma / half), jnp.zeros((), f32)])]
    for _ in range(2, DEGREE + 1):
        sigma_new = 1.0 / (tau - sigma)
        scale = 2.0 * sigma_new / half
        coefs.append(jnp.stack([scale, -centre * scale, -(sigma * sigma_new)]))
        sigma = sigma_new

    ghost = passed_along(start_block[:, :shared].astype(bf16), "cell", -1)
    edge, inner, fresh = first(coefs[0], start_block, ghost, weights)
    before = ()
    for number, coef in enumerate(coefs):
        link, chip = exchanged(fresh)
        upcoming = inner_step(coef, edge, inner, weights, *before)
        before, inner = (inner,), upcoming
        if number + 1 < len(coefs):
            edge, fresh = edge_step(
                flag, coefs[number + 1], fresh, link, chip, inner, edge, weights
            )
    edge, low, edge_product = last_edge(flag, fresh, link, chip, inner, weights)
    incoming = passed_along(edge_product, "cell", 1)
    lows = lax.all_to_all(low, "state", 0, 0, axis_index_groups=alternate(peers), tiled=True)
    filtered, inner_product = last_inner(edge, inner, weights)
    lows = lows.reshape(line * states, owned)
    shape = pltpu.VMEM((states, owned), bf16)
    image = kernel(finish_body, 0, shape, [])(
        edge_product, inner_product, incoming
    )
    neighbour = swapped(image, "state", 0)

    count = lax.axis_size("cell")
    half = (lax.axis_index("state") % 2).astype(jnp.int32).reshape(1)
    number = line * states // 32
    both = pltpu.VMEM((2, number, 8, 2 * states), f32)
    keep, handed = kernel(project_body, 1, (both, both), [])(flag, lows, image, neighbour)
    part = pltpu.VMEM((number, 8, 2 * states), f32)
    own, other = kernel(add_body, 0, (part, part), [])(keep, swapped(handed, "cell", 0))
    received = swapped(other, "state", 0)
    shape = pltpu.VMEM((number // 2, 2, 2, 8, 2 * states), f32)
    pieces = kernel(place_body, 1, shape, [])(half, own, received)
    pieces = pieces.reshape(2 * number, 8, 2 * states)
    arrived = lax.all_to_all(
        pieces, "cell", 0, 0, axis_index_groups=alternate(count), tiled=True
    )
    rows = peers * states // count
    total = jnp.sum(arrived.reshape(count // 2, rows // 16, 8, 2, states), axis=0)
    projected = jnp.swapaxes(total, 1, 2).reshape(rows, states)
    return (filtered, projected)


def solution(mesh):
    in_specs = (P("state", "cell"), P("cell", None), P("cell", None, None), P())
    out_specs = (P("state", "cell"), P("cell", "state"))
    return jax.shard_map(
        per_device, mesh=mesh, in_specs=in_specs, out_specs=out_specs, check_vma=False
    )
```

time: 178 us -> 177 us (level)
  waiting for transfers between devices: 46.2 us -> 37.9 us
  Pallas kernels: 9.26 us -> 15.9 us
    ppermute x19, waiting for transfers between devices: 39.3 us -> 32.1 us  [swapped(): return lax.ppermute(value, axis, pairs)]
    pallas_call x13 -> x22, Pallas kernels: 9.26 us -> 15.9 us  [run(): pl.pallas_call(body, in_specs=in_specs, out_specs=outs if single else (ou...]
  transfers between devices with their start and end apart: 22 -> 22, of which waited for: 13 -> 13; matrix products, arithmetic and copies ran while one was open for 3% -> 3% of each run, Pallas kernels for 0% -> 5%
where the time goes in v3:
time: 177 us; the launch traced here: 176 us
  starting transfers between devices  94.1 us (53%)
  waiting for transfers between devices  37.9 us (21%)
  blocking collectives  16.4 us (9%)
  Pallas kernels  15.9 us (9%)
  between operations  5.16 us (3%)
  local copies, waits for them, and re-layouts  2.94 us (2%)
  matrix products  2.5 us (1%)
    ppermute x19, starting transfers between devices, swapped(): return lax.ppermute(value, axis, pairs)  65.5 us
    ppermute x19, waiting for transfers between devices, swapped(): return lax.ppermute(value, axis, pairs)  32.1 us
    ppermute x2, starting transfers between devices, passed_along(): return lax.ppermute(value, axis, pairs)  18.1 us
    all_to_all x1, blocking collectives, per_device(): lax.all_to_all(pieces, 'cell', 0, 0, axis_index_groups=alternate(count),...  16.4 us
    pallas_call x22, Pallas kernels, run(): pl.pallas_call(body, in_specs=in_specs, out_specs=outs if single else (ou...  15.9 us
    all_to_all x1, starting transfers between devices, per_device(): lax.all_to_all(low, 'state', 0, 0, axis_index_groups=alternate(peers), ti...  10.5 us
  transfers between devices with their start and end apart: 22, of which 13 were waited for; matrix products, arithmetic and copies ran while one was open for 3% of the time, Pallas kernels for 5%

profile of v3, /device:TPU:1, one launch (start us, length us, event | category | flops | bytes accessed | tf_op | source)
XLA Modules:
  0.0 175.5 jit_solution(254203951912132896)
XLA Ops:
  0.6 0.8 slice.19
  1.5 16.0 %collective-permute-start = (bf16[64,64]{1,0:T(8,128)(2,1)S(1)}, bf16[64,64]{1,0:T(8,128)(2,1)S(1)}, u32[]{:S(2)}, u32[]{:S(2)}) collective-permute-start(bf16[64,64]{1,0:T(8,128)(2,1)S(1)} %slice.19), channel_id=1, source_target_pairs={{0,1008},{16,0},{32,16},{48,32},{64,48},{80,64},{96,80},{112,96},{... | collective-permute-start | bytes 24584 | tf_op jit(solution)/shard_map/ppermute | solution.py:14
  17.5 1.4 fusion.12
  22.3 2.5 %convolution_convert_fusion.weights = bf16[2,576,576]{2,1,0:T(8,128)(2,1)S(1)} fusion(s32[576]{0:T(1024)S(1)} %get-tuple-element.57, s32[576]{0:T(1024)S(1)} %get-tuple-element.58, s32[2,343]{1,0:T(2,128)} %param.5, pred[576]{0:T(1024)(128)(4,1)S(1)} %get-tuple-element.59, pred[576]{0:T(1024)(128)(4,1)S(1)} %get-tuple-element.60, ...), kind=kOutput, calls=%fused_computation.1 | convolution fusion | flops 729689472 | bytes 1806204 | tf_op jit(solution)/shard_map/cai,cak->cik/dot_general | solution.py:34
  25.1 0.8 shard_map.59
  25.9 1.9 %collective-permute-start.2 = (f32[64,128]{1,0:T(8,128)S(1)}, f32[64,128]{1,0:T(8,128)S(1)}, u32[]{:S(2)}, u32[]{:S(2)}) collective-permute-start(f32[64,128]{1,0:T(8,128)S(1)} %get-tuple-element.28.fresh), channel_id=1, source_target_pairs={{0,16},{16,0},{32,48},{48,32},{64,80},{80,64},{96,112},{112,96},{1... | collective-permute-start | bytes 98312 | tf_op jit(solution)/shard_map/ppermute | solution.py:23
  27.8 1.9 %collective-permute-start.1 = (f32[64,128]{1,0:T(8,128)S(1)}, f32[64,128]{1,0:T(8,128)S(1)}, u32[]{:S(2)}, u32[]{:S(2)}) collective-permute-start(f32[64,128]{1,0:T(8,128)S(1)} %get-tuple-element.28.fresh), channel_id=1, source_target_pairs={{16,32},{32,16},{48,64},{64,48},{80,96},{96,80},{112,128},{128,112... | collective-permute-start | bytes 98312 | tf_op jit(solution)/shard_map/ppermute | solution.py:23
  29.8 0.1 pad_maximum_fusion.6.coef
  29.9 0.9 shard_map.60.inner.rest_0_
  30.9 3.1 %collective-permute-done.1.link = f32[64,128]{1,0:T(8,128)S(1)} collective-permute-done((f32[64,128]{1,0:T(8,128)S(1)}, f32[64,128]{1,0:T(8,128)S(1)}, u32[]{:S(2)}, u32[]{:S(2)}) %collective-permute-start.1) | collective-permute-done | bytes 32800 | tf_op jit(solution)/shard_map/ppermute | solution.py:23
  34.0 0.8 shard_map.61
  34.8 5.7 %collective-permute-start.4 = (f32[64,128]{1,0:T(8,128)S(1)}, f32[64,128]{1,0:T(8,128)S(1)}, u32[]{:S(2)}, u32[]{:S(2)}) collective-permute-start(f32[64,128]{1,0:T(8,128)S(1)} %get-tuple-element.31.fresh), channel_id=1, source_target_pairs={{0,16},{16,0},{32,48},{48,32},{64,80},{80,64},{96,112},{112,96},{1... | collective-permute-start | bytes 98312 | tf_op jit(solution)/shard_map/ppermute | solution.py:23
  40.5 1.9 %collective-permute-start.3 = (f32[64,128]{1,0:T(8,128)S(1)}, f32[64,128]{1,0:T(8,128)S(1)}, u32[]{:S(2)}, u32[]{:S(2)}) collective-permute-start(f32[64,128]{1,0:T(8,128)S(1)} %get-tuple-element.31.fresh), channel_id=1, source_target_pairs={{16,32},{32,16},{48,64},{64,48},{80,96},{96,80},{112,128},{128,112... | collective-permute-start | bytes 98312 | tf_op jit(solution)/shard_map/ppermute | solution.py:23
  42.4 0.1 pad_maximum_fusion.5.coef
  42.6 0.9 shard_map.62.inner.rest_0_
  43.5 3.1 %collective-permute-done.3.link = f32[64,128]{1,0:T(8,128)S(1)} collective-permute-done((f32[64,128]{1,0:T(8,128)S(1)}, f32[64,128]{1,0:T(8,128)S(1)}, u32[]{:S(2)}, u32[]{:S(2)}) %collective-permute-start.3) | collective-permute-done | bytes 32800 | tf_op jit(solution)/shard_map/ppermute | solution.py:23
  46.6 0.8 shard_map.63
  47.4 5.2 %collective-permute-start.6 = (f32[64,128]{1,0:T(8,128)S(1)}, f32[64,128]{1,0:T(8,128)S(1)}, u32[]{:S(2)}, u32[]{:S(2)}) collective-permute-start(f32[64,128]{1,0:T(8,128)S(1)} %get-tuple-element.33.fresh), channel_id=1, source_target_pairs={{0,16},{16,0},{32,48},{48,32},{64,80},{80,64},{96,112},{112,96},{1... | collective-permute-start | bytes 98312 | tf_op jit(solution)/shard_map/ppermute | solution.py:23
  52.7 1.9 %collective-permute-start.5 = (f32[64,128]{1,0:T(8,128)S(1)}, f32[64,128]{1,0:T(8,128)S(1)}, u32[]{:S(2)}, u32[]{:S(2)}) collective-permute-start(f32[64,128]{1,0:T(8,128)S(1)} %get-tuple-element.33.fresh), channel_id=1, source_target_pairs={{16,32},{32,16},{48,64},{64,48},{80,96},{96,80},{112,128},{128,112... | collective-permute-start | bytes 98312 | tf_op jit(solution)/shard_map/ppermute | solution.py:23
  54.8 0.9 shard_map.64.inner.rest_0_
  55.7 3.1 %collective-permute-done.5.link = f32[64,128]{1,0:T(8,128)S(1)} collective-permute-done((f32[64,128]{1,0:T(8,128)S(1)}, f32[64,128]{1,0:T(8,128)S(1)}, u32[]{:S(2)}, u32[]{:S(2)}) %collective-permute-start.5) | collective-permute-done | bytes 32800 | tf_op jit(solution)/shard_map/ppermute | solution.py:23
  58.8 0.8 shard_map.65
  59.6 5.2 %collective-permute-start.8 = (f32[64,128]{1,0:T(8,128)S(1)}, f32[64,128]{1,0:T(8,128)S(1)}, u32[]{:S(2)}, u32[]{:S(2)}) collective-permute-start(f32[64,128]{1,0:T(8,128)S(1)} %get-tuple-element.35.fresh), channel_id=1, source_target_pairs={{0,16},{16,0},{32,48},{48,32},{64,80},{80,64},{96,112},{112,96},{1... | collective-permute-start | bytes 98312 | tf_op jit(solution)/shard_map/ppermute | solution.py:23
  64.8 1.9 %collective-permute-start.7 = (f32[64,128]{1,0:T(8,128)S(1)}, f32[64,128]{1,0:T(8,128)S(1)}, u32[]{:S(2)}, u32[]{:S(2)}) collective-permute-start(f32[64,128]{1,0:T(8,128)S(1)} %get-tuple-element.35.fresh), channel_id=1, source_target_pairs={{16,32},{32,16},{48,64},{64,48},{80,96},{96,80},{112,128},{128,112... | collective-permute-start | bytes 98312 | tf_op jit(solution)/shard_map/ppermute | solution.py:23
  66.8 0.1 pad_maximum_fusion.3.coef
  67.0 0.9 shard_map.66.inner.rest_0_
  67.9 3.1 %collective-permute-done.7.link = f32[64,128]{1,0:T(8,128)S(1)} collective-permute-done((f32[64,128]{1,0:T(8,128)S(1)}, f32[64,128]{1,0:T(8,128)S(1)}, u32[]{:S(2)}, u32[]{:S(2)}) %collective-permute-start.7) | collective-permute-done | bytes 32800 | tf_op jit(solution)/shard_map/ppermute | solution.py:23
  71.0 0.8 shard_map.67
  71.8 5.2 %collective-permute-start.10 = (f32[64,128]{1,0:T(8,128)S(1)}, f32[64,128]{1,0:T(8,128)S(1)}, u32[]{:S(2)}, u32[]{:S(2)}) collective-permute-start(f32[64,128]{1,0:T(8,128)S(1)} %get-tuple-element.37.fresh), channel_id=1, source_target_pairs={{0,16},{16,0},{32,48},{48,32},{64,80},{80,64},{96,112},{112,96},{1... | collective-permute-start | bytes 98312 | tf_op jit(solution)/shard_map/ppermute | solution.py:23
  77.0 1.9 %collective-permute-start.9 = (f32[64,128]{1,0:T(8,128)S(1)}, f32[64,128]{1,0:T(8,128)S(1)}, u32[]{:S(2)}, u32[]{:S(2)}) collective-permute-start(f32[64,128]{1,0:T(8,128)S(1)} %get-tuple-element.37.fresh), channel_id=1, source_target_pairs={{16,32},{32,16},{48,64},{64,48},{80,96},{96,80},{112,128},{128,112... | collective-permute-start | bytes 98312 | tf_op jit(solution)/shard_map/ppermute | solution.py:23
  79.1 0.9 shard_map.68.inner.rest_0_
  80.0 3.1 %collective-permute-done.9.link = f32[64,128]{1,0:T(8,128)S(1)} collective-permute-done((f32[64,128]{1,0:T(8,128)S(1)}, f32[64,128]{1,0:T(8,128)S(1)}, u32[]{:S(2)}, u32[]{:S(2)}) %collective-permute-start.9) | collective-permute-done | bytes 32800 | tf_op jit(solution)/shard_map/ppermute | solution.py:23
  83.2 0.8 shard_map.69
  83.9 5.2 %collective-permute-start.12 = (f32[64,128]{1,0:T(8,128)S(1)}, f32[64,128]{1,0:T(8,128)S(1)}, u32[]{:S(2)}, u32[]{:S(2)}) collective-permute-start(f32[64,128]{1,0:T(8,128)S(1)} %get-tuple-element.39.fresh), channel_id=1, source_target_pairs={{0,16},{16,0},{32,48},{48,32},{64,80},{80,64},{96,112},{112,96},{1... | collective-permute-start | bytes 98312 | tf_op jit(solution)/shard_map/ppermute | solution.py:23
  89.2 1.9 %collective-permute-start.11 = (f32[64,128]{1,0:T(8,128)S(1)}, f32[64,128]{1,0:T(8,128)S(1)}, u32[]{:S(2)}, u32[]{:S(2)}) collective-permute-start(f32[64,128]{1,0:T(8,128)S(1)} %get-tuple-element.39.fresh), channel_id=1, source_target_pairs={{16,32},{32,16},{48,64},{64,48},{80,96},{96,80},{112,128},{128,112... | collective-permute-start | bytes 98312 | tf_op jit(solution)/shard_map/ppermute | solution.py:23
  91.3 0.9 shard_map.70.inner.rest_0_
  92.2 3.1 %collective-permute-done.11.link = f32[64,128]{1,0:T(8,128)S(1)} collective-permute-done((f32[64,128]{1,0:T(8,128)S(1)}, f32[64,128]{1,0:T(8,128)S(1)}, u32[]{:S(2)}, u32[]{:S(2)}) %collective-permute-start.11) | collective-permute-done | bytes 32800 | tf_op jit(solution)/shard_map/ppermute | solution.py:23
  95.3 0.8 shard_map.71
  96.1 5.2 %collective-permute-start.14 = (f32[64,128]{1,0:T(8,128)S(1)}, f32[64,128]{1,0:T(8,128)S(1)}, u32[]{:S(2)}, u32[]{:S(2)}) collective-permute-start(f32[64,128]{1,0:T(8,128)S(1)} %get-tuple-element.41.fresh), channel_id=1, source_target_pairs={{0,16},{16,0},{32,48},{48,32},{64,80},{80,64},{96,112},{112,96},{1... | collective-permute-start | bytes 98312 | tf_op jit(solution)/shard_map/ppermute | solution.py:23
  101.4 1.9 %collective-permute-start.13 = (f32[64,128]{1,0:T(8,128)S(1)}, f32[64,128]{1,0:T(8,128)S(1)}, u32[]{:S(2)}, u32[]{:S(2)}) collective-permute-start(f32[64,128]{1,0:T(8,128)S(1)} %get-tuple-element.41.fresh), channel_id=1, source_target_pairs={{16,32},{32,16},{48,64},{64,48},{80,96},{96,80},{112,128},{128,112... | collective-permute-start | bytes 98312 | tf_op jit(solution)/shard_map/ppermute | solution.py:23
  103.4 0.9 shard_map.72.inner
  104.3 3.2 %collective-permute-done.13.link = f32[64,128]{1,0:T(8,128)S(1)} collective-permute-done((f32[64,128]{1,0:T(8,128)S(1)}, f32[64,128]{1,0:T(8,128)S(1)}, u32[]{:S(2)}, u32[]{:S(2)}) %collective-permute-start.13) | collective-permute-done | bytes 32800 | tf_op jit(solution)/shard_map/ppermute | solution.py:23
  107.5 0.8 shard_map.73
  108.3 5.2 %collective-permute-start.16 = (f32[64,128]{1,0:T(8,128)S(1)}, f32[64,128]{1,0:T(8,128)S(1)}, u32[]{:S(2)}, u32[]{:S(2)}) collective-permute-start(f32[64,128]{1,0:T(8,128)S(1)} %get-tuple-element.43.fresh), channel_id=1, source_target_pairs={{0,16},{16,0},{32,48},{48,32},{64,80},{80,64},{96,112},{112,96},{1... | collective-permute-start | bytes 98312 | tf_op jit(solution)/shard_map/ppermute | solution.py:23
  113.5 1.9 %collective-permute-start.15 = (f32[64,128]{1,0:T(8,128)S(1)}, f32[64,128]{1,0:T(8,128)S(1)}, u32[]{:S(2)}, u32[]{:S(2)}) collective-permute-start(f32[64,128]{1,0:T(8,128)S(1)} %get-tuple-element.43.fresh), channel_id=1, source_target_pairs={{16,32},{32,16},{48,64},{64,48},{80,96},{96,80},{112,128},{128,112... | collective-permute-start | bytes 98312 | tf_op jit(solution)/shard_map/ppermute | solution.py:23
  115.5 0.9 shard_map.74.inner
  116.4 3.3 %collective-permute-done.15.link = f32[64,128]{1,0:T(8,128)S(1)} collective-permute-done((f32[64,128]{1,0:T(8,128)S(1)}, f32[64,128]{1,0:T(8,128)S(1)}, u32[]{:S(2)}, u32[]{:S(2)}) %collective-permute-start.15) | collective-permute-done | bytes 32800 | tf_op jit(solution)/shard_map/ppermute | solution.py:23
  119.7 1.0 shard_map.75
  120.7 10.5 %all-to-all-start = ((bf16[8,64,512]{2,1,0:T(8,128)(2,1)}), bf16[8,64,512]{2,1,0:T(8,128)(2,1)S(1)}, u32[]{:S(2)}, u32[]{:S(2)}) async-start(bf16[8,64,512]{2,1,0:T(8,128)(2,1)} %get-tuple-element.47), calls=%async_computation | async-start | bytes 1048576 | tf_op jit(solution)/shard_map/all_to_all | solution.py:229
  131.2 2.0 %collective-permute-start.17 = (f32[64,128]{1,0:T(8,128)S(1)}, f32[64,128]{1,0:T(8,128)S(1)}, u32[]{:S(2)}, u32[]{:S(2)}) collective-permute-start(f32[64,128]{1,0:T(8,128)S(1)} %get-tuple-element.48.edge), channel_id=1, source_target_pairs={{0,16},{16,32},{32,48},{48,64},{64,80},{80,96},{96,112},{112,128},... | collective-permute-start | bytes 98312 | tf_op jit(solution)/shard_map/ppermute | solution.py:14
  133.2 0.9 shard_map.76
  134.2 2.9 %collective-permute-done.17.incoming = f32[64,128]{1,0:T(8,128)S(1)} collective-permute-done((f32[64,128]{1,0:T(8,128)S(1)}, f32[64,128]{1,0:T(8,128)S(1)}, u32[]{:S(2)}, u32[]{:S(2)}) %collective-permute-start.17) | collective-permute-done | bytes 32800 | tf_op jit(solution)/shard_map/ppermute | solution.py:14
  137.0 0.1 shard_map.77.image
  137.2 2.2 %collective-permute-start.18 = (bf16[64,512]{1,0:T(8,128)(2,1)S(1)}, bf16[64,512]{1,0:T(8,128)(2,1)S(1)}, u32[]{:S(2)}, u32[]{:S(2)}) collective-permute-start(bf16[64,512]{1,0:T(8,128)(2,1)S(1)} %shard_map.77.image), channel_id=1, source_target_pairs={{0,1},{1,0},{2,3},{3,2},{4,5},{5,4},{6,7},{7,6},{8,9},{9,8},{10,11... | collective-permute-start | bytes 196616 | tf_op jit(solution)/shard_map/ppermute | solution.py:23
  139.4 3.1 %collective-permute-done.18.neighbour = bf16[64,512]{1,0:T(8,128)(2,1)S(1)} collective-permute-done((bf16[64,512]{1,0:T(8,128)(2,1)S(1)}, bf16[64,512]{1,0:T(8,128)(2,1)S(1)}, u32[]{:S(2)}, u32[]{:S(2)}) %collective-permute-start.18) | collective-permute-done | bytes 65568 | tf_op jit(solution)/shard_map/ppermute | solution.py:23
  142.5 3.0 %all-to-all-done = bf16[8,64,512]{2,1,0:T(8,128)(2,1)S(1)} async-done(((bf16[8,64,512]{2,1,0:T(8,128)(2,1)}), bf16[8,64,512]{2,1,0:T(8,128)(2,1)S(1)}, u32[]{:S(2)}, u32[]{:S(2)}) %all-to-all-start) | async-done | bytes 524320 | tf_op jit(solution)/shard_map/all_to_all | solution.py:229
  145.4 0.4 shard_map.78
  145.8 6.6 %collective-permute-start.19 = (f32[2,16,8,128]{3,2,1,0:T(8,128)S(1)}, f32[2,16,8,128]{3,2,1,0:T(8,128)S(1)}, u32[]{:S(2)}, u32[]{:S(2)}) collective-permute-start(f32[2,16,8,128]{3,2,1,0:T(8,128)S(1)} %get-tuple-element.51), channel_id=1, source_target_pairs={{0,16},{16,0},{32,48},{48,32},{64,80},{80,64},{96,112},{112,96},{1... | collective-permute-start | bytes 393224 | tf_op jit(solution)/shard_map/ppermute | solution.py:23
  152.5 1.0 collective-permute-done.19.received
  153.4 2.2 %collective-permute-start.20 = (f32[16,8,128]{2,1,0:T(8,128)S(1)}, f32[16,8,128]{2,1,0:T(8,128)S(1)}, u32[]{:S(2)}, u32[]{:S(2)}) collective-permute-start(f32[16,8,128]{2,1,0:T(8,128)S(1)} %get-tuple-element.53), channel_id=1, source_target_pairs={{0,1},{1,0},{2,3},{3,2},{4,5},{5,4},{6,7},{7,6},{8,9},{9,8},{10,11... | collective-permute-start | bytes 196616 | tf_op jit(solution)/shard_map/ppermute | solution.py:23
  155.7 2.8 %collective-permute-done.20.received = f32[16,8,128]{2,1,0:T(8,128)S(1)} collective-permute-done((f32[16,8,128]{2,1,0:T(8,128)S(1)}, f32[16,8,128]{2,1,0:T(8,128)S(1)}, u32[]{:S(2)}, u32[]{:S(2)}) %collective-permute-start.20) | collective-permute-done | bytes 65568 | tf_op jit(solution)/shard_map/ppermute | solution.py:23
  158.5 16.4 %all_to_all.10 = f32[32,8,128]{2,1,0:T(8,128)S(1)} all-to-all(f32[32,8,128]{2,1,0:T(8,128)S(1)} %bitcast.35), channel_id=1, replica_groups={{0,32,64,96,128,160,192,224,256,288,320,352,384,416,448,480,512,544,576..., dimensions={0} | all-to-all | bytes 262144 | tf_op jit(solution)/shard_map/all_to_all | solution.py:249
  174.9 0.1 reduce_sum.12
  174.9 0.6 copy.12
  (23 shorter events, 0.5 us)
Async XLA Ops:
  0.6 21.7 %copy-start = (bf16[2,343,343]{2,0,1:T(2,128)(2,1)S(1)}, bf16[2,343,343]{2,0,1:T(2,128)(2,1)}, u32[]{:S(2)}) copy-start(bf16[2,343,343]{2,0,1:T(2,128)(2,1)} %param.6) | copy-start | bytes 1411792
  1.5 23.6 %collective-permute-start = (bf16[64,64]{1,0:T(8,128)(2,1)S(1)}, bf16[64,64]{1,0:T(8,128)(2,1)S(1)}, u32[]{:S(2)}, u32[]{:S(2)}) collective-permute-start(bf16[64,64]{1,0:T(8,128)(2,1)S(1)} %slice.19), channel_id=1, source_target_pairs={{0,1008},{16,0},{32,16},{48,32},{64,48},{80,64},{96,80},{112,96},{... | collective-permute-start | bytes 24584 | tf_op jit(solution)/shard_map/ppermute | solution.py:14
  22.3 2.8 %copy-start.1 = (f32[64,512]{1,0:T(8,128)S(1)}, f32[64,512]{1,0:T(8,128)}, u32[]{:S(2)}) copy-start(f32[64,512]{1,0:T(8,128)} %start.1) | copy-start | bytes 393220
  25.9 4.9 %collective-permute-start.2 = (f32[64,128]{1,0:T(8,128)S(1)}, f32[64,128]{1,0:T(8,128)S(1)}, u32[]{:S(2)}, u32[]{:S(2)}) collective-permute-start(f32[64,128]{1,0:T(8,128)S(1)} %get-tuple-element.28.fresh), channel_id=1, source_target_pairs={{0,16},{16,0},{32,48},{48,32},{64,80},{80,64},{96,112},{112,96},{1... | collective-permute-start | bytes 98312 | tf_op jit(solution)/shard_map/ppermute | solution.py:23
  27.8 6.1 %collective-permute-start.1 = (f32[64,128]{1,0:T(8,128)S(1)}, f32[64,128]{1,0:T(8,128)S(1)}, u32[]{:S(2)}, u32[]{:S(2)}) collective-permute-start(f32[64,128]{1,0:T(8,128)S(1)} %get-tuple-element.28.fresh), channel_id=1, source_target_pairs={{16,32},{32,16},{48,64},{64,48},{80,96},{96,80},{112,128},{128,112... | collective-permute-start | bytes 98312 | tf_op jit(solution)/shard_map/ppermute | solution.py:23
  34.8 8.7 %collective-permute-start.4 = (f32[64,128]{1,0:T(8,128)S(1)}, f32[64,128]{1,0:T(8,128)S(1)}, u32[]{:S(2)}, u32[]{:S(2)}) collective-permute-start(f32[64,128]{1,0:T(8,128)S(1)} %get-tuple-element.31.fresh), channel_id=1, source_target_pairs={{0,16},{16,0},{32,48},{48,32},{64,80},{80,64},{96,112},{112,96},{1... | collective-permute-start | bytes 98312 | tf_op jit(solution)/shard_map/ppermute | solution.py:23
  40.5 6.1 %collective-permute-start.3 = (f32[64,128]{1,0:T(8,128)S(1)}, f32[64,128]{1,0:T(8,128)S(1)}, u32[]{:S(2)}, u32[]{:S(2)}) collective-permute-start(f32[64,128]{1,0:T(8,128)S(1)} %get-tuple-element.31.fresh), channel_id=1, source_target_pairs={{16,32},{32,16},{48,64},{64,48},{80,96},{96,80},{112,128},{128,112... | collective-permute-start | bytes 98312 | tf_op jit(solution)/shard_map/ppermute | solution.py:23
  47.4 8.3 %collective-permute-start.6 = (f32[64,128]{1,0:T(8,128)S(1)}, f32[64,128]{1,0:T(8,128)S(1)}, u32[]{:S(2)}, u32[]{:S(2)}) collective-permute-start(f32[64,128]{1,0:T(8,128)S(1)} %get-tuple-element.33.fresh), channel_id=1, source_target_pairs={{0,16},{16,0},{32,48},{48,32},{64,80},{80,64},{96,112},{112,96},{1... | collective-permute-start | bytes 98312 | tf_op jit(solution)/shard_map/ppermute | solution.py:23
  52.7 6.1 %collective-permute-start.5 = (f32[64,128]{1,0:T(8,128)S(1)}, f32[64,128]{1,0:T(8,128)S(1)}, u32[]{:S(2)}, u32[]{:S(2)}) collective-permute-start(f32[64,128]{1,0:T(8,128)S(1)} %get-tuple-element.33.fresh), channel_id=1, source_target_pairs={{16,32},{32,16},{48,64},{64,48},{80,96},{96,80},{112,128},{128,112... | collective-permute-start | bytes 98312 | tf_op jit(solution)/shard_map/ppermute | solution.py:23
  59.6 8.2 %collective-permute-start.8 = (f32[64,128]{1,0:T(8,128)S(1)}, f32[64,128]{1,0:T(8,128)S(1)}, u32[]{:S(2)}, u32[]{:S(2)}) collective-permute-start(f32[64,128]{1,0:T(8,128)S(1)} %get-tuple-element.35.fresh), channel_id=1, source_target_pairs={{0,16},{16,0},{32,48},{48,32},{64,80},{80,64},{96,112},{112,96},{1... | collective-permute-start | bytes 98312 | tf_op jit(solution)/shard_map/ppermute | solution.py:23
  64.8 6.1 %collective-permute-start.7 = (f32[64,128]{1,0:T(8,128)S(1)}, f32[64,128]{1,0:T(8,128)S(1)}, u32[]{:S(2)}, u32[]{:S(2)}) collective-permute-start(f32[64,128]{1,0:T(8,128)S(1)} %get-tuple-element.35.fresh), channel_id=1, source_target_pairs={{16,32},{32,16},{48,64},{64,48},{80,96},{96,80},{112,128},{128,112... | collective-permute-start | bytes 98312 | tf_op jit(solution)/shard_map/ppermute | solution.py:23
  71.8 8.2 %collective-permute-start.10 = (f32[64,128]{1,0:T(8,128)S(1)}, f32[64,128]{1,0:T(8,128)S(1)}, u32[]{:S(2)}, u32[]{:S(2)}) collective-permute-start(f32[64,128]{1,0:T(8,128)S(1)} %get-tuple-element.37.fresh), channel_id=1, source_target_pairs={{0,16},{16,0},{32,48},{48,32},{64,80},{80,64},{96,112},{112,96},{1... | collective-permute-start | bytes 98312 | tf_op jit(solution)/shard_map/ppermute | solution.py:23
  77.0 6.1 %collective-permute-start.9 = (f32[64,128]{1,0:T(8,128)S(1)}, f32[64,128]{1,0:T(8,128)S(1)}, u32[]{:S(2)}, u32[]{:S(2)}) collective-permute-start(f32[64,128]{1,0:T(8,128)S(1)} %get-tuple-element.37.fresh), channel_id=1, source_target_pairs={{16,32},{32,16},{48,64},{64,48},{80,96},{96,80},{112,128},{128,112... | collective-permute-start | bytes 98312 | tf_op jit(solution)/shard_map/ppermute | solution.py:23
  83.9 8.3 %collective-permute-start.12 = (f32[64,128]{1,0:T(8,128)S(1)}, f32[64,128]{1,0:T(8,128)S(1)}, u32[]{:S(2)}, u32[]{:S(2)}) collective-permute-start(f32[64,128]{1,0:T(8,128)S(1)} %get-tuple-element.39.fresh), channel_id=1, source_target_pairs={{0,16},{16,0},{32,48},{48,32},{64,80},{80,64},{96,112},{112,96},{1... | collective-permute-start | bytes 98312 | tf_op jit(solution)/shard_map/ppermute | solution.py:23
  89.2 6.1 %collective-permute-start.11 = (f32[64,128]{1,0:T(8,128)S(1)}, f32[64,128]{1,0:T(8,128)S(1)}, u32[]{:S(2)}, u32[]{:S(2)}) collective-permute-start(f32[64,128]{1,0:T(8,128)S(1)} %get-tuple-element.39.fresh), channel_id=1, source_target_pairs={{16,32},{32,16},{48,64},{64,48},{80,96},{96,80},{112,128},{128,112... | collective-permute-start | bytes 98312 | tf_op jit(solution)/shard_map/ppermute | solution.py:23
  96.1 8.2 %collective-permute-start.14 = (f32[64,128]{1,0:T(8,128)S(1)}, f32[64,128]{1,0:T(8,128)S(1)}, u32[]{:S(2)}, u32[]{:S(2)}) collective-permute-start(f32[64,128]{1,0:T(8,128)S(1)} %get-tuple-element.41.fresh), channel_id=1, source_target_pairs={{0,16},{16,0},{32,48},{48,32},{64,80},{80,64},{96,112},{112,96},{1... | collective-permute-start | bytes 98312 | tf_op jit(solution)/shard_map/ppermute | solution.py:23
  101.4 6.1 %collective-permute-start.13 = (f32[64,128]{1,0:T(8,128)S(1)}, f32[64,128]{1,0:T(8,128)S(1)}, u32[]{:S(2)}, u32[]{:S(2)}) collective-permute-start(f32[64,128]{1,0:T(8,128)S(1)} %get-tuple-element.41.fresh), channel_id=1, source_target_pairs={{16,32},{32,16},{48,64},{64,48},{80,96},{96,80},{112,128},{128,112... | collective-permute-start | bytes 98312 | tf_op jit(solution)/shard_map/ppermute | solution.py:23
  108.3 8.1 %collective-permute-start.16 = (f32[64,128]{1,0:T(8,128)S(1)}, f32[64,128]{1,0:T(8,128)S(1)}, u32[]{:S(2)}, u32[]{:S(2)}) collective-permute-start(f32[64,128]{1,0:T(8,128)S(1)} %get-tuple-element.43.fresh), channel_id=1, source_target_pairs={{0,16},{16,0},{32,48},{48,32},{64,80},{80,64},{96,112},{112,96},{1... | collective-permute-start | bytes 98312 | tf_op jit(solution)/shard_map/ppermute | solution.py:23
  113.5 6.1 %collective-permute-start.15 = (f32[64,128]{1,0:T(8,128)S(1)}, f32[64,128]{1,0:T(8,128)S(1)}, u32[]{:S(2)}, u32[]{:S(2)}) collective-permute-start(f32[64,128]{1,0:T(8,128)S(1)} %get-tuple-element.43.fresh), channel_id=1, source_target_pairs={{16,32},{32,16},{48,64},{64,48},{80,96},{96,80},{112,128},{128,112... | collective-permute-start | bytes 98312 | tf_op jit(solution)/shard_map/ppermute | solution.py:23
  120.7 24.8 %all-to-all-start = ((bf16[8,64,512]{2,1,0:T(8,128)(2,1)}), bf16[8,64,512]{2,1,0:T(8,128)(2,1)S(1)}, u32[]{:S(2)}, u32[]{:S(2)}) async-start(bf16[8,64,512]{2,1,0:T(8,128)(2,1)} %get-tuple-element.47), calls=%async_computation | async-start | bytes 1048576 | tf_op jit(solution)/shard_map/all_to_all | solution.py:229
  131.2 5.9 %collective-permute-start.17 = (f32[64,128]{1,0:T(8,128)S(1)}, f32[64,128]{1,0:T(8,128)S(1)}, u32[]{:S(2)}, u32[]{:S(2)}) collective-permute-start(f32[64,128]{1,0:T(8,128)S(1)} %get-tuple-element.48.edge), channel_id=1, source_target_pairs={{0,16},{16,32},{32,48},{48,64},{64,80},{80,96},{96,112},{112,128},... | collective-permute-start | bytes 98312 | tf_op jit(solution)/shard_map/ppermute | solution.py:14
  137.2 5.3 %collective-permute-start.18 = (bf16[64,512]{1,0:T(8,128)(2,1)S(1)}, bf16[64,512]{1,0:T(8,128)(2,1)S(1)}, u32[]{:S(2)}, u32[]{:S(2)}) collective-permute-start(bf16[64,512]{1,0:T(8,128)(2,1)S(1)} %shard_map.77.image), channel_id=1, source_target_pairs={{0,1},{1,0},{2,3},{3,2},{4,5},{5,4},{6,7},{7,6},{8,9},{9,8},{10,11... | collective-permute-start | bytes 196616 | tf_op jit(solution)/shard_map/ppermute | solution.py:23
  145.8 7.6 %collective-permute-start.19 = (f32[2,16,8,128]{3,2,1,0:T(8,128)S(1)}, f32[2,16,8,128]{3,2,1,0:T(8,128)S(1)}, u32[]{:S(2)}, u32[]{:S(2)}) collective-permute-start(f32[2,16,8,128]{3,2,1,0:T(8,128)S(1)} %get-tuple-element.51), channel_id=1, source_target_pairs={{0,16},{16,0},{32,48},{48,32},{64,80},{80,64},{96,112},{112,96},{1... | collective-permute-start | bytes 393224 | tf_op jit(solution)/shard_map/ppermute | solution.py:23
  153.4 5.0 %collective-permute-start.20 = (f32[16,8,128]{2,1,0:T(8,128)S(1)}, f32[16,8,128]{2,1,0:T(8,128)S(1)}, u32[]{:S(2)}, u32[]{:S(2)}) collective-permute-start(f32[16,8,128]{2,1,0:T(8,128)S(1)} %get-tuple-element.53), channel_id=1, source_target_pairs={{0,1},{1,0},{2,3},{3,2},{4,5},{5,4},{6,7},{7,6},{8,9},{9,8},{10,11... | collective-permute-start | bytes 196616 | tf_op jit(solution)/shard_map/ppermute | solution.py:23

commit v4 on v3

--- a/solution.py
+++ b/solution.py
@@ -58,11 +58,12 @@
     extended[:, width:] = inner.astype(jnp.bfloat16)
 
 
-def multiplied(extended, weights, begin, end):
+def multiplied(values, weights, begin, end, row=0):
     total = None
+    stop = row + values.shape[1]
     for cell in range(weights.shape[0]):
         part = jnp.dot(
-            extended[...], weights[cell, :, begin:end], preferred_element_type=jnp.float32
+            values, weights[cell, row:stop, begin:end], preferred_element_type=jnp.float32
         )
         total = part if total is None else total + part
     return total
@@ -74,43 +75,44 @@
     edge[...] = values
     inner[...] = start[:, shared:]
     fill(extended, values, inner[...])
-    product = multiplied(extended, weights, 0, 2 * shared)
+    product = multiplied(extended[...], weights, 0, 2 * shared)
     upcoming[...] = coef[0] * product + jnp.where(in_own(values), coef[1] * values, 0.0)
 
 
-def edge_body(flag, coef, fresh, link, chip, inner, before, weights, edge, upcoming, extended):
+def edge_body(flag, coef, fresh, link, chip, ahead, before, weights, edge, upcoming):
     values = completed(flag, fresh[...], link[...], chip[...])
     edge[...] = values
-    fill(extended, values, inner[...])
-    product = multiplied(extended, weights, 0, values.shape[1])
+    width = values.shape[1]
+    product = ahead[...] + multiplied(values.astype(jnp.bfloat16), weights, 0, width)
     kept = coef[1] * values + coef[2] * before[...]
     upcoming[...] = coef[0] * product + jnp.where(in_own(values), kept, 0.0)
 
 
 def inner_body(coef, edge, inner, weights, *rest):
-    before, upcoming, extended = rest if len(rest) == 3 else (None, *rest)
+    before, upcoming, ahead, extended = rest if len(rest) == 4 else (None, *rest)
+    width = edge.shape[1]
     fill(extended, edge[...], inner[...])
-    product = multiplied(extended, weights, edge.shape[1], weights.shape[2])
+    product = multiplied(extended[...], weights, width, weights.shape[2])
     fresh = coef[0] * product + coef[1] * inner[...]
     if before is not None:
         fresh = fresh + coef[2] * before[...]
     upcoming[...] = fresh
-
-
-def last_edge_body(flag, fresh, link, chip, inner, weights, edge, low, product, extended):
+    ahead[...] = multiplied(fresh.astype(jnp.bfloat16), weights, 0, width, width)
+
+
+def last_edge_body(flag, fresh, link, chip, inner, ahead, weights, edge, low, product):
     values = completed(flag, fresh[...], link[...], chip[...])
     edge[...] = values
-    fill(extended, values, inner[...])
-    shared = values.shape[1] // 2
-    rounded = jnp.concatenate([inner[...], values[:, :shared]], axis=1).astype(jnp.bfloat16)
+    width = values.shape[1]
+    rounded = jnp.concatenate([inner[...], values[:, : width // 2]], axis=1).astype(jnp.bfloat16)
     low[...] = jnp.broadcast_to(rounded[None], low.shape)
-    product[...] = multiplied(extended, weights, 0, values.shape[1])
+    product[...] = ahead[...] + multiplied(values.astype(jnp.bfloat16), weights, 0, width)
 
 
 def last_inner_body(edge, inner, weights, filtered, product, extended):
     shared = edge.shape[1] // 2
     fill(extended, edge[...], inner[...])
-    product[...] = multiplied(extended, weights, edge.shape[1], weights.shape[2])
+    product[...] = multiplied(extended[...], weights, edge.shape[1], weights.shape[2])
     filtered[...] = jnp.concatenate([edge[:, :shared], inner[...]], axis=1)
 
 
@@ -194,10 +196,10 @@
     core = pltpu.VMEM((states, owned - shared), f32)
     scratch = [pltpu.VMEM((states, extent), bf16)]
     first = kernel(first_body, 1, (rim, core, rim), scratch)
-    edge_step = kernel(edge_body, 2, (rim, rim), scratch)
-    inner_step = kernel(inner_body, 1, core, scratch)
+    edge_step = kernel(edge_body, 2, (rim, rim), [])
+    inner_step = kernel(inner_body, 1, (core, rim), scratch)
     lows = pltpu.VMEM((line, states, owned), bf16)
-    last_edge = kernel(last_edge_body, 1, (rim, lows, rim), scratch)
+    last_edge = kernel(last_edge_body, 1, (rim, lows, rim), [])
     out = jax.ShapeDtypeStruct((states, owned), f32)
     last_inner = kernel(last_inner_body, 0, (out, core), scratch)
 
@@ -218,13 +220,13 @@
     before = ()
     for number, coef in enumerate(coefs):
         link, chip = exchanged(fresh)
-        upcoming = inner_step(coef, edge, inner, weights, *before)
+        upcoming, ahead = inner_step(coef, edge, inner, weights, *before)
         before, inner = (inner,), upcoming
         if number + 1 < len(coefs):
             edge, fresh = edge_step(
-                flag, coefs[number + 1], fresh, link, chip, inner, edge, weights
+                flag, coefs[number + 1], fresh, link, chip, ahead, edge, weights
             )
-    edge, low, edge_product = last_edge(flag, fresh, link, chip, inner, weights)
+    edge, low, edge_product = last_edge(flag, fresh, link, chip, inner, ahead, weights)
     incoming = passed_along(edge_product, "cell", 1)
     lows = lax.all_to_all(low, "state", 0, 0, axis_index_groups=alternate(peers), tiled=True)
     filtered, inner_product = last_inner(edge, inner, weights)

time: 177 us -> 176 us (level)
  no operation moved by 1% of the time
where the time goes in v4:
time: 176 us; the launch traced here: 175 us
  starting transfers between devices  94.1 us (53%)
  waiting for transfers between devices  36.7 us (21%)
  Pallas kernels  16.9 us (10%)
  blocking collectives  16.4 us (9%)
  between operations  5.06 us (3%)
  local copies, waits for them, and re-layouts  2.94 us (2%)
  matrix products  2.5 us (1%)
    ppermute x19, starting transfers between devices, swapped(): return lax.ppermute(value, axis, pairs)  65.5 us
    ppermute x19, waiting for transfers between devices, swapped(): return lax.ppermute(value, axis, pairs)  30.9 us
    ppermute x2, starting transfers between devices, passed_along(): return lax.ppermute(value, axis, pairs)  18.1 us
    pallas_call x22, Pallas kernels, run(): pl.pallas_call(body, in_specs=in_specs, out_specs=outs if single else (ou...  16.9 us
    all_to_all x1, blocking collectives, per_device(): lax.all_to_all(pieces, 'cell', 0, 0, axis_index_groups=alternate(count),...  16.4 us
    all_to_all x1, starting transfers between devices, per_device(): lax.all_to_all(low, 'state', 0, 0, axis_index_groups=alternate(peers), ti...  10.5 us
  transfers between devices with their start and end apart: 22, of which 13 were waited for; matrix products, arithmetic and copies ran while one was open for 3% of the time, Pallas kernels for 5%

profile of v4, /device:TPU:1, one launch (start us, length us, event | category | flops | bytes accessed | tf_op | source)
XLA Modules:
  0.0 175.2 jit_solution(3032707456511618039)
XLA Ops:
  0.6 0.8 slice.19
  1.5 16.0 %collective-permute-start = (bf16[64,64]{1,0:T(8,128)(2,1)S(1)}, bf16[64,64]{1,0:T(8,128)(2,1)S(1)}, u32[]{:S(2)}, u32[]{:S(2)}) collective-permute-start(bf16[64,64]{1,0:T(8,128)(2,1)S(1)} %slice.19), channel_id=1, source_target_pairs={{0,1008},{16,0},{32,16},{48,32},{64,48},{80,64},{96,80},{112,96},{... | collective-permute-start | bytes 24584 | tf_op jit(solution)/shard_map/ppermute | solution.py:14
  17.5 1.4 fusion.12
  22.3 2.5 %convolution_convert_fusion.weights = bf16[2,576,576]{2,1,0:T(8,128)(2,1)S(1)} fusion(s32[576]{0:T(1024)S(1)} %get-tuple-element.89, s32[576]{0:T(1024)S(1)} %get-tuple-element.90, s32[2,343]{1,0:T(2,128)} %param.5, pred[576]{0:T(1024)(128)(4,1)S(1)} %get-tuple-element.91, pred[576]{0:T(1024)(128)(4,1)S(1)} %get-tuple-element.92, ...), kind=kOutput, calls=%fused_computation.1 | convolution fusion | flops 729689472 | bytes 1806204 | tf_op jit(solution)/shard_map/cai,cak->cik/dot_general | solution.py:34
  24.8 0.1 pad_maximum_fusion.7.coef
  25.1 0.8 shard_map.59
  25.9 1.9 %collective-permute-start.2 = (f32[64,128]{1,0:T(8,128)S(1)}, f32[64,128]{1,0:T(8,128)S(1)}, u32[]{:S(2)}, u32[]{:S(2)}) collective-permute-start(f32[64,128]{1,0:T(8,128)S(1)} %get-tuple-element.44.fresh), channel_id=1, source_target_pairs={{0,16},{16,0},{32,48},{48,32},{64,80},{80,64},{96,112},{112,96},{1... | collective-permute-start | bytes 98312 | tf_op jit(solution)/shard_map/ppermute | solution.py:23
  27.8 1.9 %collective-permute-start.1 = (f32[64,128]{1,0:T(8,128)S(1)}, f32[64,128]{1,0:T(8,128)S(1)}, u32[]{:S(2)}, u32[]{:S(2)}) collective-permute-start(f32[64,128]{1,0:T(8,128)S(1)} %get-tuple-element.44.fresh), channel_id=1, source_target_pairs={{16,32},{32,16},{48,64},{64,48},{80,96},{96,80},{112,128},{128,112... | collective-permute-start | bytes 98312 | tf_op jit(solution)/shard_map/ppermute | solution.py:23
  29.8 0.1 pad_maximum_fusion.6.coef
  29.9 1.0 shard_map.60
  31.0 3.0 %collective-permute-done.1.link = f32[64,128]{1,0:T(8,128)S(1)} collective-permute-done((f32[64,128]{1,0:T(8,128)S(1)}, f32[64,128]{1,0:T(8,128)S(1)}, u32[]{:S(2)}, u32[]{:S(2)}) %collective-permute-start.1) | collective-permute-done | bytes 32800 | tf_op jit(solution)/shard_map/ppermute | solution.py:23
  34.0 0.7 shard_map.61
  34.7 5.7 %collective-permute-start.4 = (f32[64,128]{1,0:T(8,128)S(1)}, f32[64,128]{1,0:T(8,128)S(1)}, u32[]{:S(2)}, u32[]{:S(2)}) collective-permute-start(f32[64,128]{1,0:T(8,128)S(1)} %get-tuple-element.48.fresh), channel_id=1, source_target_pairs={{0,16},{16,0},{32,48},{48,32},{64,80},{80,64},{96,112},{112,96},{1... | collective-permute-start | bytes 98312 | tf_op jit(solution)/shard_map/ppermute | solution.py:23
  40.4 1.9 %collective-permute-start.3 = (f32[64,128]{1,0:T(8,128)S(1)}, f32[64,128]{1,0:T(8,128)S(1)}, u32[]{:S(2)}, u32[]{:S(2)}) collective-permute-start(f32[64,128]{1,0:T(8,128)S(1)} %get-tuple-element.48.fresh), channel_id=1, source_target_pairs={{16,32},{32,16},{48,64},{64,48},{80,96},{96,80},{112,128},{128,112... | collective-permute-start | bytes 98312 | tf_op jit(solution)/shard_map/ppermute | solution.py:23
  42.4 0.1 pad_maximum_fusion.5.coef
  42.5 1.1 shard_map.62
  43.6 3.0 %collective-permute-done.3.link = f32[64,128]{1,0:T(8,128)S(1)} collective-permute-done((f32[64,128]{1,0:T(8,128)S(1)}, f32[64,128]{1,0:T(8,128)S(1)}, u32[]{:S(2)}, u32[]{:S(2)}) %collective-permute-start.3) | collective-permute-done | bytes 32800 | tf_op jit(solution)/shard_map/ppermute | solution.py:23
  46.6 0.7 shard_map.63
  47.3 5.2 %collective-permute-start.6 = (f32[64,128]{1,0:T(8,128)S(1)}, f32[64,128]{1,0:T(8,128)S(1)}, u32[]{:S(2)}, u32[]{:S(2)}) collective-permute-start(f32[64,128]{1,0:T(8,128)S(1)} %get-tuple-element.52.fresh), channel_id=1, source_target_pairs={{0,16},{16,0},{32,48},{48,32},{64,80},{80,64},{96,112},{112,96},{1... | collective-permute-start | bytes 98312 | tf_op jit(solution)/shard_map/ppermute | solution.py:23
  52.6 1.9 %collective-permute-start.5 = (f32[64,128]{1,0:T(8,128)S(1)}, f32[64,128]{1,0:T(8,128)S(1)}, u32[]{:S(2)}, u32[]{:S(2)}) collective-permute-start(f32[64,128]{1,0:T(8,128)S(1)} %get-tuple-element.52.fresh), channel_id=1, source_target_pairs={{16,32},{32,16},{48,64},{64,48},{80,96},{96,80},{112,128},{128,112... | collective-permute-start | bytes 98312 | tf_op jit(solution)/shard_map/ppermute | solution.py:23
  54.7 1.0 shard_map.64
  55.7 3.0 %collective-permute-done.5.link = f32[64,128]{1,0:T(8,128)S(1)} collective-permute-done((f32[64,128]{1,0:T(8,128)S(1)}, f32[64,128]{1,0:T(8,128)S(1)}, u32[]{:S(2)}, u32[]{:S(2)}) %collective-permute-start.5) | collective-permute-done | bytes 32800 | tf_op jit(solution)/shard_map/ppermute | solution.py:23
  58.7 0.7 shard_map.65
  59.5 5.2 %collective-permute-start.8 = (f32[64,128]{1,0:T(8,128)S(1)}, f32[64,128]{1,0:T(8,128)S(1)}, u32[]{:S(2)}, u32[]{:S(2)}) collective-permute-start(f32[64,128]{1,0:T(8,128)S(1)} %get-tuple-element.56.fresh), channel_id=1, source_target_pairs={{0,16},{16,0},{32,48},{48,32},{64,80},{80,64},{96,112},{112,96},{1... | collective-permute-start | bytes 98312 | tf_op jit(solution)/shard_map/ppermute | solution.py:23
  64.7 1.9 %collective-permute-start.7 = (f32[64,128]{1,0:T(8,128)S(1)}, f32[64,128]{1,0:T(8,128)S(1)}, u32[]{:S(2)}, u32[]{:S(2)}) collective-permute-start(f32[64,128]{1,0:T(8,128)S(1)} %get-tuple-element.56.fresh), channel_id=1, source_target_pairs={{16,32},{32,16},{48,64},{64,48},{80,96},{96,80},{112,128},{128,112... | collective-permute-start | bytes 98312 | tf_op jit(solution)/shard_map/ppermute | solution.py:23
  66.8 1.1 shard_map.66
  67.9 3.0 %collective-permute-done.7.link = f32[64,128]{1,0:T(8,128)S(1)} collective-permute-done((f32[64,128]{1,0:T(8,128)S(1)}, f32[64,128]{1,0:T(8,128)S(1)}, u32[]{:S(2)}, u32[]{:S(2)}) %collective-permute-start.7) | collective-permute-done | bytes 32800 | tf_op jit(solution)/shard_map/ppermute | solution.py:23
  70.8 0.7 shard_map.67
  71.6 5.2 %collective-permute-start.10 = (f32[64,128]{1,0:T(8,128)S(1)}, f32[64,128]{1,0:T(8,128)S(1)}, u32[]{:S(2)}, u32[]{:S(2)}) collective-permute-start(f32[64,128]{1,0:T(8,128)S(1)} %get-tuple-element.60.fresh), channel_id=1, source_target_pairs={{0,16},{16,0},{32,48},{48,32},{64,80},{80,64},{96,112},{112,96},{1... | collective-permute-start | bytes 98312 | tf_op jit(solution)/shard_map/ppermute | solution.py:23
  76.8 1.9 %collective-permute-start.9 = (f32[64,128]{1,0:T(8,128)S(1)}, f32[64,128]{1,0:T(8,128)S(1)}, u32[]{:S(2)}, u32[]{:S(2)}) collective-permute-start(f32[64,128]{1,0:T(8,128)S(1)} %get-tuple-element.60.fresh), channel_id=1, source_target_pairs={{16,32},{32,16},{48,64},{64,48},{80,96},{96,80},{112,128},{128,112... | collective-permute-start | bytes 98312 | tf_op jit(solution)/shard_map/ppermute | solution.py:23
  78.9 1.1 shard_map.68
  80.0 3.0 %collective-permute-done.9.link = f32[64,128]{1,0:T(8,128)S(1)} collective-permute-done((f32[64,128]{1,0:T(8,128)S(1)}, f32[64,128]{1,0:T(8,128)S(1)}, u32[]{:S(2)}, u32[]{:S(2)}) %collective-permute-start.9) | collective-permute-done | bytes 32800 | tf_op jit(solution)/shard_map/ppermute | solution.py:23
  83.0 0.7 shard_map.69
  83.7 5.2 %collective-permute-start.12 = (f32[64,128]{1,0:T(8,128)S(1)}, f32[64,128]{1,0:T(8,128)S(1)}, u32[]{:S(2)}, u32[]{:S(2)}) collective-permute-start(f32[64,128]{1,0:T(8,128)S(1)} %get-tuple-element.64.fresh), channel_id=1, source_target_pairs={{0,16},{16,0},{32,48},{48,32},{64,80},{80,64},{96,112},{112,96},{1... | collective-permute-start | bytes 98312 | tf_op jit(solution)/shard_map/ppermute | solution.py:23
  89.0 1.9 %collective-permute-start.11 = (f32[64,128]{1,0:T(8,128)S(1)}, f32[64,128]{1,0:T(8,128)S(1)}, u32[]{:S(2)}, u32[]{:S(2)}) collective-permute-start(f32[64,128]{1,0:T(8,128)S(1)} %get-tuple-element.64.fresh), channel_id=1, source_target_pairs={{16,32},{32,16},{48,64},{64,48},{80,96},{96,80},{112,128},{128,112... | collective-permute-start | bytes 98312 | tf_op jit(solution)/shard_map/ppermute | solution.py:23
  91.1 1.0 shard_map.70
  92.1 3.0 %collective-permute-done.11.link = f32[64,128]{1,0:T(8,128)S(1)} collective-permute-done((f32[64,128]{1,0:T(8,128)S(1)}, f32[64,128]{1,0:T(8,128)S(1)}, u32[]{:S(2)}, u32[]{:S(2)}) %collective-permute-start.11) | collective-permute-done | bytes 32800 | tf_op jit(solution)/shard_map/ppermute | solution.py:23
  95.1 0.7 shard_map.71
  95.8 5.2 %collective-permute-start.14 = (f32[64,128]{1,0:T(8,128)S(1)}, f32[64,128]{1,0:T(8,128)S(1)}, u32[]{:S(2)}, u32[]{:S(2)}) collective-permute-start(f32[64,128]{1,0:T(8,128)S(1)} %get-tuple-element.68.fresh), channel_id=1, source_target_pairs={{0,16},{16,0},{32,48},{48,32},{64,80},{80,64},{96,112},{112,96},{1... | collective-permute-start | bytes 98312 | tf_op jit(solution)/shard_map/ppermute | solution.py:23
  101.1 1.9 %collective-permute-start.13 = (f32[64,128]{1,0:T(8,128)S(1)}, f32[64,128]{1,0:T(8,128)S(1)}, u32[]{:S(2)}, u32[]{:S(2)}) collective-permute-start(f32[64,128]{1,0:T(8,128)S(1)} %get-tuple-element.68.fresh), channel_id=1, source_target_pairs={{16,32},{32,16},{48,64},{64,48},{80,96},{96,80},{112,128},{128,112... | collective-permute-start | bytes 98312 | tf_op jit(solution)/shard_map/ppermute | solution.py:23
  103.1 1.1 shard_map.72
  104.2 3.1 %collective-permute-done.13.link = f32[64,128]{1,0:T(8,128)S(1)} collective-permute-done((f32[64,128]{1,0:T(8,128)S(1)}, f32[64,128]{1,0:T(8,128)S(1)}, u32[]{:S(2)}, u32[]{:S(2)}) %collective-permute-start.13) | collective-permute-done | bytes 32800 | tf_op jit(solution)/shard_map/ppermute | solution.py:23
  107.2 0.7 shard_map.73
  108.0 5.2 %collective-permute-start.16 = (f32[64,128]{1,0:T(8,128)S(1)}, f32[64,128]{1,0:T(8,128)S(1)}, u32[]{:S(2)}, u32[]{:S(2)}) collective-permute-start(f32[64,128]{1,0:T(8,128)S(1)} %get-tuple-element.72.fresh), channel_id=1, source_target_pairs={{0,16},{16,0},{32,48},{48,32},{64,80},{80,64},{96,112},{112,96},{1... | collective-permute-start | bytes 98312 | tf_op jit(solution)/shard_map/ppermute | solution.py:23
  113.2 1.9 %collective-permute-start.15 = (f32[64,128]{1,0:T(8,128)S(1)}, f32[64,128]{1,0:T(8,128)S(1)}, u32[]{:S(2)}, u32[]{:S(2)}) collective-permute-start(f32[64,128]{1,0:T(8,128)S(1)} %get-tuple-element.72.fresh), channel_id=1, source_target_pairs={{16,32},{32,16},{48,64},{64,48},{80,96},{96,80},{112,128},{128,112... | collective-permute-start | bytes 98312 | tf_op jit(solution)/shard_map/ppermute | solution.py:23
  115.1 1.1 shard_map.74
  116.2 3.1 %collective-permute-done.15.link = f32[64,128]{1,0:T(8,128)S(1)} collective-permute-done((f32[64,128]{1,0:T(8,128)S(1)}, f32[64,128]{1,0:T(8,128)S(1)}, u32[]{:S(2)}, u32[]{:S(2)}) %collective-permute-start.15) | collective-permute-done | bytes 32800 | tf_op jit(solution)/shard_map/ppermute | solution.py:23
  119.4 1.0 shard_map.75
  120.3 10.5 %all-to-all-start = ((bf16[8,64,512]{2,1,0:T(8,128)(2,1)}), bf16[8,64,512]{2,1,0:T(8,128)(2,1)S(1)}, u32[]{:S(2)}, u32[]{:S(2)}) async-start(bf16[8,64,512]{2,1,0:T(8,128)(2,1)} %get-tuple-element.79), calls=%async_computation | async-start | bytes 1048576 | tf_op jit(solution)/shard_map/all_to_all | solution.py:231
  130.8 2.0 %collective-permute-start.17 = (f32[64,128]{1,0:T(8,128)S(1)}, f32[64,128]{1,0:T(8,128)S(1)}, u32[]{:S(2)}, u32[]{:S(2)}) collective-permute-start(f32[64,128]{1,0:T(8,128)S(1)} %get-tuple-element.80.edge), channel_id=1, source_target_pairs={{0,16},{16,32},{32,48},{48,64},{64,80},{80,96},{96,112},{112,128},... | collective-permute-start | bytes 98312 | tf_op jit(solution)/shard_map/ppermute | solution.py:14
  132.9 0.9 shard_map.76
  133.8 2.9 %collective-permute-done.17.incoming = f32[64,128]{1,0:T(8,128)S(1)} collective-permute-done((f32[64,128]{1,0:T(8,128)S(1)}, f32[64,128]{1,0:T(8,128)S(1)}, u32[]{:S(2)}, u32[]{:S(2)}) %collective-permute-start.17) | collective-permute-done | bytes 32800 | tf_op jit(solution)/shard_map/ppermute | solution.py:14
  136.7 0.1 shard_map.77.image
  136.8 2.2 %collective-permute-start.18 = (bf16[64,512]{1,0:T(8,128)(2,1)S(1)}, bf16[64,512]{1,0:T(8,128)(2,1)S(1)}, u32[]{:S(2)}, u32[]{:S(2)}) collective-permute-start(bf16[64,512]{1,0:T(8,128)(2,1)S(1)} %shard_map.77.image), channel_id=1, source_target_pairs={{0,1},{1,0},{2,3},{3,2},{4,5},{5,4},{6,7},{7,6},{8,9},{9,8},{10,11... | collective-permute-start | bytes 196616 | tf_op jit(solution)/shard_map/ppermute | solution.py:23
  139.0 3.1 %collective-permute-done.18.neighbour = bf16[64,512]{1,0:T(8,128)(2,1)S(1)} collective-permute-done((bf16[64,512]{1,0:T(8,128)(2,1)S(1)}, bf16[64,512]{1,0:T(8,128)(2,1)S(1)}, u32[]{:S(2)}, u32[]{:S(2)}) %collective-permute-start.18) | collective-permute-done | bytes 65568 | tf_op jit(solution)/shard_map/ppermute | solution.py:23
  142.1 3.0 %all-to-all-done = bf16[8,64,512]{2,1,0:T(8,128)(2,1)S(1)} async-done(((bf16[8,64,512]{2,1,0:T(8,128)(2,1)}), bf16[8,64,512]{2,1,0:T(8,128)(2,1)S(1)}, u32[]{:S(2)}, u32[]{:S(2)}) %all-to-all-start) | async-done | bytes 524320 | tf_op jit(solution)/shard_map/all_to_all | solution.py:231
  145.1 0.4 shard_map.78
  145.5 6.6 %collective-permute-start.19 = (f32[2,16,8,128]{3,2,1,0:T(8,128)S(1)}, f32[2,16,8,128]{3,2,1,0:T(8,128)S(1)}, u32[]{:S(2)}, u32[]{:S(2)}) collective-permute-start(f32[2,16,8,128]{3,2,1,0:T(8,128)S(1)} %get-tuple-element.83), channel_id=1, source_target_pairs={{0,16},{16,0},{32,48},{48,32},{64,80},{80,64},{96,112},{112,96},{1... | collective-permute-start | bytes 393224 | tf_op jit(solution)/shard_map/ppermute | solution.py:23
  152.1 1.0 collective-permute-done.19.received
  153.1 2.2 %collective-permute-start.20 = (f32[16,8,128]{2,1,0:T(8,128)S(1)}, f32[16,8,128]{2,1,0:T(8,128)S(1)}, u32[]{:S(2)}, u32[]{:S(2)}) collective-permute-start(f32[16,8,128]{2,1,0:T(8,128)S(1)} %get-tuple-element.85), channel_id=1, source_target_pairs={{0,1},{1,0},{2,3},{3,2},{4,5},{5,4},{6,7},{7,6},{8,9},{9,8},{10,11... | collective-permute-start | bytes 196616 | tf_op jit(solution)/shard_map/ppermute | solution.py:23
  155.3 2.8 %collective-permute-done.20.received = f32[16,8,128]{2,1,0:T(8,128)S(1)} collective-permute-done((f32[16,8,128]{2,1,0:T(8,128)S(1)}, f32[16,8,128]{2,1,0:T(8,128)S(1)}, u32[]{:S(2)}, u32[]{:S(2)}) %collective-permute-start.20) | collective-permute-done | bytes 65568 | tf_op jit(solution)/shard_map/ppermute | solution.py:23
  158.1 16.4 %all_to_all.10 = f32[32,8,128]{2,1,0:T(8,128)S(1)} all-to-all(f32[32,8,128]{2,1,0:T(8,128)S(1)} %bitcast.35), channel_id=1, replica_groups={{0,32,64,96,128,160,192,224,256,288,320,352,384,416,448,480,512,544,576..., dimensions={0} | all-to-all | bytes 262144 | tf_op jit(solution)/shard_map/all_to_all | solution.py:251
  174.5 0.1 reduce_sum.12
  174.6 0.6 copy.12
  (23 shorter events, 0.5 us)
Async XLA Ops:
  0.6 21.6 %copy-start = (bf16[2,343,343]{2,0,1:T(2,128)(2,1)S(1)}, bf16[2,343,343]{2,0,1:T(2,128)(2,1)}, u32[]{:S(2)}) copy-start(bf16[2,343,343]{2,0,1:T(2,128)(2,1)} %param.6) | copy-start | bytes 1411792
  1.5 23.6 %collective-permute-start = (bf16[64,64]{1,0:T(8,128)(2,1)S(1)}, bf16[64,64]{1,0:T(8,128)(2,1)S(1)}, u32[]{:S(2)}, u32[]{:S(2)}) collective-permute-start(bf16[64,64]{1,0:T(8,128)(2,1)S(1)} %slice.19), channel_id=1, source_target_pairs={{0,1008},{16,0},{32,16},{48,32},{64,48},{80,64},{96,80},{112,96},{... | collective-permute-start | bytes 24584 | tf_op jit(solution)/shard_map/ppermute | solution.py:14
  22.3 2.8 %copy-start.1 = (f32[64,512]{1,0:T(8,128)S(1)}, f32[64,512]{1,0:T(8,128)}, u32[]{:S(2)}) copy-start(f32[64,512]{1,0:T(8,128)} %start.1) | copy-start | bytes 393220
  25.9 5.1 %collective-permute-start.2 = (f32[64,128]{1,0:T(8,128)S(1)}, f32[64,128]{1,0:T(8,128)S(1)}, u32[]{:S(2)}, u32[]{:S(2)}) collective-permute-start(f32[64,128]{1,0:T(8,128)S(1)} %get-tuple-element.44.fresh), channel_id=1, source_target_pairs={{0,16},{16,0},{32,48},{48,32},{64,80},{80,64},{96,112},{112,96},{1... | collective-permute-start | bytes 98312 | tf_op jit(solution)/shard_map/ppermute | solution.py:23
  27.8 6.1 %collective-permute-start.1 = (f32[64,128]{1,0:T(8,128)S(1)}, f32[64,128]{1,0:T(8,128)S(1)}, u32[]{:S(2)}, u32[]{:S(2)}) collective-permute-start(f32[64,128]{1,0:T(8,128)S(1)} %get-tuple-element.44.fresh), channel_id=1, source_target_pairs={{16,32},{32,16},{48,64},{64,48},{80,96},{96,80},{112,128},{128,112... | collective-permute-start | bytes 98312 | tf_op jit(solution)/shard_map/ppermute | solution.py:23
  34.7 8.9 %collective-permute-start.4 = (f32[64,128]{1,0:T(8,128)S(1)}, f32[64,128]{1,0:T(8,128)S(1)}, u32[]{:S(2)}, u32[]{:S(2)}) collective-permute-start(f32[64,128]{1,0:T(8,128)S(1)} %get-tuple-element.48.fresh), channel_id=1, source_target_pairs={{0,16},{16,0},{32,48},{48,32},{64,80},{80,64},{96,112},{112,96},{1... | collective-permute-start | bytes 98312 | tf_op jit(solution)/shard_map/ppermute | solution.py:23
  40.4 6.1 %collective-permute-start.3 = (f32[64,128]{1,0:T(8,128)S(1)}, f32[64,128]{1,0:T(8,128)S(1)}, u32[]{:S(2)}, u32[]{:S(2)}) collective-permute-start(f32[64,128]{1,0:T(8,128)S(1)} %get-tuple-element.48.fresh), channel_id=1, source_target_pairs={{16,32},{32,16},{48,64},{64,48},{80,96},{96,80},{112,128},{128,112... | collective-permute-start | bytes 98312 | tf_op jit(solution)/shard_map/ppermute | solution.py:23
  47.3 8.4 %collective-permute-start.6 = (f32[64,128]{1,0:T(8,128)S(1)}, f32[64,128]{1,0:T(8,128)S(1)}, u32[]{:S(2)}, u32[]{:S(2)}) collective-permute-start(f32[64,128]{1,0:T(8,128)S(1)} %get-tuple-element.52.fresh), channel_id=1, source_target_pairs={{0,16},{16,0},{32,48},{48,32},{64,80},{80,64},{96,112},{112,96},{1... | collective-permute-start | bytes 98312 | tf_op jit(solution)/shard_map/ppermute | solution.py:23
  52.6 6.1 %collective-permute-start.5 = (f32[64,128]{1,0:T(8,128)S(1)}, f32[64,128]{1,0:T(8,128)S(1)}, u32[]{:S(2)}, u32[]{:S(2)}) collective-permute-start(f32[64,128]{1,0:T(8,128)S(1)} %get-tuple-element.52.fresh), channel_id=1, source_target_pairs={{16,32},{32,16},{48,64},{64,48},{80,96},{96,80},{112,128},{128,112... | collective-permute-start | bytes 98312 | tf_op jit(solution)/shard_map/ppermute | solution.py:23
  59.5 8.4 %collective-permute-start.8 = (f32[64,128]{1,0:T(8,128)S(1)}, f32[64,128]{1,0:T(8,128)S(1)}, u32[]{:S(2)}, u32[]{:S(2)}) collective-permute-start(f32[64,128]{1,0:T(8,128)S(1)} %get-tuple-element.56.fresh), channel_id=1, source_target_pairs={{0,16},{16,0},{32,48},{48,32},{64,80},{80,64},{96,112},{112,96},{1... | collective-permute-start | bytes 98312 | tf_op jit(solution)/shard_map/ppermute | solution.py:23
  64.7 6.1 %collective-permute-start.7 = (f32[64,128]{1,0:T(8,128)S(1)}, f32[64,128]{1,0:T(8,128)S(1)}, u32[]{:S(2)}, u32[]{:S(2)}) collective-permute-start(f32[64,128]{1,0:T(8,128)S(1)} %get-tuple-element.56.fresh), channel_id=1, source_target_pairs={{16,32},{32,16},{48,64},{64,48},{80,96},{96,80},{112,128},{128,112... | collective-permute-start | bytes 98312 | tf_op jit(solution)/shard_map/ppermute | solution.py:23
  71.6 8.4 %collective-permute-start.10 = (f32[64,128]{1,0:T(8,128)S(1)}, f32[64,128]{1,0:T(8,128)S(1)}, u32[]{:S(2)}, u32[]{:S(2)}) collective-permute-start(f32[64,128]{1,0:T(8,128)S(1)} %get-tuple-element.60.fresh), channel_id=1, source_target_pairs={{0,16},{16,0},{32,48},{48,32},{64,80},{80,64},{96,112},{112,96},{1... | collective-permute-start | bytes 98312 | tf_op jit(solution)/shard_map/ppermute | solution.py:23
  76.8 6.1 %collective-permute-start.9 = (f32[64,128]{1,0:T(8,128)S(1)}, f32[64,128]{1,0:T(8,128)S(1)}, u32[]{:S(2)}, u32[]{:S(2)}) collective-permute-start(f32[64,128]{1,0:T(8,128)S(1)} %get-tuple-element.60.fresh), channel_id=1, source_target_pairs={{16,32},{32,16},{48,64},{64,48},{80,96},{96,80},{112,128},{128,112... | collective-permute-start | bytes 98312 | tf_op jit(solution)/shard_map/ppermute | solution.py:23
  83.7 8.4 %collective-permute-start.12 = (f32[64,128]{1,0:T(8,128)S(1)}, f32[64,128]{1,0:T(8,128)S(1)}, u32[]{:S(2)}, u32[]{:S(2)}) collective-permute-start(f32[64,128]{1,0:T(8,128)S(1)} %get-tuple-element.64.fresh), channel_id=1, source_target_pairs={{0,16},{16,0},{32,48},{48,32},{64,80},{80,64},{96,112},{112,96},{1... | collective-permute-start | bytes 98312 | tf_op jit(solution)/shard_map/ppermute | solution.py:23
  89.0 6.1 %collective-permute-start.11 = (f32[64,128]{1,0:T(8,128)S(1)}, f32[64,128]{1,0:T(8,128)S(1)}, u32[]{:S(2)}, u32[]{:S(2)}) collective-permute-start(f32[64,128]{1,0:T(8,128)S(1)} %get-tuple-element.64.fresh), channel_id=1, source_target_pairs={{16,32},{32,16},{48,64},{64,48},{80,96},{96,80},{112,128},{128,112... | collective-permute-start | bytes 98312 | tf_op jit(solution)/shard_map/ppermute | solution.py:23
  95.8 8.3 %collective-permute-start.14 = (f32[64,128]{1,0:T(8,128)S(1)}, f32[64,128]{1,0:T(8,128)S(1)}, u32[]{:S(2)}, u32[]{:S(2)}) collective-permute-start(f32[64,128]{1,0:T(8,128)S(1)} %get-tuple-element.68.fresh), channel_id=1, source_target_pairs={{0,16},{16,0},{32,48},{48,32},{64,80},{80,64},{96,112},{112,96},{1... | collective-permute-start | bytes 98312 | tf_op jit(solution)/shard_map/ppermute | solution.py:23
  101.1 6.1 %collective-permute-start.13 = (f32[64,128]{1,0:T(8,128)S(1)}, f32[64,128]{1,0:T(8,128)S(1)}, u32[]{:S(2)}, u32[]{:S(2)}) collective-permute-start(f32[64,128]{1,0:T(8,128)S(1)} %get-tuple-element.68.fresh), channel_id=1, source_target_pairs={{16,32},{32,16},{48,64},{64,48},{80,96},{96,80},{112,128},{128,112... | collective-permute-start | bytes 98312 | tf_op jit(solution)/shard_map/ppermute | solution.py:23
  108.0 8.2 %collective-permute-start.16 = (f32[64,128]{1,0:T(8,128)S(1)}, f32[64,128]{1,0:T(8,128)S(1)}, u32[]{:S(2)}, u32[]{:S(2)}) collective-permute-start(f32[64,128]{1,0:T(8,128)S(1)} %get-tuple-element.72.fresh), channel_id=1, source_target_pairs={{0,16},{16,0},{32,48},{48,32},{64,80},{80,64},{96,112},{112,96},{1... | collective-permute-start | bytes 98312 | tf_op jit(solution)/shard_map/ppermute | solution.py:23
  113.2 6.1 %collective-permute-start.15 = (f32[64,128]{1,0:T(8,128)S(1)}, f32[64,128]{1,0:T(8,128)S(1)}, u32[]{:S(2)}, u32[]{:S(2)}) collective-permute-start(f32[64,128]{1,0:T(8,128)S(1)} %get-tuple-element.72.fresh), channel_id=1, source_target_pairs={{16,32},{32,16},{48,64},{64,48},{80,96},{96,80},{112,128},{128,112... | collective-permute-start | bytes 98312 | tf_op jit(solution)/shard_map/ppermute | solution.py:23
  120.3 24.8 %all-to-all-start = ((bf16[8,64,512]{2,1,0:T(8,128)(2,1)}), bf16[8,64,512]{2,1,0:T(8,128)(2,1)S(1)}, u32[]{:S(2)}, u32[]{:S(2)}) async-start(bf16[8,64,512]{2,1,0:T(8,128)(2,1)} %get-tuple-element.79), calls=%async_computation | async-start | bytes 1048576 | tf_op jit(solution)/shard_map/all_to_all | solution.py:231
  130.8 5.9 %collective-permute-start.17 = (f32[64,128]{1,0:T(8,128)S(1)}, f32[64,128]{1,0:T(8,128)S(1)}, u32[]{:S(2)}, u32[]{:S(2)}) collective-permute-start(f32[64,128]{1,0:T(8,128)S(1)} %get-tuple-element.80.edge), channel_id=1, source_target_pairs={{0,16},{16,32},{32,48},{48,64},{64,80},{80,96},{96,112},{112,128},... | collective-permute-start | bytes 98312 | tf_op jit(solution)/shard_map/ppermute | solution.py:14
  136.8 5.3 %collective-permute-start.18 = (bf16[64,512]{1,0:T(8,128)(2,1)S(1)}, bf16[64,512]{1,0:T(8,128)(2,1)S(1)}, u32[]{:S(2)}, u32[]{:S(2)}) collective-permute-start(bf16[64,512]{1,0:T(8,128)(2,1)S(1)} %shard_map.77.image), channel_id=1, source_target_pairs={{0,1},{1,0},{2,3},{3,2},{4,5},{5,4},{6,7},{7,6},{8,9},{9,8},{10,11... | collective-permute-start | bytes 196616 | tf_op jit(solution)/shard_map/ppermute | solution.py:23
  145.5 7.6 %collective-permute-start.19 = (f32[2,16,8,128]{3,2,1,0:T(8,128)S(1)}, f32[2,16,8,128]{3,2,1,0:T(8,128)S(1)}, u32[]{:S(2)}, u32[]{:S(2)}) collective-permute-start(f32[2,16,8,128]{3,2,1,0:T(8,128)S(1)} %get-tuple-element.83), channel_id=1, source_target_pairs={{0,16},{16,0},{32,48},{48,32},{64,80},{80,64},{96,112},{112,96},{1... | collective-permute-start | bytes 393224 | tf_op jit(solution)/shard_map/ppermute | solution.py:23
  153.1 5.0 %collective-permute-start.20 = (f32[16,8,128]{2,1,0:T(8,128)S(1)}, f32[16,8,128]{2,1,0:T(8,128)S(1)}, u32[]{:S(2)}, u32[]{:S(2)}) collective-permute-start(f32[16,8,128]{2,1,0:T(8,128)S(1)} %get-tuple-element.85), channel_id=1, source_target_pairs={{0,1},{1,0},{2,3},{3,2},{4,5},{5,4},{6,7},{7,6},{8,9},{9,8},{10,11... | collective-permute-start | bytes 196616 | tf_op jit(solution)/shard_map/ppermute | solution.py:23
